TPU v7x, 256 devices: a whole 4x4x8 slice. The times are simulated.
256 devices in a mesh: rep: 4 (over z_hi), tok: 4 (over z_lo, core), voc: 16 (over x, y).
Axes of the slice: x: 4, y: 4, z: 8 (z_hi: 4, z_lo: 2; z = z_hi * 2 + z_lo), core: 2. Of those that a mesh axis runs over, the one named last changes fastest.
Arguments:
- hidden: bfloat16 [4, 512, 4096], P('rep', ('tok', 'voc')), may hold values from -500 to 500
- targets: int32 [4, 512], P('rep', ('tok', 'voc')), may hold values from 0 to 65535
- unembed: bfloat16 [4, 65536, 4096], P('rep', ('tok', 'voc')), may hold values from -1 to 1
- outer_weight: float32 [8192, 4096], P(('tok', 'voc'), 'rep'), may hold values from -0.9 to 0.9
- momentum: float32 [8192, 4096], P(('tok', 'voc'), 'rep'), may hold values from -0.18 to 0.18
Outputs:
- token_loss: float32 [4, 512], P('rep', ('tok', 'voc'))
- hidden_grad: float32 [4, 512, 4096], P('rep', ('tok', 'voc'))
- new_outer: float32 [8192, 4096], P(('tok', 'voc'), 'rep')
- new_momentum: float32 [8192, 4096], P(('tok', 'voc'), 'rep')
- next_inner: bfloat16 [8192, 4096], P(('tok', 'voc'))
All inputs are finite; a program needn't handle non-finite values.
Results may differ from a plain program's by a relative error of at most 0.0085.
Values may be sent and summed in bfloat16 or wider, within the bound.
No kernel may reach another device: no remote copies, remote signals or barrier semaphores. Data moves between devices by JAX's collectives and lax.ppermute only.
A program may use at most 64 MiB of HBM per device.

v0:
```python
import functools

import jax
import jax.numpy as jnp
from jax import lax
from jax.experimental import pallas as pl
from jax.experimental.pallas import tpu as pltpu
from jax.sharding import Mesh
from jax.sharding import PartitionSpec as P

TOK = ("tok_0", "tok_1")
VOC = ("voc_0", "voc_1")
TOK_VOC = ("tok_0", "tok_1", "voc_0", "voc_1")
Z, CORE, X, Y = TOK_VOC
F32, BF16 = jnp.float32, jnp.bfloat16

PARTS = (
    (0, 0, 0, 4), (1, 0, 0, 4),
    (0, 1, 0, 4), (0, 3, 0, 4), (1, 1, 0, 4), (1, 3, 0, 4),
    (0, 2, 0, 2), (0, 2, 2, 2), (1, 2, 0, 2), (1, 2, 2, 2),
)


inner_rate = 0.5
outer_rate = 0.7
momentum_coef = 0.9
SMEM = pl.BlockSpec(memory_space=pltpu.SMEM)
VMEM = pl.BlockSpec(memory_space=pltpu.VMEM)


def call(kernel, out, *operands, flops=0, scratch=(), limit=16, specs={}):
    moved = sum(leaf.size * leaf.dtype.itemsize for leaf in jax.tree.leaves((operands, out)))
    return pl.pallas_call(
        kernel,
        in_specs=[SMEM] + [specs.get(k, VMEM) for k in range(1, len(operands))],
        out_specs=jax.tree.map(lambda _: VMEM, out),
        out_shape=out,
        scratch_shapes=scratch,
        compiler_params=pltpu.CompilerParams(vmem_limit_bytes=limit << 20),
        cost_estimate=pl.CostEstimate(
            flops=flops or moved, bytes_accessed=moved, transcendentals=0
        ),
    )(*operands)


def shaped(dtype, *shape):
    return jax.ShapeDtypeStruct(shape, dtype)


def by_core(k, inner):
    pairs = []
    for core in range(2):
        for x in range(4):
            for y in range(4):
                along_x = (core == 1) != inner
                fx, fy = ((x + k) % 4, y) if along_x else (x, (y + k) % 4)
                pairs.append(((core * 4 + fx) * 4 + fy, (core * 4 + x) * 4 + y))
    return pairs


def take_outer(value, k):
    return lax.ppermute(value, (CORE, X, Y), by_core(k, False))


def take_inner(value, k):
    return lax.ppermute(value, (CORE, X, Y), by_core(k, True))


def take(value, axis, k):
    n = lax.axis_size(axis)
    return lax.ppermute(value, axis, [((i + k) % n, i) for i in range(n)])


def along(axis):
    return lambda value, k: take(value, axis, k)


def ring_gather(value, take):
    half = value.shape[0] // 2
    up, down = take(value, 1), take(value, -1)
    far = (take(up[:half], 1), take(down[half:], -1))
    return value, up, *far, down


def to_f32(value):
    return value.astype(F32)


def ring_reduce(pieces, take):
    here, up, first, second, down = pieces
    half = first.shape[0]
    from_up = take(second, 1)
    from_down = take(first, -1)
    up = jnp.concatenate((to_f32(up[:half]) + to_f32(from_down), to_f32(up[half:])))
    down = jnp.concatenate((to_f32(down[:half]), to_f32(down[half:]) + to_f32(from_up)))
    up = take(up.astype(BF16), -1)
    down = take(down.astype(BF16), 1)
    return here, up, down


def part_tokens(here, own, other, a, first, count):
    row = lax.broadcasted_iota(jnp.int32, (count * 2 * own, 1), 0)
    t, plane, b = row % own, row // own % 2, row // (2 * own) + first
    z, c = (here[0] + plane) % 2, (here[1] + other) % 2
    x = (here[2] + jnp.where(c == 0, b, a)) % 4
    y = (here[3] + jnp.where(c == 0, a, b)) % 4
    return (((z * 2 + c) * 4 + x) * 4 + y) * own + t


def token_table(here, tokens, own):
    lane = lax.broadcasted_iota(jnp.int32, (1, tokens), 1)
    rows = [
        part_tokens(here, own, other, a, first, count) == lane for other, a, first, count in PARTS
    ]
    return jnp.concatenate([one.astype(F32) for one in rows]).astype(BF16)


def in_three(value):
    high = value.astype(BF16)
    rest = value - high.astype(F32)
    middle = rest.astype(BF16)
    return high, middle, (rest - middle.astype(F32)).astype(BF16)


def reordered(value, table, dims):
    dot = lambda one: lax.dot_general(one, table, (dims, ((), ())), preferred_element_type=F32)
    return sum(dot(one) for one in in_three(value))


def logits_kernel(own, count, before, here, *refs):
    parts, refs = refs[:count], refs[count:]
    first = not before
    w_in, tables, (logits, ids, states, table, *more) = refs[0], refs[1 : 1 + before], refs[1 + before :]
    w = more[0] if first else w_in
    vocab_rows, width = w.shape
    block = 256

    def copy(k):
        at = pl.ds(k * block, block)
        return pltpu.make_async_copy(w_in.at[at, :], w.at[at, :], more[1].at[k])

    if first:
        for k in range(vocab_rows // block):
            copy(k).start()
    start = 0
    for part in parts:
        at = pl.ds(start, part.shape[0])
        states[at, :] = part[:, :width]
        codes = part[:, width:].astype(F32).astype(jnp.int32)
        ids[at, :] = codes[:, :1] * 256 + codes[:, 1:2]
        start += part.shape[0]
    if first:
        for k in range(vocab_rows // block):
            copy(k).wait()
    rows = states.shape[0]
    lane = lax.broadcasted_iota(jnp.int32, (1, 128), 1)

    def step(j, carry):
        top, total, target = carry
        column = pl.multiple_of(j * block, block)
        out = lax.dot_general(
            states[...], w[pl.ds(column, block), :], (((1,), (1,)), ((), ())),
            preferred_element_type=F32,
        ) * (width ** (-0.5))
        logits[:, pl.ds(column, block)] = out
        hits = ids[...] - (here[4] + column)
        lanes = [out[:, k : k + 128] for k in range(0, block, 128)]
        peak = top
        for one in lanes:
            peak = jnp.maximum(peak, one)
        total = total * jnp.exp(top - peak)
        for k, one in enumerate(lanes):
            total = total + jnp.exp(one - peak)
            target = target + jnp.where(hits - k * 128 == lane, one, 0.0)
        return peak, total, target

    zero = jnp.zeros((rows, 128), F32)
    peak, total, target = lax.fori_loop(
        0, vocab_rows // block, step, (jnp.full((rows, 128), -jnp.inf, F32), zero, zero)
    )
    best = jnp.max(peak, axis=1, keepdims=True)
    mass = jnp.sum(total * jnp.exp(peak - best), axis=1, keepdims=True)
    hit = jnp.sum(target, axis=1, keepdims=True)
    mine = jnp.where(lane == 0, best, jnp.where(lane == 1, mass, jnp.where(lane == 2, hit, 0.0)))
    if before < 2:
        table[...] = mine
    else:
        every = jnp.concatenate([one[...] for one in tables] + [mine])
        table[...] = reordered(every, token_table(here, every.shape[0], own), ((0,), (0,)))[:8]


def merged(parts):
    top = parts[0][0:1]
    for one in parts[1:]:
        top = jnp.maximum(top, one[0:1])
    total = sum(one[1:2] * jnp.exp(one[0:1] - top) for one in parts)
    return top, total, sum(one[2:3] for one in parts)


def merge_kernel(here, *refs):
    got, out = refs[:-1], refs[-1]
    got = [got[0][k] for k in range(4)] if len(got) == 1 else [one[...] for one in got]
    top, total, target = merged(got)
    row = lax.broadcasted_iota(jnp.int32, out.shape, 0)
    out[...] = jnp.where(row == 0, top, jnp.where(row == 1, total, jnp.where(row == 2, target, 0.0)))


def slab_kernel(own, part, here, *refs):
    got, logits, ids, states, outs = refs[:4], refs[4:7], refs[7:10], refs[10:13], refs[13:]
    loss, log_total, mine, up, first, second, down, errors = outs
    tokens = errors.shape[0]
    width = 4 * part
    top, total, target = merged([one[...] for one in got])
    every = top + jnp.log(total)
    row = lax.broadcasted_iota(jnp.int32, got[0].shape, 0)
    both = jnp.where(row == 0, every, jnp.where(row == 1, every - target, 0.0))
    table = token_table(here, tokens, own)
    columns = sum(
        lax.dot_general(table, one, (((1,), (1,)), ((), ())), preferred_element_type=F32)
        for one in in_three(both)
    )
    log_total[...] = columns[:, 0:1]
    loss[...] = columns[:own, 1:2]
    strip = mine.shape[0]
    lane = lax.broadcasted_iota(jnp.int32, (1, strip), 1)
    start = 0
    for values, id_part in zip(logits, ids):
        end = start + values.shape[0]
        onehot = (id_part[...] - here[4] == lane).astype(F32)
        errors[start:end, :] = (
            jnp.exp(values[:, :strip] - columns[start:end, 0:1]) - onehot
        ).astype(BF16)
        start = end

    def grad(k):
        at = pl.multiple_of(lax.rem(here[5] + k, 4) * part, part)
        total, start = 0.0, 0
        for state in states:
            end = start + state.shape[0]
            total += lax.dot_general(
                errors[start:end, :], state[:, pl.ds(at, part)], (((0,), (0,)), ((), ())),
                preferred_element_type=F32,
            )
            start = end
        return total * (width ** (-0.5))

    half = first.shape[0]
    across = grad(2).astype(BF16)
    first[...], second[...] = across[:half], across[half:]
    up[...] = grad(1).astype(BF16)
    down[...] = grad(3).astype(BF16)
    mine[...] = grad(0)


def hidden_kernel(here, *refs):
    logits, ids, (log_total, w, keep, send, errors) = refs[:3], refs[3:6], refs[6:]
    vocab_rows, width = w.shape
    block, strip = 512, 128
    lane = lax.broadcasted_iota(jnp.int32, (1, strip), 1)
    start = 0
    for values, id_part in zip(logits, ids):
        at = pl.ds(start, values.shape[0])
        hits = id_part[...] - here[4]
        for k in range(0, vocab_rows, strip):
            onehot = (hits - k == lane).astype(F32)
            errors[at, k : k + strip] = (
                jnp.exp(values[:, k : k + strip] - log_total[at, :]) - onehot
            ).astype(BF16)
        start += values.shape[0]

    places = []
    unit = keep.shape[0] // 4
    start = 0
    for other, a, first, count in PARTS:
        rows = unit * count // 4
        places.append((send if other else keep, a * unit + unit * first // 4, start, rows))
        start += rows

    def step(j, _):
        cols = pl.ds(pl.multiple_of(j * block, block), block)
        grad = (jnp.dot(errors[...], w[:, cols], preferred_element_type=F32) * (width ** (-0.5))).astype(BF16)
        for out, to, start, rows in places:
            out[to : to + rows, cols] = grad[start : start + rows]
        return 0

    lax.fori_loop(0, width // block, step, 0)


def outer_kernel(here, outer, momentum, w0, w1, w2, w3, g0, g1, g2, new_outer, new_momentum, rounded):
    mean_weight = (to_f32(w0[...]) + to_f32(w1[...]) + to_f32(w2[...]) + to_f32(w3[...])) / 4
    slab_grad = g0[...] + to_f32(g1[...]) + to_f32(g2[...])
    pseudo_grad = outer[...] - (mean_weight - (inner_rate / 4) * slab_grad)
    moved = momentum_coef * momentum[...] + pseudo_grad
    new_momentum[...] = moved
    out = outer[...] - outer_rate * (pseudo_grad + momentum_coef * moved)
    new_outer[...] = out
    rounded[...] = out.astype(BF16)


def place_kernel(part, here, first, *refs):
    pieces, out = (first, *refs[:-1]), refs[-1]
    mine, up, low, high, down = pieces
    half = low.shape[0]
    at = lambda k: pl.ds(pl.multiple_of(lax.rem(here[5] + k, 4) * part, part), part)
    out[:, at(0)] = mine[...]
    out[:, at(1)] = up[...]
    out[:half, at(2)] = low[...]
    out[half:, at(2)] = high[...]
    out[:, at(3)] = down[...]


def per_device(hidden, targets, unembed, outer_weight, momentum):
    weights = unembed[0]
    vocab_rows, width = weights.shape
    own = hidden.shape[1]
    slab_rows, part = outer_weight.shape
    reps = lax.axis_size("rep")
    rep = lax.axis_index("rep")
    tokens = own * lax.axis_size(TOK_VOC)
    group_index = lax.axis_index(TOK) * lax.axis_size(VOC) + lax.axis_index(VOC)
    here = jnp.stack(
        [lax.axis_index(a) for a in TOK_VOC] + [group_index * vocab_rows, rep]
    ).astype(jnp.int32)

    ids = targets[0]
    codes = jnp.stack((ids >> 8, ids & 255), 1).astype(BF16)
    piece = jnp.concatenate((hidden[0], jnp.pad(codes, ((0, 0), (0, 126)))), 1)
    across = take(piece, Z, 1)
    piece = jnp.concatenate((piece, across))
    line = jnp.concatenate((piece, take_inner(piece, 1), take_inner(piece, 2), take_inner(piece, -1)))
    up = take_outer(line, 1)
    down = take_outer(line, -1)
    cut = line.shape[0] // 2
    far_up = take_outer(up[:cut], 1)
    far_down = take_outer(down[cut:], -1)

    def with_other(*parts):
        return (*parts, *[take(one, CORE, 1) for one in parts])

    def features(value, k):
        return lax.dynamic_slice_in_dim(value, ((rep + k) % reps) * part, part, 1)

    slab = weights[:slab_rows]
    slab_weights = [features(slab, 0)]
    for k in (1, 2, 3):
        slab_weights.append(take(features(slab, -k), "rep", k))

    def logits_of(parts, w, tables):
        rows = sum(one.shape[0] for one in parts)
        out = [
            shaped(F32, rows, vocab_rows),
            shaped(jnp.int32, rows, 1),
            shaped(BF16, rows, width),
            shaped(F32, *((8, tokens) if len(tables) == 2 else (rows, 128))),
        ]
        kind = {}
        if not tables:
            out.append(shaped(BF16, vocab_rows, width))
            kind = dict(
                scratch=[pltpu.SemaphoreType.DMA((4,))],
                specs={len(parts) + 1: pl.BlockSpec(memory_space=pltpu.HBM)},
            )
        return call(
            functools.partial(logits_kernel, own, len(parts), len(tables)),
            out, here, *parts, w, *tables,
            flops=2 * max(rows, 256) * vocab_rows * width, **kind,
        )

    logits_0, ids_0, states_0, table_0, w = logits_of(with_other(line), weights, ())
    logits_1, ids_1, states_1, table_1 = logits_of(with_other(up, down), w, (table_0,))
    logits_2, ids_2, states_2, stats = logits_of(with_other(far_up, far_down), w, (table_0, table_1))
    logits, every_id = (logits_0, logits_1, logits_2), (ids_0, ids_1, ids_2)
    states = (states_0, states_1, states_2)

    def ring_stats(value, axis):
        return [value] + [take(value, axis, k) for k in (1, 2, 3)]

    stats = lax.all_gather(stats, TOK)
    stats = call(merge_kernel, shaped(F32, 8, tokens), here, stats)
    stats = call(merge_kernel, shaped(F32, 8, tokens), here, *ring_stats(stats, X))
    stats = ring_stats(stats, Y)

    half = slab_rows // 2
    loss, log_total, *grads = call(
        functools.partial(slab_kernel, own, part),
        (
            shaped(F32, own, 1),
            shaped(F32, tokens, 1),
            shaped(F32, slab_rows, part),
            shaped(BF16, slab_rows, part),
            shaped(BF16, half, part),
            shaped(BF16, half, part),
            shaped(BF16, slab_rows, part),
        ),
        here, *stats, *logits, *every_id, *states,
        flops=2 * tokens * slab_rows * width,
        scratch=[pltpu.VMEM((tokens, slab_rows), BF16)],
    )
    token_loss = loss.reshape(1, own)

    keep, send = call(
        hidden_kernel,
        (shaped(BF16, tokens // 2, width), shaped(BF16, tokens // 2, width)),
        here, *logits, *every_id, log_total, w,
        flops=2 * tokens * vocab_rows * width,
        scratch=[pltpu.VMEM((tokens, vocab_rows), BF16)],
    )

    slab_grads = ring_reduce(grads, along("rep"))
    new_outer, new_momentum, rounded = call(
        outer_kernel,
        (shaped(F32, slab_rows, part), shaped(F32, slab_rows, part), shaped(BF16, slab_rows, part)),
        here, outer_weight, momentum, *slab_weights, *slab_grads,
    )
    pieces = ring_gather(rounded, along("rep"))
    next_inner = call(
        functools.partial(place_kernel, part), shaped(BF16, slab_rows, width), here, *pieces
    )

    total = (to_f32(keep) + to_f32(take(send, CORE, 1))).reshape(4, 8 * own, width)
    rounded = total.astype(BF16)
    parts = (total[0], total[1], rounded[2, : 4 * own], rounded[2, 4 * own :], total[3])
    here_part, *got = ring_reduce(parts, take_outer)
    line = (here_part + to_f32(got[0]) + to_f32(got[1])).reshape(4, 2 * own, width)
    rounded = line.astype(BF16)
    pair = line[0] + sum(to_f32(take_inner(rounded[k], -k)) for k in (1, 2, 3))
    token_grad = pair[:own] + to_f32(take(pair[own:].astype(BF16), Z, 1))
    return (token_loss, token_grad[None], new_outer, new_momentum, next_inner)


def solution(mesh):
    finer = Mesh(
        mesh.devices.reshape(mesh.shape["rep"], 2, 2, 4, 4),
        ("rep", "tok_0", "tok_1", "voc_0", "voc_1"),
    )
    in_specs = (
        P("rep", TOK_VOC, None),
        P("rep", TOK_VOC),
        P("rep", TOK_VOC, None),
        P(TOK_VOC, "rep"),
        P(TOK_VOC, "rep"),
    )
    out_specs = (
        P("rep", TOK_VOC),
        P("rep", TOK_VOC, None),
        P(TOK_VOC, "rep"),
        P(TOK_VOC, "rep"),
        P(TOK_VOC, None),
    )

    return jax.shard_map(per_device, mesh=finer, in_specs=in_specs, out_specs=out_specs, check_vma=False)
```

profile of v0, /device:TPU:32, one launch (start us, length us, event | category | flops | bytes accessed | tf_op | source)
XLA Modules:
  0.0 178.5 jit_solution(14520269657394624819)
XLA Ops:
  0.6 0.7 convert_bitcast_fusion.1
  1.4 0.8 pad_maximum_fusion.5
  2.3 1.9 %collective-permute-start = (bf16[8,4224]{1,0:T(8,128)(2,1)S(1)}, bf16[8,4224]{1,0:T(8,128)(2,1)S(1)}, u32[]{:S(2)}, u32[]{:S(2)}) collective-permute-start(bf16[8,4224]{1,0:T(8,128)(2,1)S(1)} %get-tuple-element.72), channel_id=1, source_target_pairs={{32,0},{0,32},{33,1},{1,33},{34,2},{2,34},{35,3},{3,35},{36,4},{4,... | collective-permute-start | bytes 202760 | tf_op jit(solution)/shard_map/ppermute | solution.py:71
  4.2 2.5 %collective-permute-done = bf16[8,4224]{1,0:T(8,128)(2,1)S(1)} collective-permute-done((bf16[8,4224]{1,0:T(8,128)(2,1)S(1)}, bf16[8,4224]{1,0:T(8,128)(2,1)S(1)}, u32[]{:S(2)}, u32[]{:S(2)}) %collective-permute-start) | collective-permute-done | bytes 67616 | tf_op jit(solution)/shard_map/ppermute | solution.py:71
  6.6 0.9 pad_maximum_fusion.4
  7.5 2.8 %collective-permute-start.1 = (bf16[16,4224]{1,0:T(8,128)(2,1)S(1)}, bf16[16,4224]{1,0:T(8,128)(2,1)S(1)}, u32[]{:S(2)}, u32[]{:S(2)}) collective-permute-start(bf16[16,4224]{1,0:T(8,128)(2,1)S(1)} %pad_maximum_fusion.4), channel_id=1, source_target_pairs={{4,0},{5,1},{6,2},{7,3},{8,4},{9,5},{10,6},{11,7},{12,8},{13,9},{1... | collective-permute-start | bytes 405512 | tf_op jit(solution)/shard_map/ppermute | solution.py:66
  10.3 0.8 collective-permute-start.2
  11.1 0.9 collective-permute-start.3
  12.0 2.3 %collective-permute-done.1 = bf16[16,4224]{1,0:T(8,128)(2,1)S(1)} collective-permute-done((bf16[16,4224]{1,0:T(8,128)(2,1)S(1)}, bf16[16,4224]{1,0:T(8,128)(2,1)S(1)}, u32[]{:S(2)}, u32[]{:S(2)}) %collective-permute-start.1) | collective-permute-done | bytes 135200 | tf_op jit(solution)/shard_map/ppermute | solution.py:66
  14.4 2.6 %collective-permute-done.2 = bf16[16,4224]{1,0:T(8,128)(2,1)S(1)} collective-permute-done((bf16[16,4224]{1,0:T(8,128)(2,1)S(1)}, bf16[16,4224]{1,0:T(8,128)(2,1)S(1)}, u32[]{:S(2)}, u32[]{:S(2)}) %collective-permute-start.2) | collective-permute-done | bytes 135200 | tf_op jit(solution)/shard_map/ppermute | solution.py:66
  17.0 1.3 collective-permute-done.3
  18.3 3.1 %collective-permute-start.4 = (bf16[64,4224]{1,0:T(8,128)(2,1)S(1)}, bf16[64,4224]{1,0:T(8,128)(2,1)S(1)}, u32[]{:S(2)}, u32[]{:S(2)}) collective-permute-start(bf16[64,4224]{1,0:T(8,128)(2,1)S(1)} %constant_dynamic-update-slice_fusion.refs_0_), channel_id=1, source_target_pairs={{1,0},{2,1},{3,2},{0,3},{5,4},{6,5},{7,6},{4,7},{9,8},{10,9},{11,1... | collective-permute-start | bytes 1622024 | tf_op jit(solution)/shard_map/ppermute | solution.py:62
  21.4 6.9 %collective-permute-done.4.refs_0_ = bf16[64,4224]{1,0:T(8,128)(2,1)S(1)} collective-permute-done((bf16[64,4224]{1,0:T(8,128)(2,1)S(1)}, bf16[64,4224]{1,0:T(8,128)(2,1)S(1)}, u32[]{:S(2)}, u32[]{:S(2)}) %collective-permute-start.4) | collective-permute-done | bytes 540704 | tf_op jit(solution)/shard_map/ppermute | solution.py:62
  28.3 3.7 %collective-permute-done.6.refs_1_ = bf16[64,4224]{1,0:T(8,128)(2,1)S(1)} collective-permute-done((bf16[64,4224]{1,0:T(8,128)(2,1)S(1)}, bf16[64,4224]{1,0:T(8,128)(2,1)S(1)}, u32[]{:S(2)}, u32[]{:S(2)}) %collective-permute-start.6) | collective-permute-done | bytes 540704 | tf_op jit(solution)/shard_map/ppermute | solution.py:62
  32.0 0.7 slice.107
  33.2 0.7 slice.108
  33.9 1.5 collective-permute-start.7
  35.5 3.8 %collective-permute-done.5.refs_0_ = bf16[32,4224]{1,0:T(8,128)(2,1)S(1)} collective-permute-done((bf16[32,4224]{1,0:T(8,128)(2,1)}, bf16[32,4224]{1,0:T(8,128)(2,1)S(1)}, u32[]{:S(2)}, u32[]{:S(2)}) %collective-permute-start.5) | collective-permute-done | bytes 270368 | tf_op jit(solution)/shard_map/ppermute | solution.py:62
  39.4 2.5 %collective-permute-done.7.refs_1_ = bf16[32,4224]{1,0:T(8,128)(2,1)} collective-permute-done((bf16[32,4224]{1,0:T(8,128)(2,1)}, bf16[32,4224]{1,0:T(8,128)(2,1)}, u32[]{:S(2)}, u32[]{:S(2)}) %collective-permute-start.7) | collective-permute-done | bytes 270368 | tf_op jit(solution)/shard_map/ppermute | solution.py:62
  41.9 3.4 %copy-done = bf16[1,1024,4096]{2,1,0:T(8,128)(2,1)S(1)} copy-done((bf16[1,1024,4096]{2,1,0:T(8,128)(2,1)S(1)}, bf16[1,1024,4096]{2,1,0:T(8,128)(2,1)}, u32[]{:S(2)}) %copy-start) | copy-done | bytes 8388632
  45.3 4.9 %shard_map.92 = (f32[128,1024]{1,0:T(8,128)S(1)}, s32[128,1]{1,0:T(8,128)S(1)}, bf16[128,4096]{1,0:T(8,128)(2,1)S(1)}, f32[128,128]{1,0:T(8,128)S(1)}, bf16[1024,4096]{1,0:T(8,128)(2,1)S(1)}) custom-call(s32[6]{0:T(128)S(1)} %stack.33.here, bf16[64,4224]{1,0:T(8,128)(2,1)S(1)} %constant_dynamic-update-slice_fusion.refs_0_, ...), custom_call_target="tpu_custom_call" | custom-call | flops 2147483648 | bytes 19497496 | tf_op jit(solution)/shard_map/pallas_call | solution.py:33
  50.2 4.2 %shard_map.93 = (f32[256,1024]{1,0:T(8,128)S(1)}, s32[256,1]{1,0:T(8,128)S(1)}, bf16[256,4096]{1,0:T(8,128)(2,1)S(1)}, f32[256,128]{1,0:T(8,128)S(1)}) custom-call(s32[6]{0:T(128)S(1)} %stack.33.here, bf16[64,4224]{1,0:T(8,128)(2,1)S(1)} %collective-permute-done.4.refs_0_, bf16[64,4224]{1,0:T(8,128)(2,1)S(1)} %collective-permute-done.6.refs_1_, ...), custom_call_target="tpu_custom_call" | custom-call | flops 2147483648 | bytes 13894680 | tf_op jit(solution)/shard_map/pallas_call | solution.py:33
  54.4 5.3 %shard_map.94 = (f32[128,1024]{1,0:T(8,128)S(1)}, s32[128,1]{1,0:T(8,128)S(1)}, bf16[128,4096]{1,0:T(8,128)(2,1)S(1)}, f32[8,512]{1,0:T(8,128)S(1)}) custom-call(s32[6]{0:T(128)S(1)} %stack.33.here, bf16[32,4224]{1,0:T(8,128)(2,1)S(1)} %collective-permute-done.5.refs_0_, bf16[32,4224]{1,0:T(8,128)(2,1)} %collective-permute-done.7.refs_1_, ...), custom_call_target="tpu_custom_call" | custom-call | flops 2147483648 | bytes 11256344 | tf_op jit(solution)/shard_map/pallas_call | solution.py:33
  59.7 5.4 %all-gather = f32[32,512]{1,0:T(8,128)S(1)} all-gather(f32[8,512]{1,0:T(8,128)S(1)} %get-tuple-element.33), channel_id=2, replica_groups=mesh['rep'=4,'tok_0'=2,'tok_1'=2,'voc_0'=4,'voc_1'=4] {'tok_0','tok_1'}, dimensions={0}, use_global_device_ids=true | all-gather | bytes 81920 | tf_op jit(solution)/shard_map/all_gather | solution.py:378
  65.1 0.6 shard_map.95.refs_0_
  65.7 0.6 collective-permute-start.13
  66.3 0.9 collective-permute-start.14
  67.3 0.7 collective-permute-start.15
  68.0 1.5 collective-permute-done.13.refs_1_
  69.5 2.1 %collective-permute-done.14.refs_2_ = f32[8,512]{1,0:T(8,128)S(1)} collective-permute-done((f32[8,512]{1,0:T(8,128)S(1)}, f32[8,512]{1,0:T(8,128)S(1)}, u32[]{:S(2)}, u32[]{:S(2)}) %collective-permute-start.14) | collective-permute-done | bytes 16416 | tf_op jit(solution)/shard_map/ppermute | solution.py:71
  71.6 0.6 collective-permute-done.15.refs_3_
  72.2 0.6 shard_map.96.refs_0_
  72.9 2.4 %collective-permute-start.17 = (f32[8,512]{1,0:T(8,128)S(1)}, f32[8,512]{1,0:T(8,128)S(1)}, u32[]{:S(2)}, u32[]{:S(2)}) collective-permute-start(f32[8,512]{1,0:T(8,128)S(1)} %shard_map.96.refs_0_), channel_id=1, source_target_pairs={{2,0},{3,1},{0,2},{1,3},{6,4},{7,5},{4,6},{5,7},{10,8},{11,9},{8,1... | collective-permute-start | bytes 49160 | tf_op jit(solution)/shard_map/ppermute | solution.py:71
  75.2 1.4 collective-permute-done.16.refs_1_
  76.6 1.6 collective-permute-done.17.refs_2_
  78.2 2.0 %collective-permute-done.18.refs_3_ = f32[8,512]{1,0:T(8,128)S(1)} collective-permute-done((f32[8,512]{1,0:T(8,128)S(1)}, f32[8,512]{1,0:T(8,128)S(1)}, u32[]{:S(2)}, u32[]{:S(2)}) %collective-permute-start.18) | collective-permute-done | bytes 16416 | tf_op jit(solution)/shard_map/ppermute | solution.py:71
  80.2 3.1 %shard_map.97 = (f32[8,1]{1,0:T(8,128)S(1)}, f32[512,1]{1,0:T(8,128)S(1)}, f32[128,1024]{1,0:T(8,128)S(1)}, bf16[128,1024]{1,0:T(8,128)(2,1)S(1)}, bf16[64,1024]...) custom-call(s32[6]{0:T(128)S(1)} %stack.33.here, f32[8,512]{1,0:T(8,128)S(1)} %shard_map.96.refs_0_, ...), custom_call_target="tpu_custom_call" | custom-call | flops 536870912 | bytes 7671864 | tf_op jit(solution)/shard_map/pallas_call | solution.py:33
  83.3 8.8 %shard_map.98 = (bf16[256,4096]{1,0:T(8,128)(2,1)S(1)}, bf16[256,4096]{1,0:T(8,128)(2,1)}) custom-call(s32[6]{0:T(128)S(1)} %stack.33.here, f32[128,1024]{1,0:T(8,128)S(1)} %get-tuple-element.34.refs_4_.refs_0_, f32[256,1024]{1,0:T(8,128)S(1)} %get-tuple-element.35.refs_5_.refs_1_, f32[128,1024]{1,0:T(8,128)S(1)} %get-tuple-element.36.refs_6_.refs_2_, ...), custom_call_target="tpu_custom_call" | custom-call | flops 4294967296 | bytes 14684184 | tf_op jit(solution)/shard_map/pallas_call | solution.py:33
  92.2 2.3 %slice.100 = bf16[1,128,4096]{2,1,0:T(8,128)(2,1)} slice(bf16[1,1024,4096]{2,1,0:T(8,128)(2,1)} %param.7), slice={[0:1], [0:128], [0:4096]} | slice | bytes 2097152 | tf_op jit(solution)/shard_map/slice | solution.py:343
  94.5 3.3 %collective-permute-start.31 = (bf16[64,1024]{1,0:T(8,128)(2,1)S(1)}, bf16[64,1024]{1,0:T(8,128)(2,1)S(1)}, u32[]{:S(2)}, u32[]{:S(2)}) collective-permute-start(bf16[64,1024]{1,0:T(8,128)(2,1)S(1)} %get-tuple-element.49), channel_id=1, source_target_pairs={{192,0},{0,64},{64,128},{128,192},{193,1},{1,65},{65,129},{129,193... | collective-permute-start | bytes 393224 | tf_op jit(solution)/shard_map/ppermute | solution.py:71
  97.7 1.3 dynamic-slice_bitcast_fusion
  99.0 2.2 %collective-permute-start.28 = (bf16[128,1024]{1,0:T(8,128)(2,1)S(1)}, bf16[128,1024]{1,0:T(8,128)(2,1)S(1)}, u32[]{:S(2)}, u32[]{:S(2)}) collective-permute-start(bf16[128,1024]{1,0:T(8,128)(2,1)S(1)} %get-tuple-element.67), channel_id=1, source_target_pairs={{64,0},{128,64},{192,128},{0,192},{65,1},{129,65},{193,129},{1,193... | collective-permute-start | bytes 786440 | tf_op jit(solution)/shard_map/ppermute | solution.py:71
  101.2 5.0 %collective-permute-start.29 = (bf16[128,1024]{1,0:T(8,128)(2,1)S(1)}, bf16[128,1024]{1,0:T(8,128)(2,1)S(1)}, u32[]{:S(2)}, u32[]{:S(2)}) collective-permute-start(bf16[128,1024]{1,0:T(8,128)(2,1)S(1)} %get-tuple-element.66), channel_id=1, source_target_pairs={{128,0},{192,64},{0,128},{64,192},{129,1},{193,65},{1,129},{65,193... | collective-permute-start | bytes 786440 | tf_op jit(solution)/shard_map/ppermute | solution.py:71
  106.9 2.5 %fusion.4 = (bf16[256,4096]{1,0:T(8,128)(2,1)S(1)}, f32[256,4096]{1,0:T(8,128)S(1)}) fusion(bf16[256,4096]{1,0:T(8,128)(2,1)} %collective-permute-done.19, bf16[256,4096]{1,0:T(8,128)(2,1)S(1)} %get-tuple-element.45), kind=kLoop, calls=%fused_computation.33 | loop fusion | flops 4194304 | bytes 10485760 | tf_op jit(solution)/shard_map/convert_element_type | solution.py:421
  109.7 3.2 %collective-permute-start.22 = (bf16[32,4096]{1,0:T(8,128)(2,1)S(1)}, bf16[32,4096]{1,0:T(8,128)(2,1)S(1)}, u32[]{:S(2)}, u32[]{:S(2)}) collective-permute-start(bf16[32,4096]{1,0:T(8,128)(2,1)S(1)} %get-tuple-element.62), channel_id=1, source_target_pairs={{1,0},{2,1},{3,2},{0,3},{5,4},{6,5},{7,6},{4,7},{9,8},{10,9},{11,1... | collective-permute-start | bytes 786440 | tf_op jit(solution)/shard_map/ppermute | solution.py:62
  113.0 4.3 %collective-permute-done.20 = bf16[32,4096]{1,0:T(8,128)(2,1)S(1)} collective-permute-done((bf16[32,4096]{1,0:T(8,128)(2,1)S(1)}, bf16[32,4096]{1,0:T(8,128)(2,1)S(1)}, u32[]{:S(2)}, u32[]{:S(2)}) %collective-permute-start.20) | collective-permute-done | bytes 262176 | tf_op jit(solution)/shard_map/ppermute | solution.py:62
  117.3 3.6 %collective-permute-start.33 = (bf16[64,1024]{1,0:T(8,128)(2,1)S(1)}, bf16[64,1024]{1,0:T(8,128)(2,1)S(1)}, u32[]{:S(2)}, u32[]{:S(2)}) collective-permute-start(bf16[64,1024]{1,0:T(8,128)(2,1)S(1)} %get-tuple-element.51), channel_id=1, source_target_pairs={{64,0},{128,64},{192,128},{0,192},{65,1},{129,65},{193,129},{1,193... | collective-permute-start | bytes 393224 | tf_op jit(solution)/shard_map/ppermute | solution.py:71
  121.2 10.7 %collective-permute-done.33 = bf16[64,1024]{1,0:T(8,128)(2,1)S(1)} collective-permute-done((bf16[64,1024]{1,0:T(8,128)(2,1)S(1)}, bf16[64,1024]{1,0:T(8,128)(2,1)S(1)}, u32[]{:S(2)}, u32[]{:S(2)}) %collective-permute-start.33) | collective-permute-done | bytes 131104 | tf_op jit(solution)/shard_map/ppermute | solution.py:71
  132.0 3.3 %collective-permute-start.32 = (bf16[128,1024]{1,0:T(8,128)(2,1)S(1)}, bf16[128,1024]{1,0:T(8,128)(2,1)S(1)}, u32[]{:S(2)}, u32[]{:S(2)}) collective-permute-start(bf16[128,1024]{1,0:T(8,128)(2,1)S(1)} %pad_maximum_fusion.2), channel_id=1, source_target_pairs={{192,0},{0,64},{64,128},{128,192},{193,1},{1,65},{65,129},{129,193... | collective-permute-start | bytes 786440 | tf_op jit(solution)/shard_map/ppermute | solution.py:71
  135.3 0.9 collective-permute-start.34
  136.2 10.6 %collective-permute-done.32.g1 = bf16[128,1024]{1,0:T(8,128)(2,1)S(1)} collective-permute-done((bf16[128,1024]{1,0:T(8,128)(2,1)S(1)}, bf16[128,1024]{1,0:T(8,128)(2,1)S(1)}, u32[]{:S(2)}, u32[]{:S(2)}) %collective-permute-start.32) | collective-permute-done | bytes 262176 | tf_op jit(solution)/shard_map/ppermute | solution.py:71
  146.8 2.2 %collective-permute-done.34.g2 = bf16[128,1024]{1,0:T(8,128)(2,1)S(1)} collective-permute-done((bf16[128,1024]{1,0:T(8,128)(2,1)S(1)}, bf16[128,1024]{1,0:T(8,128)(2,1)S(1)}, u32[]{:S(2)}, u32[]{:S(2)}) %collective-permute-start.34) | collective-permute-done | bytes 262176 | tf_op jit(solution)/shard_map/ppermute | solution.py:71
  149.0 1.8 %shard_map.99 = (f32[128,1024]{1,0:T(8,128)}, f32[128,1024]{1,0:T(8,128)}, bf16[128,1024]{1,0:T(8,128)(2,1)S(1)}) custom-call(s32[6]{0:T(128)S(1)} %stack.33.here, f32[128,1024]{1,0:T(8,128)S(1)} %copy-done.1, f32[128,1024]{1,0:T(8,128)S(1)} %copy-done.2, bf16[128,1024]{1,0:T(8,128)(2,1)S(1)} %get-tuple-element.68.w0, ...), custom_call_target="tpu_custom_call" | custom-call | flops 4456472 | bytes 4456472 | tf_op jit(solution)/shard_map/pallas_call | solution.py:33
  150.8 2.4 %collective-permute-start.35 = (bf16[128,1024]{1,0:T(8,128)(2,1)S(1)}, bf16[128,1024]{1,0:T(8,128)(2,1)S(1)}, u32[]{:S(2)}, u32[]{:S(2)}) collective-permute-start(bf16[128,1024]{1,0:T(8,128)(2,1)S(1)} %get-tuple-element.54.first), channel_id=1, source_target_pairs={{64,0},{128,64},{192,128},{0,192},{65,1},{129,65},{193,129},{1,193... | collective-permute-start | bytes 786440 | tf_op jit(solution)/shard_map/ppermute | solution.py:71
  153.9 2.4 %collective-permute-start.26 = (bf16[16,4096]{1,0:T(8,128)(2,1)S(1)}, bf16[16,4096]{1,0:T(8,128)(2,1)S(1)}, u32[]{:S(2)}, u32[]{:S(2)}) collective-permute-start(bf16[16,4096]{1,0:T(8,128)(2,1)S(1)} %get-tuple-element.70), channel_id=1, source_target_pairs={{4,0},{5,1},{6,2},{7,3},{8,4},{9,5},{10,6},{11,7},{12,8},{13,9},{1... | collective-permute-start | bytes 393224 | tf_op jit(solution)/shard_map/ppermute | solution.py:66
  156.7 1.3 collective-permute-start.24
  158.0 6.9 %collective-permute-done.35.refs_0_ = bf16[128,1024]{1,0:T(8,128)(2,1)S(1)} collective-permute-done((bf16[128,1024]{1,0:T(8,128)(2,1)S(1)}, bf16[128,1024]{1,0:T(8,128)(2,1)S(1)}, u32[]{:S(2)}, u32[]{:S(2)}) %collective-permute-start.35) | collective-permute-done | bytes 262176 | tf_op jit(solution)/shard_map/ppermute | solution.py:71
  165.0 3.3 %collective-permute-start.36 = (bf16[64,1024]{1,0:T(8,128)(2,1)S(1)}, bf16[64,1024]{1,0:T(8,128)(2,1)S(1)}, u32[]{:S(2)}, u32[]{:S(2)}) collective-permute-start(bf16[64,1024]{1,0:T(8,128)(2,1)S(1)} %slice.122), channel_id=1, source_target_pairs={{64,0},{128,64},{192,128},{0,192},{65,1},{129,65},{193,129},{1,193... | collective-permute-start | bytes 393224 | tf_op jit(solution)/shard_map/ppermute | solution.py:71
  168.5 1.4 collective-permute-start.27
  169.9 0.6 reduce
  170.6 1.3 collective-permute-done.36.refs_1_
  171.9 4.4 %collective-permute-done.38.refs_2_ = bf16[64,1024]{1,0:T(8,128)(2,1)S(1)} collective-permute-done((bf16[64,1024]{1,0:T(8,128)(2,1)S(1)}, bf16[64,1024]{1,0:T(8,128)(2,1)S(1)}, u32[]{:S(2)}, u32[]{:S(2)}) %collective-permute-start.38) | collective-permute-done | bytes 131104 | tf_op jit(solution)/shard_map/ppermute | solution.py:71
  176.3 1.6 shard_map.100
  177.9 0.7 fusion.3
  (65 shorter events, 3.5 us)
Async XLA Ops:
  2.3 4.4 %collective-permute-start = (bf16[8,4224]{1,0:T(8,128)(2,1)S(1)}, bf16[8,4224]{1,0:T(8,128)(2,1)S(1)}, u32[]{:S(2)}, u32[]{:S(2)}) collective-permute-start(bf16[8,4224]{1,0:T(8,128)(2,1)S(1)} %get-tuple-element.72), channel_id=1, source_target_pairs={{32,0},{0,32},{33,1},{1,33},{34,2},{2,34},{35,3},{3,35},{36,4},{4,... | collective-permute-start | bytes 202760 | tf_op jit(solution)/shard_map/ppermute | solution.py:71
  7.5 6.8 %collective-permute-start.1 = (bf16[16,4224]{1,0:T(8,128)(2,1)S(1)}, bf16[16,4224]{1,0:T(8,128)(2,1)S(1)}, u32[]{:S(2)}, u32[]{:S(2)}) collective-permute-start(bf16[16,4224]{1,0:T(8,128)(2,1)S(1)} %pad_maximum_fusion.4), channel_id=1, source_target_pairs={{4,0},{5,1},{6,2},{7,3},{8,4},{9,5},{10,6},{11,7},{12,8},{13,9},{1... | collective-permute-start | bytes 405512 | tf_op jit(solution)/shard_map/ppermute | solution.py:66
  10.3 6.6 %collective-permute-start.2 = (bf16[16,4224]{1,0:T(8,128)(2,1)S(1)}, bf16[16,4224]{1,0:T(8,128)(2,1)S(1)}, u32[]{:S(2)}, u32[]{:S(2)}) collective-permute-start(bf16[16,4224]{1,0:T(8,128)(2,1)S(1)} %pad_maximum_fusion.4), channel_id=1, source_target_pairs={{8,0},{9,1},{10,2},{11,3},{12,4},{13,5},{14,6},{15,7},{0,8},{1,9},... | collective-permute-start | bytes 405512 | tf_op jit(solution)/shard_map/ppermute | solution.py:66
  11.1 7.2 %collective-permute-start.3 = (bf16[16,4224]{1,0:T(8,128)(2,1)S(1)}, bf16[16,4224]{1,0:T(8,128)(2,1)S(1)}, u32[]{:S(2)}, u32[]{:S(2)}) collective-permute-start(bf16[16,4224]{1,0:T(8,128)(2,1)S(1)} %pad_maximum_fusion.4), channel_id=1, source_target_pairs={{12,0},{13,1},{14,2},{15,3},{0,4},{1,5},{2,6},{3,7},{4,8},{5,9},{6... | collective-permute-start | bytes 405512 | tf_op jit(solution)/shard_map/ppermute | solution.py:66
  18.3 10.0 %collective-permute-start.4 = (bf16[64,4224]{1,0:T(8,128)(2,1)S(1)}, bf16[64,4224]{1,0:T(8,128)(2,1)S(1)}, u32[]{:S(2)}, u32[]{:S(2)}) collective-permute-start(bf16[64,4224]{1,0:T(8,128)(2,1)S(1)} %constant_dynamic-update-slice_fusion.refs_0_), channel_id=1, source_target_pairs={{1,0},{2,1},{3,2},{0,3},{5,4},{6,5},{7,6},{4,7},{9,8},{10,9},{11,1... | collective-permute-start | bytes 1622024 | tf_op jit(solution)/shard_map/ppermute | solution.py:62
  21.4 10.6 %collective-permute-start.6 = (bf16[64,4224]{1,0:T(8,128)(2,1)S(1)}, bf16[64,4224]{1,0:T(8,128)(2,1)S(1)}, u32[]{:S(2)}, u32[]{:S(2)}) collective-permute-start(bf16[64,4224]{1,0:T(8,128)(2,1)S(1)} %constant_dynamic-update-slice_fusion.refs_0_), channel_id=1, source_target_pairs={{3,0},{0,1},{1,2},{2,3},{7,4},{4,5},{5,6},{6,7},{11,8},{8,9},{9,10... | collective-permute-start | bytes 1622024 | tf_op jit(solution)/shard_map/ppermute | solution.py:62
  21.4 20.5 %collective-permute-start.10 = (bf16[64,4224]{1,0:T(8,128)(2,1)S(1)}, bf16[64,4224]{1,0:T(8,128)(2,1)S(1)}, u32[]{:S(2)}, u32[]{:S(2)}) collective-permute-start(bf16[64,4224]{1,0:T(8,128)(2,1)S(1)} %constant_dynamic-update-slice_fusion.refs_0_), channel_id=1, source_target_pairs={{16,0},{0,16},{17,1},{1,17},{18,2},{2,18},{19,3},{3,19},{20,4},{4,... | collective-permute-start | bytes 1622024 | tf_op jit(solution)/shard_map/ppermute | solution.py:71
  28.3 21.9 %collective-permute-start.11 = (bf16[64,4224]{1,0:T(8,128)(2,1)S(1)}, bf16[64,4224]{1,0:T(8,128)(2,1)S(1)}, u32[]{:S(2)}, u32[]{:S(2)}) collective-permute-start(bf16[64,4224]{1,0:T(8,128)(2,1)S(1)} %collective-permute-done.4.refs_0_), channel_id=1, source_target_pairs={{16,0},{0,16},{17,1},{1,17},{18,2},{2,18},{19,3},{3,19},{20,4},{4,... | collective-permute-start | bytes 1622024 | tf_op jit(solution)/shard_map/ppermute | solution.py:71
  32.0 18.2 %collective-permute-start.12 = (bf16[64,4224]{1,0:T(8,128)(2,1)S(1)}, bf16[64,4224]{1,0:T(8,128)(2,1)S(1)}, u32[]{:S(2)}, u32[]{:S(2)}) collective-permute-start(bf16[64,4224]{1,0:T(8,128)(2,1)S(1)} %collective-permute-done.6.refs_1_), channel_id=1, source_target_pairs={{16,0},{0,16},{17,1},{1,17},{18,2},{2,18},{19,3},{3,19},{20,4},{4,... | collective-permute-start | bytes 1622024 | tf_op jit(solution)/shard_map/ppermute | solution.py:71
  32.7 6.7 %collective-permute-start.5 = (bf16[32,4224]{1,0:T(8,128)(2,1)}, bf16[32,4224]{1,0:T(8,128)(2,1)S(1)}, u32[]{:S(2)}, u32[]{:S(2)}) collective-permute-start(bf16[32,4224]{1,0:T(8,128)(2,1)} %slice.107), channel_id=1, source_target_pairs={{1,0},{2,1},{3,2},{0,3},{5,4},{6,5},{7,6},{4,7},{9,8},{10,9},{11,1... | collective-permute-start | bytes 811016 | tf_op jit(solution)/shard_map/ppermute | solution.py:62
  33.9 8.0 %collective-permute-start.7 = (bf16[32,4224]{1,0:T(8,128)(2,1)}, bf16[32,4224]{1,0:T(8,128)(2,1)}, u32[]{:S(2)}, u32[]{:S(2)}) collective-permute-start(bf16[32,4224]{1,0:T(8,128)(2,1)} %slice.108), channel_id=1, source_target_pairs={{3,0},{0,1},{1,2},{2,3},{7,4},{4,5},{5,6},{6,7},{11,8},{8,9},{9,10... | collective-permute-start | bytes 811016 | tf_op jit(solution)/shard_map/ppermute | solution.py:62
  39.4 15.0 %collective-permute-start.8 = (bf16[32,4224]{1,0:T(8,128)(2,1)S(1)}, bf16[32,4224]{1,0:T(8,128)(2,1)S(1)}, u32[]{:S(2)}, u32[]{:S(2)}) collective-permute-start(bf16[32,4224]{1,0:T(8,128)(2,1)S(1)} %collective-permute-done.5.refs_0_), channel_id=1, source_target_pairs={{16,0},{0,16},{17,1},{1,17},{18,2},{2,18},{19,3},{3,19},{20,4},{4,... | collective-permute-start | bytes 811016 | tf_op jit(solution)/shard_map/ppermute | solution.py:71
  41.9 12.5 %collective-permute-start.9 = (bf16[32,4224]{1,0:T(8,128)(2,1)}, bf16[32,4224]{1,0:T(8,128)(2,1)S(1)}, u32[]{:S(2)}, u32[]{:S(2)}) collective-permute-start(bf16[32,4224]{1,0:T(8,128)(2,1)} %collective-permute-done.7.refs_1_), channel_id=1, source_target_pairs={{16,0},{0,16},{17,1},{1,17},{18,2},{2,18},{19,3},{3,19},{20,4},{4,... | collective-permute-start | bytes 811016 | tf_op jit(solution)/shard_map/ppermute | solution.py:71
  41.9 3.4 %copy-start = (bf16[1,1024,4096]{2,1,0:T(8,128)(2,1)S(1)}, bf16[1,1024,4096]{2,1,0:T(8,128)(2,1)}, u32[]{:S(2)}) copy-start(bf16[1,1024,4096]{2,1,0:T(8,128)(2,1)} %param.7) | copy-start | bytes 25165828
  65.7 3.8 %collective-permute-start.13 = (f32[8,512]{1,0:T(8,128)S(1)}, f32[8,512]{1,0:T(8,128)S(1)}, u32[]{:S(2)}, u32[]{:S(2)}) collective-permute-start(f32[8,512]{1,0:T(8,128)S(1)} %shard_map.95.refs_0_), channel_id=1, source_target_pairs={{4,0},{8,4},{12,8},{0,12},{5,1},{9,5},{13,9},{1,13},{6,2},{10,6},{... | collective-permute-start | bytes 49160 | tf_op jit(solution)/shard_map/ppermute | solution.py:71
  66.3 5.2 %collective-permute-start.14 = (f32[8,512]{1,0:T(8,128)S(1)}, f32[8,512]{1,0:T(8,128)S(1)}, u32[]{:S(2)}, u32[]{:S(2)}) collective-permute-start(f32[8,512]{1,0:T(8,128)S(1)} %shard_map.95.refs_0_), channel_id=1, source_target_pairs={{8,0},{12,4},{0,8},{4,12},{9,1},{13,5},{1,9},{5,13},{10,2},{14,6},... | collective-permute-start | bytes 49160 | tf_op jit(solution)/shard_map/ppermute | solution.py:71
  67.3 4.9 %collective-permute-start.15 = (f32[8,512]{1,0:T(8,128)S(1)}, f32[8,512]{1,0:T(8,128)S(1)}, u32[]{:S(2)}, u32[]{:S(2)}) collective-permute-start(f32[8,512]{1,0:T(8,128)S(1)} %shard_map.95.refs_0_), channel_id=1, source_target_pairs={{12,0},{0,4},{4,8},{8,12},{13,1},{1,5},{5,9},{9,13},{14,2},{2,6},{... | collective-permute-start | bytes 49160 | tf_op jit(solution)/shard_map/ppermute | solution.py:71
  72.8 3.8 %collective-permute-start.16 = (f32[8,512]{1,0:T(8,128)S(1)}, f32[8,512]{1,0:T(8,128)S(1)}, u32[]{:S(2)}, u32[]{:S(2)}) collective-permute-start(f32[8,512]{1,0:T(8,128)S(1)} %shard_map.96.refs_0_), channel_id=1, source_target_pairs={{1,0},{2,1},{3,2},{0,3},{5,4},{6,5},{7,6},{4,7},{9,8},{10,9},{11,1... | collective-permute-start | bytes 49160 | tf_op jit(solution)/shard_map/ppermute | solution.py:71
  72.9 5.3 %collective-permute-start.17 = (f32[8,512]{1,0:T(8,128)S(1)}, f32[8,512]{1,0:T(8,128)S(1)}, u32[]{:S(2)}, u32[]{:S(2)}) collective-permute-start(f32[8,512]{1,0:T(8,128)S(1)} %shard_map.96.refs_0_), channel_id=1, source_target_pairs={{2,0},{3,1},{0,2},{1,3},{6,4},{7,5},{4,6},{5,7},{10,8},{11,9},{8,1... | collective-permute-start | bytes 49160 | tf_op jit(solution)/shard_map/ppermute | solution.py:71
  75.2 4.9 %collective-permute-start.18 = (f32[8,512]{1,0:T(8,128)S(1)}, f32[8,512]{1,0:T(8,128)S(1)}, u32[]{:S(2)}, u32[]{:S(2)}) collective-permute-start(f32[8,512]{1,0:T(8,128)S(1)} %shard_map.96.refs_0_), channel_id=1, source_target_pairs={{3,0},{0,1},{1,2},{2,3},{7,4},{4,5},{5,6},{6,7},{11,8},{8,9},{9,10... | collective-permute-start | bytes 49160 | tf_op jit(solution)/shard_map/ppermute | solution.py:71
  92.2 14.7 %collective-permute-start.19 = (bf16[256,4096]{1,0:T(8,128)(2,1)}, bf16[256,4096]{1,0:T(8,128)(2,1)}, u32[]{:S(2)}, u32[]{:S(2)}) collective-permute-start(bf16[256,4096]{1,0:T(8,128)(2,1)} %get-tuple-element.46), channel_id=1, source_target_pairs={{16,0},{0,16},{17,1},{1,17},{18,2},{2,18},{19,3},{3,19},{20,4},{4,... | collective-permute-start | bytes 6291464 | tf_op jit(solution)/shard_map/ppermute | solution.py:71
  94.5 12.4 %collective-permute-start.31 = (bf16[64,1024]{1,0:T(8,128)(2,1)S(1)}, bf16[64,1024]{1,0:T(8,128)(2,1)S(1)}, u32[]{:S(2)}, u32[]{:S(2)}) collective-permute-start(bf16[64,1024]{1,0:T(8,128)(2,1)S(1)} %get-tuple-element.49), channel_id=1, source_target_pairs={{192,0},{0,64},{64,128},{128,192},{193,1},{1,65},{65,129},{129,193... | collective-permute-start | bytes 393224 | tf_op jit(solution)/shard_map/ppermute | solution.py:71
  99.0 33.0 %collective-permute-start.28 = (bf16[128,1024]{1,0:T(8,128)(2,1)S(1)}, bf16[128,1024]{1,0:T(8,128)(2,1)S(1)}, u32[]{:S(2)}, u32[]{:S(2)}) collective-permute-start(bf16[128,1024]{1,0:T(8,128)(2,1)S(1)} %get-tuple-element.67), channel_id=1, source_target_pairs={{64,0},{128,64},{192,128},{0,192},{65,1},{129,65},{193,129},{1,193... | collective-permute-start | bytes 786440 | tf_op jit(solution)/shard_map/ppermute | solution.py:71
  101.2 34.1 %collective-permute-start.29 = (bf16[128,1024]{1,0:T(8,128)(2,1)S(1)}, bf16[128,1024]{1,0:T(8,128)(2,1)S(1)}, u32[]{:S(2)}, u32[]{:S(2)}) collective-permute-start(bf16[128,1024]{1,0:T(8,128)(2,1)S(1)} %get-tuple-element.66), channel_id=1, source_target_pairs={{128,0},{192,64},{0,128},{64,192},{129,1},{193,65},{1,129},{65,193... | collective-permute-start | bytes 786440 | tf_op jit(solution)/shard_map/ppermute | solution.py:71
  106.2 30.0 %collective-permute-start.30 = (bf16[128,1024]{1,0:T(8,128)(2,1)S(1)}, bf16[128,1024]{1,0:T(8,128)(2,1)S(1)}, u32[]{:S(2)}, u32[]{:S(2)}) collective-permute-start(bf16[128,1024]{1,0:T(8,128)(2,1)S(1)} %get-tuple-element.65), channel_id=1, source_target_pairs={{192,0},{0,64},{64,128},{128,192},{193,1},{1,65},{65,129},{129,193... | collective-permute-start | bytes 786440 | tf_op jit(solution)/shard_map/ppermute | solution.py:71
  109.4 7.9 %collective-permute-start.20 = (bf16[32,4096]{1,0:T(8,128)(2,1)S(1)}, bf16[32,4096]{1,0:T(8,128)(2,1)S(1)}, u32[]{:S(2)}, u32[]{:S(2)}) collective-permute-start(bf16[32,4096]{1,0:T(8,128)(2,1)S(1)} %get-tuple-element.61), channel_id=1, source_target_pairs={{3,0},{0,1},{1,2},{2,3},{7,4},{4,5},{5,6},{6,7},{11,8},{8,9},{9,10... | collective-permute-start | bytes 786440 | tf_op jit(solution)/shard_map/ppermute | solution.py:62
  109.7 11.1 %collective-permute-start.22 = (bf16[32,4096]{1,0:T(8,128)(2,1)S(1)}, bf16[32,4096]{1,0:T(8,128)(2,1)S(1)}, u32[]{:S(2)}, u32[]{:S(2)}) collective-permute-start(bf16[32,4096]{1,0:T(8,128)(2,1)S(1)} %get-tuple-element.62), channel_id=1, source_target_pairs={{1,0},{2,1},{3,2},{0,3},{5,4},{6,5},{7,6},{4,7},{9,8},{10,9},{11,1... | collective-permute-start | bytes 786440 | tf_op jit(solution)/shard_map/ppermute | solution.py:62
  117.3 14.6 %collective-permute-start.33 = (bf16[64,1024]{1,0:T(8,128)(2,1)S(1)}, bf16[64,1024]{1,0:T(8,128)(2,1)S(1)}, u32[]{:S(2)}, u32[]{:S(2)}) collective-permute-start(bf16[64,1024]{1,0:T(8,128)(2,1)S(1)} %get-tuple-element.51), channel_id=1, source_target_pairs={{64,0},{128,64},{192,128},{0,192},{65,1},{129,65},{193,129},{1,193... | collective-permute-start | bytes 393224 | tf_op jit(solution)/shard_map/ppermute | solution.py:71
  121.0 28.0 %copy-start.1 = (f32[128,1024]{1,0:T(8,128)S(1)}, f32[128,1024]{1,0:T(8,128)}, u32[]{:S(2)}) copy-start(f32[128,1024]{1,0:T(8,128)} %outer.1) | copy-start | bytes 1572868
  121.0 28.0 %copy-start.2 = (f32[128,1024]{1,0:T(8,128)S(1)}, f32[128,1024]{1,0:T(8,128)}, u32[]{:S(2)}) copy-start(f32[128,1024]{1,0:T(8,128)} %momentum.1) | copy-start | bytes 1572868
  121.1 32.7 %collective-permute-start.23 = (bf16[64,4096]{1,0:T(8,128)(2,1)S(1)}, bf16[64,4096]{1,0:T(8,128)(2,1)S(1)}, u32[]{:S(2)}, u32[]{:S(2)}) collective-permute-start(bf16[64,4096]{1,0:T(8,128)(2,1)S(1)} %pad_maximum_fusion.1), channel_id=1, source_target_pairs={{1,0},{2,1},{3,2},{0,3},{5,4},{6,5},{7,6},{4,7},{9,8},{10,9},{11,1... | collective-permute-start | bytes 1572872 | tf_op jit(solution)/shard_map/ppermute | solution.py:62
  131.9 21.8 %collective-permute-start.21 = (bf16[64,4096]{1,0:T(8,128)(2,1)S(1)}, bf16[64,4096]{1,0:T(8,128)(2,1)S(1)}, u32[]{:S(2)}, u32[]{:S(2)}) collective-permute-start(bf16[64,4096]{1,0:T(8,128)(2,1)S(1)} %pad_maximum_fusion), channel_id=1, source_target_pairs={{3,0},{0,1},{1,2},{2,3},{7,4},{4,5},{5,6},{6,7},{11,8},{8,9},{9,10... | collective-permute-start | bytes 1572872 | tf_op jit(solution)/shard_map/ppermute | solution.py:62
  132.0 14.8 %collective-permute-start.32 = (bf16[128,1024]{1,0:T(8,128)(2,1)S(1)}, bf16[128,1024]{1,0:T(8,128)(2,1)S(1)}, u32[]{:S(2)}, u32[]{:S(2)}) collective-permute-start(bf16[128,1024]{1,0:T(8,128)(2,1)S(1)} %pad_maximum_fusion.2), channel_id=1, source_target_pairs={{192,0},{0,64},{64,128},{128,192},{193,1},{1,65},{65,129},{129,193... | collective-permute-start | bytes 786440 | tf_op jit(solution)/shard_map/ppermute | solution.py:71
  135.3 13.6 %collective-permute-start.34 = (bf16[128,1024]{1,0:T(8,128)(2,1)S(1)}, bf16[128,1024]{1,0:T(8,128)(2,1)S(1)}, u32[]{:S(2)}, u32[]{:S(2)}) collective-permute-start(bf16[128,1024]{1,0:T(8,128)(2,1)S(1)} %pad_maximum_fusion.3), channel_id=1, source_target_pairs={{64,0},{128,64},{192,128},{0,192},{65,1},{129,65},{193,129},{1,193... | collective-permute-start | bytes 786440 | tf_op jit(solution)/shard_map/ppermute | solution.py:71
  150.8 14.1 %collective-permute-start.35 = (bf16[128,1024]{1,0:T(8,128)(2,1)S(1)}, bf16[128,1024]{1,0:T(8,128)(2,1)S(1)}, u32[]{:S(2)}, u32[]{:S(2)}) collective-permute-start(bf16[128,1024]{1,0:T(8,128)(2,1)S(1)} %get-tuple-element.54.first), channel_id=1, source_target_pairs={{64,0},{128,64},{192,128},{0,192},{65,1},{129,65},{193,129},{1,193... | collective-permute-start | bytes 786440 | tf_op jit(solution)/shard_map/ppermute | solution.py:71
  153.2 15.0 %collective-permute-start.37 = (bf16[128,1024]{1,0:T(8,128)(2,1)S(1)}, bf16[128,1024]{1,0:T(8,128)(2,1)S(1)}, u32[]{:S(2)}, u32[]{:S(2)}) collective-permute-start(bf16[128,1024]{1,0:T(8,128)(2,1)S(1)} %get-tuple-element.54.first), channel_id=1, source_target_pairs={{192,0},{0,64},{64,128},{128,192},{193,1},{1,65},{65,129},{129,193... | collective-permute-start | bytes 786440 | tf_op jit(solution)/shard_map/ppermute | solution.py:71
  153.9 14.4 %collective-permute-start.26 = (bf16[16,4096]{1,0:T(8,128)(2,1)S(1)}, bf16[16,4096]{1,0:T(8,128)(2,1)S(1)}, u32[]{:S(2)}, u32[]{:S(2)}) collective-permute-start(bf16[16,4096]{1,0:T(8,128)(2,1)S(1)} %get-tuple-element.70), channel_id=1, source_target_pairs={{4,0},{5,1},{6,2},{7,3},{8,4},{9,5},{10,6},{11,7},{12,8},{13,9},{1... | collective-permute-start | bytes 393224 | tf_op jit(solution)/shard_map/ppermute | solution.py:66
  156.4 12.0 %collective-permute-start.25 = (bf16[16,4096]{1,0:T(8,128)(2,1)S(1)}, bf16[16,4096]{1,0:T(8,128)(2,1)S(1)}, u32[]{:S(2)}, u32[]{:S(2)}) collective-permute-start(bf16[16,4096]{1,0:T(8,128)(2,1)S(1)} %get-tuple-element.71), channel_id=1, source_target_pairs={{8,0},{9,1},{10,2},{11,3},{12,4},{13,5},{14,6},{15,7},{0,8},{1,9},... | collective-permute-start | bytes 393224 | tf_op jit(solution)/shard_map/ppermute | solution.py:66
  156.7 11.7 %collective-permute-start.24 = (bf16[16,4096]{1,0:T(8,128)(2,1)S(1)}, bf16[16,4096]{1,0:T(8,128)(2,1)S(1)}, u32[]{:S(2)}, u32[]{:S(2)}) collective-permute-start(bf16[16,4096]{1,0:T(8,128)(2,1)S(1)} %get-tuple-element.69), channel_id=1, source_target_pairs={{12,0},{13,1},{14,2},{15,3},{0,4},{1,5},{2,6},{3,7},{4,8},{5,9},{6... | collective-permute-start | bytes 393224 | tf_op jit(solution)/shard_map/ppermute | solution.py:66
  165.0 7.0 %collective-permute-start.36 = (bf16[64,1024]{1,0:T(8,128)(2,1)S(1)}, bf16[64,1024]{1,0:T(8,128)(2,1)S(1)}, u32[]{:S(2)}, u32[]{:S(2)}) collective-permute-start(bf16[64,1024]{1,0:T(8,128)(2,1)S(1)} %slice.122), channel_id=1, source_target_pairs={{64,0},{128,64},{192,128},{0,192},{65,1},{129,65},{193,129},{1,193... | collective-permute-start | bytes 393224 | tf_op jit(solution)/shard_map/ppermute | solution.py:71
  168.3 8.0 %collective-permute-start.38 = (bf16[64,1024]{1,0:T(8,128)(2,1)S(1)}, bf16[64,1024]{1,0:T(8,128)(2,1)S(1)}, u32[]{:S(2)}, u32[]{:S(2)}) collective-permute-start(bf16[64,1024]{1,0:T(8,128)(2,1)S(1)} %slice.123), channel_id=1, source_target_pairs={{192,0},{0,64},{64,128},{128,192},{193,1},{1,65},{65,129},{129,193... | collective-permute-start | bytes 393224 | tf_op jit(solution)/shard_map/ppermute | solution.py:71
  168.5 9.4 %collective-permute-start.27 = (bf16[8,4096]{1,0:T(8,128)(2,1)S(1)}, bf16[8,4096]{1,0:T(8,128)(2,1)S(1)}, u32[]{:S(2)}, u32[]{:S(2)}) collective-permute-start(bf16[8,4096]{1,0:T(8,128)(2,1)S(1)} %slice.142), channel_id=1, source_target_pairs={{32,0},{0,32},{33,1},{1,33},{34,2},{2,34},{35,3},{3,35},{36,4},{4,... | collective-permute-start | bytes 196616 | tf_op jit(solution)/shard_map/ppermute | solution.py:71
where the time goes:
time: 180 us; the launch traced here: 179 us
  waiting for transfers between devices  75.5 us (42%)
  starting transfers between devices  50.3 us (28%)
  Pallas kernels  30.9 us (17%)
  local copies, waits for them, and re-layouts  8.78 us (5%)
  other arithmetic  6.69 us (4%)
  blocking collectives  5.42 us (3%)
    ppermute x25, waiting for transfers between devices, take(): return lax.ppermute(value, axis, [((i + k) % n, i) for i in range(n)])  48 us
    ppermute x25, starting transfers between devices, take(): return lax.ppermute(value, axis, [((i + k) % n, i) for i in range(n)])  33 us
    pallas_call x9, Pallas kernels, call(): pl.pallas_call(kernel, in_specs=[SMEM] + [specs.get(k, VMEM) for k in ran...  30.9 us
    ppermute x8, waiting for transfers between devices, take_outer(): return lax.ppermute(value, (CORE, X, Y), by_core(k, False))  21.3 us
    ppermute x8, starting transfers between devices, take_outer(): return lax.ppermute(value, (CORE, X, Y), by_core(k, False))  8.73 us
    ppermute x6, starting transfers between devices, take_inner(): return lax.ppermute(value, (CORE, X, Y), by_core(k, True))  8.58 us
    ppermute x6, waiting for transfers between devices, take_inner(): return lax.ppermute(value, (CORE, X, Y), by_core(k, True))  6.24 us
    all_gather x1, blocking collectives, per_device(): stats = lax.all_gather(stats, TOK)  5.42 us
  transfers between devices with their start and end apart: 39, of which 22 were waited for; matrix products, arithmetic and copies ran while one was open for 5% of the time, Pallas kernels for 7%

commit v1 on v0

v1 whole, which is shorter than its diff:
```python
import functools

import jax
import jax.numpy as jnp
from jax import lax
from jax.experimental import pallas as pl
from jax.experimental.pallas import tpu as pltpu
from jax.sharding import Mesh
from jax.sharding import PartitionSpec as P

TOK = ("tok_0", "tok_1")
VOC = ("voc_0", "voc_1")
TOK_VOC = ("tok_0", "tok_1", "voc_0", "voc_1")
Z, CORE, X, Y = TOK_VOC
F32, BF16 = jnp.float32, jnp.bfloat16

PARTS = (
    (0, 0, 0, 4), (1, 0, 0, 4),
    (0, 1, 0, 4), (0, 3, 0, 4), (1, 1, 0, 4), (1, 3, 0, 4),
    (0, 2, 0, 2), (0, 2, 2, 2), (1, 2, 0, 2), (1, 2, 2, 2),
)


inner_rate = 0.5
outer_rate = 0.7
momentum_coef = 0.9
SMEM = pl.BlockSpec(memory_space=pltpu.SMEM)
VMEM = pl.BlockSpec(memory_space=pltpu.VMEM)


def call(kernel, out, *operands, flops=0, scratch=(), limit=16, specs={}, out_spec=VMEM):
    moved = sum(leaf.size * leaf.dtype.itemsize for leaf in jax.tree.leaves((operands, out)))
    return pl.pallas_call(
        kernel,
        in_specs=[SMEM] + [specs.get(k, VMEM) for k in range(1, len(operands))],
        out_specs=jax.tree.map(lambda _: out_spec, out),
        out_shape=out,
        scratch_shapes=scratch,
        compiler_params=pltpu.CompilerParams(vmem_limit_bytes=limit << 20),
        cost_estimate=pl.CostEstimate(
            flops=flops or moved, bytes_accessed=moved, transcendentals=0
        ),
    )(*operands)


def shaped(dtype, *shape):
    return jax.ShapeDtypeStruct(shape, dtype)


def by_core(k, inner):
    pairs = []
    for core in range(2):
        for x in range(4):
            for y in range(4):
                along_x = (core == 1) != inner
                fx, fy = ((x + k) % 4, y) if along_x else (x, (y + k) % 4)
                pairs.append(((core * 4 + fx) * 4 + fy, (core * 4 + x) * 4 + y))
    return pairs


def take_outer(value, k):
    return lax.ppermute(value, (CORE, X, Y), by_core(k, False))


def take_inner(value, k):
    return lax.ppermute(value, (CORE, X, Y), by_core(k, True))


def take_across(value, k):
    pairs = by_core(k, True)
    half = len(pairs)
    both = [(a + (1 - z) * half, b + z * half) for z in range(2) for a, b in pairs]
    return lax.ppermute(value, (Z, CORE, X, Y), both)


def take(value, axis, k):
    n = lax.axis_size(axis)
    return lax.ppermute(value, axis, [((i + k) % n, i) for i in range(n)])


def along(axis):
    return lambda value, k: take(value, axis, k)


def ring_gather(value, take):
    half = value.shape[0] // 2
    up = take(value, 1)
    down = take(value, -1)
    far_up = take(up[:half], 1)
    far_down = take(down[half:], -1)
    return value, up, far_up, far_down, down


def to_f32(value):
    return value.astype(F32)


def arrivals(pieces, take):
    found = []
    for k, piece in zip((2, 1, 3), (pieces[1], pieces[0], pieces[2])):
        found.append(take(piece, -k))
    return found


def part_tokens(here, own, other, a, first, count):
    row = lax.broadcasted_iota(jnp.int32, (count * 2 * own, 1), 0)
    t, plane, b = row % own, row // own % 2, row // (2 * own) + first
    z, c = (here[0] + plane) % 2, (here[1] + other) % 2
    x = (here[2] + jnp.where(c == 0, b, a)) % 4
    y = (here[3] + jnp.where(c == 0, a, b)) % 4
    return (((z * 2 + c) * 4 + x) * 4 + y) * own + t


def token_table(here, tokens, own):
    lane = lax.broadcasted_iota(jnp.int32, (1, tokens), 1)
    rows = [
        part_tokens(here, own, other, a, first, count) == lane for other, a, first, count in PARTS
    ]
    return jnp.concatenate([one.astype(F32) for one in rows]).astype(BF16)


def in_three(value):
    high = value.astype(BF16)
    rest = value - high.astype(F32)
    middle = rest.astype(BF16)
    return high, middle, (rest - middle.astype(F32)).astype(BF16)


def reordered(value, table, dims):
    dot = lambda one: lax.dot_general(one, table, (dims, ((), ())), preferred_element_type=F32)
    return sum(dot(one) for one in in_three(value))


def logits_kernel(count, before, here, *refs):
    parts, refs = refs[:count], refs[count:]
    first = not before
    w_in, tables, (logits, ids, states, table, *more) = refs[0], refs[1 : 1 + before], refs[1 + before :]
    w = more[0] if first else w_in
    vocab_rows, width = w.shape
    block = 256

    def copy(k):
        at = pl.ds(k * block, block)
        return pltpu.make_async_copy(w_in.at[at, :], w.at[at, :], more[1].at[k])

    if first:
        for k in range(vocab_rows // block):
            copy(k).start()
    start = 0
    for part in parts:
        at = pl.ds(start, part.shape[0])
        states[at, :] = part[:, :width]
        codes = part[:, width:].astype(F32).astype(jnp.int32)
        ids[at, :] = codes[:, :1] * 256 + codes[:, 1:2]
        start += part.shape[0]
    rows = states.shape[0]
    lane = lax.broadcasted_iota(jnp.int32, (1, 128), 1)

    def step(j, carry):
        top, total, target = carry
        column = pl.multiple_of(j * block, block)
        if first:
            rows_at = pl.ds(column, block)
            pltpu.make_async_copy(w_in.at[rows_at, :], w.at[rows_at, :], more[1].at[j]).wait()
        out = lax.dot_general(
            states[...], w[pl.ds(column, block), :], (((1,), (1,)), ((), ())),
            preferred_element_type=F32,
        ) * (width ** (-0.5))
        logits[:, pl.ds(column, block)] = out
        hits = ids[...] - (here[4] + column)
        lanes = [out[:, k : k + 128] for k in range(0, block, 128)]
        peak = top
        for one in lanes:
            peak = jnp.maximum(peak, one)
        total = total * jnp.exp(top - peak)
        for k, one in enumerate(lanes):
            total = total + jnp.exp(one - peak)
            target = target + jnp.where(hits - k * 128 == lane, one, 0.0)
        return peak, total, target

    zero = jnp.zeros((rows, 128), F32)
    peak, total, target = lax.fori_loop(
        0, vocab_rows // block, step, (jnp.full((rows, 128), -jnp.inf, F32), zero, zero)
    )
    best = jnp.max(peak, axis=1, keepdims=True)
    mass = jnp.sum(total * jnp.exp(peak - best), axis=1, keepdims=True)
    hit = jnp.sum(target, axis=1, keepdims=True)
    mine = jnp.where(lane == 0, best, jnp.where(lane == 1, mass, jnp.where(lane == 2, hit, 0.0)))
    if before < 3:
        table[...] = mine
    else:
        every = jnp.concatenate([one[...] for one in tables[:2]] + [mine])
        table[...] = reordered(every, tables[2][...], ((0,), (0,)))[:8]


def merged(parts):
    top = parts[0][0:1]
    for one in parts[1:]:
        top = jnp.maximum(top, one[0:1])
    total = sum(one[1:2] * jnp.exp(one[0:1] - top) for one in parts)
    return top, total, sum(one[2:3] for one in parts)


def merge_kernel(here, got, out):
    top, total, target = merged([got[k] for k in range(got.shape[0])])
    row = lax.broadcasted_iota(jnp.int32, out.shape[1:], 0)
    stats = jnp.where(row == 0, top, jnp.where(row == 1, total, jnp.where(row == 2, target, 0.0)))
    for k in range(out.shape[0]):
        out[k] = stats


def slab_kernel(own, part, here, *refs):
    got, logits, ids, states, table, outs = refs[0], refs[1:4], refs[4:7], refs[7:10], refs[10], refs[11:]
    loss, log_total, mine, *sent, errors = outs
    width = 4 * part
    top, total, target = merged([got[k] for k in range(got.shape[0])])
    every = top + jnp.log(total)
    row = lax.broadcasted_iota(jnp.int32, got.shape[1:], 0)
    both = jnp.where(row == 0, every, jnp.where(row == 1, every - target, 0.0))
    columns = sum(
        lax.dot_general(table[...], one, (((1,), (1,)), ((), ())), preferred_element_type=F32)
        for one in in_three(both)
    )
    log_total[...] = columns[:, 0:1]
    loss[...] = columns[:own, 1:2]
    strip = mine.shape[0]
    lane = lax.broadcasted_iota(jnp.int32, (1, strip), 1)
    start = 0
    for values, id_part in zip(logits, ids):
        end = start + values.shape[0]
        onehot = (id_part[...] - here[4] == lane).astype(F32)
        part_errors = jnp.exp(values[:, :strip] - columns[start:end, 0:1]) - onehot
        errors[:, start:end] = part_errors.T.astype(BF16)
        start = end

    def grad(k):
        at = pl.multiple_of(lax.rem(here[5] + k, 4) * part, part)
        total, start = 0.0, 0
        for state in states:
            end = start + state.shape[0]
            total += jnp.dot(
                errors[:, start:end], state[:, pl.ds(at, part)], preferred_element_type=F32
            )
            start = end
        return total * (width ** (-0.5))

    for k in (2, 1, 3):
        sent[k - 1][...] = grad(k).astype(BF16)
    mine[...] = grad(0)


def hidden_kernel(other, here, *refs):
    logits, ids, (log_total, w, out, errors) = refs[:3], refs[3:6], refs[6:]
    vocab_rows, width = w.shape
    block, strip = 512, 128
    lane = lax.broadcasted_iota(jnp.int32, (1, strip), 1)
    unit = out.shape[0] // 4
    start = 0
    for values, id_part, lines in zip(logits, ids, ((0,), (1, 3), (2,))):
        for n, line in enumerate(lines):
            first = (other * len(lines) + n) * unit
            hits = id_part[first : first + unit, :] - here[4]
            total = log_total[start + first : start + first + unit, :]
            for k in range(0, vocab_rows, strip):
                onehot = (hits - k == lane).astype(F32)
                errors[line * unit : (line + 1) * unit, k : k + strip] = (
                    jnp.exp(values[first : first + unit, k : k + strip] - total) - onehot
                ).astype(BF16)
        start += values.shape[0]

    def step(j, _):
        cols = pl.ds(pl.multiple_of(j * block, block), block)
        grad = jnp.dot(errors[...], w[:, cols], preferred_element_type=F32) * (width ** (-0.5))
        out[:, cols] = grad.astype(BF16)
        return 0

    lax.fori_loop(0, width // block, step, 0)


def outer_kernel(here, outer, momentum, w0, w1, w2, w3, g0, g1, g2, g3, *outs):
    mean_weight = (to_f32(w0[...]) + to_f32(w1[...]) + to_f32(w2[...]) + to_f32(w3[...])) / 4
    slab_grad = g0[...] + to_f32(g1[...]) + to_f32(g2[...]) + to_f32(g3[...])
    pseudo_grad = outer[...] - (mean_weight - (inner_rate / 4) * slab_grad)
    moved = momentum_coef * momentum[...] + pseudo_grad
    new_outer = outer[...] - outer_rate * (pseudo_grad + momentum_coef * moved)
    outs[0][...] = new_outer.astype(outs[0].dtype)
    if len(outs) == 2:
        outs[1][...] = moved


def join_kernel(here, *refs):
    pieces, out = refs[:-1], refs[-1]
    rows = pieces[0].shape[0]
    for k, piece in enumerate(pieces):
        out[k * rows : (k + 1) * rows, :] = piece[...]


def table_kernel(own, here, out):
    out[...] = token_table(here, out.shape[0], own)


def loss_kernel(here, column, row):
    size = column.shape[0]
    at = [lax.broadcasted_iota(jnp.int32, (size, size), dim) for dim in (0, 1)]
    row[...] = jnp.sum(jnp.where(at[0] == at[1], column[...], 0.0), axis=0, keepdims=True)


def place_kernel(part, here, mine, up, low, high, down, out, sems):
    half = low.shape[0]

    def copy(piece, k, first, n):
        at = pl.multiple_of(lax.rem(here[5] + k, 4) * part, part)
        to = out.at[pl.ds(first, piece.shape[0]), pl.ds(at, part)]
        return pltpu.make_async_copy(piece, to, sems.at[n])

    copies = [
        copy(mine, 0, 0, 0), copy(up, 1, 0, 1), copy(low, 2, 0, 2), copy(high, 2, half, 3), copy(down, 3, 0, 4)
    ]
    for one in copies:
        one.start()
    for one in copies:
        one.wait()


def per_device(hidden, targets, unembed, outer_weight, momentum):
    weights = unembed[0]
    vocab_rows, width = weights.shape
    own = hidden.shape[1]
    slab_rows, part = outer_weight.shape
    reps = lax.axis_size("rep")
    rep = lax.axis_index("rep")
    tokens = own * lax.axis_size(TOK_VOC)
    group_index = lax.axis_index(TOK) * lax.axis_size(VOC) + lax.axis_index(VOC)
    here = jnp.stack(
        [lax.axis_index(a) for a in TOK_VOC] + [group_index * vocab_rows, rep]
    ).astype(jnp.int32)

    ids = targets[0]
    codes = jnp.stack((ids >> 8, ids & 255), 1).astype(BF16)
    piece = jnp.concatenate((hidden[0], jnp.pad(codes, ((0, 0), (0, 126)))), 1)
    cells = {(0, 0): piece}
    order = call(functools.partial(table_kernel, own), shaped(BF16, tokens, tokens), here)
    for k in (2, 1, 3, 0):
        for plane, get in ((1, take_across), (0, take_inner)):
            if k or plane:
                cells[k, plane] = get(piece, k)
    cells = [cells[k, plane] for k in range(4) for plane in range(2)]
    line = call(join_kernel, shaped(BF16, 8 * own, piece.shape[1]), here, *cells)
    up = take_outer(line, 1)
    down = take_outer(line, -1)
    cut = line.shape[0] // 2
    far_up = take_outer(up[:cut], 1)
    far_down = take_outer(down[cut:], -1)

    def with_other(*parts):
        return (*parts, *[take(one, CORE, 1) for one in parts])

    def features(value, k):
        return lax.dynamic_slice_in_dim(value, ((rep + k) % reps) * part, part, 1)

    slab = weights[:slab_rows]
    slab_weights = [features(slab, 0)]
    for k in (1, 2, 3):
        slab_weights.append(take(features(slab, -k), "rep", k))

    def logits_of(parts, w, tables):
        rows = sum(one.shape[0] for one in parts)
        out = [
            shaped(F32, rows, vocab_rows),
            shaped(jnp.int32, rows, 1),
            shaped(BF16, rows, width),
            shaped(F32, *((8, tokens) if len(tables) == 3 else (rows, 128))),
        ]
        kind = {}
        if not tables:
            out.append(shaped(BF16, vocab_rows, width))
            kind = dict(
                scratch=[pltpu.SemaphoreType.DMA((4,))],
                specs={len(parts) + 1: pl.BlockSpec(memory_space=pltpu.HBM)},
                limit=40,
            )
        return call(
            functools.partial(logits_kernel, len(parts), len(tables)),
            out, here, *parts, w, *tables,
            flops=2 * max(rows, 256) * vocab_rows * width, **kind,
        )

    logits_0, ids_0, states_0, table_0, w = logits_of(with_other(line), weights, ())
    logits_1, ids_1, states_1, table_1 = logits_of(with_other(up, down), w, (table_0,))
    logits_2, ids_2, states_2, stats = logits_of(with_other(far_up, far_down), w, (table_0, table_1, order))
    logits, every_id = (logits_0, logits_1, logits_2), (ids_0, ids_1, ids_2)
    states = (states_0, states_1, states_2)

    stats = lax.all_gather(stats, TOK)
    stats = call(merge_kernel, shaped(F32, lax.axis_size(VOC), 4, tokens), here, stats)
    stats = lax.all_to_all(stats, VOC, 0, 0, tiled=True)

    loss, log_total, mine, *grads = call(
        functools.partial(slab_kernel, own, part),
        (
            shaped(F32, own, 1),
            shaped(F32, tokens, 1),
            shaped(F32, slab_rows, part),
            *[shaped(BF16, slab_rows, part)] * 3,
        ),
        here, stats, *logits, *every_id, *states, order,
        flops=2 * tokens * slab_rows * width,
        scratch=[pltpu.VMEM((slab_rows, tokens), BF16)],
    )
    token_loss = call(loss_kernel, shaped(F32, 1, own), here, loss)

    def hidden_terms(other):
        return call(
            functools.partial(hidden_kernel, other), shaped(BF16, tokens // 2, width),
            here, *logits, *every_id, log_total, w,
            flops=tokens * vocab_rows * width,
            scratch=[pltpu.VMEM((tokens // 2, vocab_rows), BF16)],
        )

    send = hidden_terms(1)
    keep = hidden_terms(0)

    slab_grads = [mine, *arrivals(grads, along("rep"))]
    operands = (here, outer_weight, momentum, *slab_weights, *slab_grads)
    rounded = call(outer_kernel, shaped(BF16, slab_rows, part), *operands)
    new_outer, new_momentum = call(outer_kernel, [shaped(F32, slab_rows, part)] * 2, *operands)
    pieces = ring_gather(rounded, along("rep"))
    next_inner = call(
        functools.partial(place_kernel, part), shaped(BF16, slab_rows, width), here, *pieces,
        scratch=[pltpu.SemaphoreType.DMA((5,))], out_spec=pl.BlockSpec(memory_space=pltpu.HBM),
    )

    got = take(send, CORE, 1)
    total = (to_f32(keep) + to_f32(got)).reshape(4, 8 * own, width)
    rounded = total.astype(BF16)
    got = arrivals(rounded[1:], take_outer)
    line = (total[0] + sum(to_f32(one) for one in got)).reshape(4, 2 * own, width)
    rounded = line.astype(BF16)
    pair = line[0] + sum(to_f32(take_inner(rounded[k], -k)) for k in (1, 2, 3))
    pair_sent = take(pair[own:].astype(BF16), Z, 1)
    token_grad = (pair[:own] + to_f32(pair_sent))[None]
    return (token_loss, token_grad, new_outer, new_momentum, next_inner)


def solution(mesh):
    finer = Mesh(
        mesh.devices.reshape(mesh.shape["rep"], 2, 2, 4, 4),
        ("rep", "tok_0", "tok_1", "voc_0", "voc_1"),
    )
    in_specs = (
        P("rep", TOK_VOC, None),
        P("rep", TOK_VOC),
        P("rep", TOK_VOC, None),
        P(TOK_VOC, "rep"),
        P(TOK_VOC, "rep"),
    )
    out_specs = (
        P("rep", TOK_VOC),
        P("rep", TOK_VOC, None),
        P(TOK_VOC, "rep"),
        P(TOK_VOC, "rep"),
        P(TOK_VOC, None),
    )

    return jax.shard_map(per_device, mesh=finer, in_specs=in_specs, out_specs=out_specs, check_vma=False)
```

time: 180 us -> 173 us (0.961)
  waiting for transfers between devices: 75.5 us -> 57.8 us
  blocking collectives: 5.42 us -> 16.2 us
  Pallas kernels: 30.9 us -> 35.5 us
  other arithmetic: 6.69 us -> 4.84 us
    ppermute x25 -> x17, waiting for transfers between devices: 48 us -> 37.2 us  [take(): return lax.ppermute(value, axis, [((i + k) % n, i) for i in range(n)])]
    all_to_all x0 -> x1, blocking collectives: none -> 10.6 us  [per_device(): stats = lax.all_to_all(stats, VOC, 0, 0, tiled=True)]
    ppermute x0 -> x4, starting transfers between devices: none -> 8 us  [take_across(): return lax.ppermute(value, (Z, CORE, X, Y), both)]
    ppermute x8 -> x7, waiting for transfers between devices: 21.3 us -> 15.8 us  [take_outer(): return lax.ppermute(value, (CORE, X, Y), by_core(k, False))]
    ppermute x25 -> x17, starting transfers between devices: 33 us -> 27.6 us  [take(): return lax.ppermute(value, axis, [((i + k) % n, i) for i in range(n)])]
    ppermute x6, waiting for transfers between devices: 6.24 us -> 1.1 us  [take_inner(): return lax.ppermute(value, (CORE, X, Y), by_core(k, True))]
    pallas_call x9 -> x13, Pallas kernels: 30.9 us -> 35.5 us  [call(): pl.pallas_call(kernel, in_specs=[SMEM] + [specs.get(k, VMEM) for k in ran...]
    ppermute x0 -> x4, waiting for transfers between devices: none -> 3.79 us  [take_across(): return lax.ppermute(value, (Z, CORE, X, Y), both)]
  transfers between devices with their start and end apart: 39 -> 34, of which waited for: 22 -> 14; matrix products, arithmetic and copies ran while one was open for 5% -> 4% of each run, Pallas kernels for 7% -> 12%
where the time goes in v1:
time: 173 us; the launch traced here: 172 us
  waiting for transfers between devices  57.8 us (33%)
  starting transfers between devices  49.6 us (29%)
  Pallas kernels  35.5 us (21%)
  blocking collectives  16.2 us (9%)
  local copies, waits for them, and re-layouts  7.43 us (4%)
  other arithmetic  4.84 us (3%)
    ppermute x17, waiting for transfers between devices, take(): return lax.ppermute(value, axis, [((i + k) % n, i) for i in range(n)])  37.2 us
    pallas_call x13, Pallas kernels, call(): pl.pallas_call(kernel, in_specs=[SMEM] + [specs.get(k, VMEM) for k in ran...  35.5 us
    ppermute x17, starting transfers between devices, take(): return lax.ppermute(value, axis, [((i + k) % n, i) for i in range(n)])  27.6 us
    ppermute x7, waiting for transfers between devices, take_outer(): return lax.ppermute(value, (CORE, X, Y), by_core(k, False))  15.8 us
    all_to_all x1, blocking collectives, per_device(): stats = lax.all_to_all(stats, VOC, 0, 0, tiled=True)  10.6 us
    ppermute x7, starting transfers between devices, take_outer(): return lax.ppermute(value, (CORE, X, Y), by_core(k, False))  8.52 us
    ppermute x4, starting transfers between devices, take_across(): return lax.ppermute(value, (Z, CORE, X, Y), both)  8 us
    all_gather x1, blocking collectives, per_device(): stats = lax.all_gather(stats, TOK)  5.62 us
  transfers between devices with their start and end apart: 34, of which 14 were waited for; matrix products, arithmetic and copies ran while one was open for 4% of the time, Pallas kernels for 12%

profile of v1, /device:TPU:32, one launch (start us, length us, event | category | flops | bytes accessed | tf_op | source)
XLA Modules:
  0.0 172.3 jit_solution(16585707118101384360)
XLA Ops:
  0.6 0.7 convert_bitcast_fusion.1
  1.4 0.8 fusion.2.refs_0_
  2.2 1.8 %collective-permute-start = (bf16[8,4224]{1,0:T(8,128)(2,1)S(1)}, bf16[8,4224]{1,0:T(8,128)(2,1)S(1)}, u32[]{:S(2)}, u32[]{:S(2)}) collective-permute-start(bf16[8,4224]{1,0:T(8,128)(2,1)S(1)} %fusion.2.refs_0_), channel_id=1, source_target_pairs={{32,0},{33,1},{34,2},{35,3},{36,4},{37,5},{38,6},{39,7},{40,8},{41... | collective-permute-start | bytes 202760 | tf_op jit(solution)/shard_map/ppermute | solution.py:73
  4.1 1.1 collective-permute-start.1
  5.1 2.2 %collective-permute-start.2 = (bf16[8,4224]{1,0:T(8,128)(2,1)S(1)}, bf16[8,4224]{1,0:T(8,128)(2,1)S(1)}, u32[]{:S(2)}, u32[]{:S(2)}) collective-permute-start(bf16[8,4224]{1,0:T(8,128)(2,1)S(1)} %fusion.2.refs_0_), channel_id=1, source_target_pairs={{36,0},{37,1},{38,2},{39,3},{40,4},{41,5},{42,6},{43,7},{44,8},{45... | collective-permute-start | bytes 202760 | tf_op jit(solution)/shard_map/ppermute | solution.py:73
  7.3 0.5 collective-permute-start.3
  7.8 2.6 %collective-permute-start.4 = (bf16[8,4224]{1,0:T(8,128)(2,1)S(1)}, bf16[8,4224]{1,0:T(8,128)(2,1)S(1)}, u32[]{:S(2)}, u32[]{:S(2)}) collective-permute-start(bf16[8,4224]{1,0:T(8,128)(2,1)S(1)} %fusion.2.refs_0_), channel_id=1, source_target_pairs={{40,0},{41,1},{42,2},{43,3},{44,4},{45,5},{46,6},{47,7},{32,8},{33... | collective-permute-start | bytes 202760 | tf_op jit(solution)/shard_map/ppermute | solution.py:73
  10.4 1.2 collective-permute-start.5
  11.6 1.4 collective-permute-start.6
  13.1 1.7 collective-permute-done.4.refs_5_
  14.8 1.1 collective-permute-done.5.refs_6_
  15.9 2.1 %collective-permute-done.6.refs_7_ = bf16[8,4224]{1,0:T(8,128)(2,1)S(1)} collective-permute-done((bf16[8,4224]{1,0:T(8,128)(2,1)S(1)}, bf16[8,4224]{1,0:T(8,128)(2,1)S(1)}, u32[]{:S(2)}, u32[]{:S(2)}) %collective-permute-start.6) | collective-permute-done | bytes 67616 | tf_op jit(solution)/shard_map/ppermute | solution.py:73
  18.0 0.6 shard_map.92.refs_0_
  18.6 3.1 %collective-permute-start.7 = (bf16[64,4224]{1,0:T(8,128)(2,1)S(1)}, bf16[64,4224]{1,0:T(8,128)(2,1)S(1)}, u32[]{:S(2)}, u32[]{:S(2)}) collective-permute-start(bf16[64,4224]{1,0:T(8,128)(2,1)S(1)} %shard_map.92.refs_0_), channel_id=1, source_target_pairs={{1,0},{2,1},{3,2},{0,3},{5,4},{6,5},{7,6},{4,7},{9,8},{10,9},{11,1... | collective-permute-start | bytes 1622024 | tf_op jit(solution)/shard_map/ppermute | solution.py:62
  21.7 6.9 %collective-permute-done.7.refs_0_ = bf16[64,4224]{1,0:T(8,128)(2,1)S(1)} collective-permute-done((bf16[64,4224]{1,0:T(8,128)(2,1)S(1)}, bf16[64,4224]{1,0:T(8,128)(2,1)S(1)}, u32[]{:S(2)}, u32[]{:S(2)}) %collective-permute-start.7) | collective-permute-done | bytes 540704 | tf_op jit(solution)/shard_map/ppermute | solution.py:62
  28.5 3.7 %collective-permute-done.9.refs_1_ = bf16[64,4224]{1,0:T(8,128)(2,1)S(1)} collective-permute-done((bf16[64,4224]{1,0:T(8,128)(2,1)S(1)}, bf16[64,4224]{1,0:T(8,128)(2,1)S(1)}, u32[]{:S(2)}, u32[]{:S(2)}) %collective-permute-start.9) | collective-permute-done | bytes 540704 | tf_op jit(solution)/shard_map/ppermute | solution.py:62
  32.2 0.6 collective-permute-start.8
  32.9 1.6 collective-permute-start.10
  34.5 0.9 shard_map.95.refs_7_.refs_10_
  35.4 3.4 %collective-permute-done.8.refs_0_ = bf16[32,4224]{1,0:T(8,128)(2,1)S(1)} collective-permute-done((bf16[32,4224]{1,0:T(8,128)(2,1)S(1)}, bf16[32,4224]{1,0:T(8,128)(2,1)S(1)}, u32[]{:S(2)}, u32[]{:S(2)}) %collective-permute-start.8) | collective-permute-done | bytes 270368 | tf_op jit(solution)/shard_map/ppermute | solution.py:62
  38.8 1.8 %collective-permute-done.10.refs_1_ = bf16[32,4224]{1,0:T(8,128)(2,1)S(1)} collective-permute-done((bf16[32,4224]{1,0:T(8,128)(2,1)S(1)}, bf16[32,4224]{1,0:T(8,128)(2,1)S(1)}, u32[]{:S(2)}, u32[]{:S(2)}) %collective-permute-start.10) | collective-permute-done | bytes 270368 | tf_op jit(solution)/shard_map/ppermute | solution.py:62
  40.6 5.8 %shard_map.93 = (f32[128,1024]{1,0:T(8,128)S(1)}, s32[128,1]{1,0:T(8,128)S(1)}, bf16[128,4096]{1,0:T(8,128)(2,1)S(1)}, f32[128,128]{1,0:T(8,128)S(1)}, bf16[1024,4096]{1,0:T(8,128)(2,1)S(1)}) custom-call(s32[6]{0:T(128)S(1)} %stack.33.here, bf16[64,4224]{1,0:T(8,128)(2,1)S(1)} %shard_map.92.refs_0_, bf16[64,4224]{1,0:T(8,128)(2,1)S(1)} %collective-permute-done.13.refs_1_, ...), custom_call_target="tpu_custom_call" | custom-call | flops 2147483648 | bytes 19497496 | tf_op jit(solution)/shard_map/pallas_call | solution.py:33
  46.4 4.2 %shard_map.94 = (f32[256,1024]{1,0:T(8,128)S(1)}, s32[256,1]{1,0:T(8,128)S(1)}, bf16[256,4096]{1,0:T(8,128)(2,1)S(1)}, f32[256,128]{1,0:T(8,128)S(1)}) custom-call(s32[6]{0:T(128)S(1)} %stack.33.here, bf16[64,4224]{1,0:T(8,128)(2,1)S(1)} %collective-permute-done.7.refs_0_, bf16[64,4224]{1,0:T(8,128)(2,1)S(1)} %collective-permute-done.9.refs_1_, ...), custom_call_target="tpu_custom_call" | custom-call | flops 2147483648 | bytes 13894680 | tf_op jit(solution)/shard_map/pallas_call | solution.py:33
  50.7 4.6 %shard_map.96 = (f32[128,1024]{1,0:T(8,128)S(1)}, s32[128,1]{1,0:T(8,128)S(1)}, bf16[128,4096]{1,0:T(8,128)(2,1)S(1)}, f32[8,512]{1,0:T(8,128)S(1)}) custom-call(s32[6]{0:T(128)S(1)} %stack.33.here, bf16[32,4224]{1,0:T(8,128)(2,1)S(1)} %collective-permute-done.8.refs_0_, bf16[32,4224]{1,0:T(8,128)(2,1)S(1)} %collective-permute-done.10.refs_1_, ...), custom_call_target="tpu_custom_call" | custom-call | flops 2147483648 | bytes 11780632 | tf_op jit(solution)/shard_map/pallas_call | solution.py:33
  55.3 5.6 %all-gather = f32[32,512]{1,0:T(8,128)S(1)} all-gather(f32[8,512]{1,0:T(8,128)S(1)} %get-tuple-element.29), channel_id=2, replica_groups=mesh['rep'=4,'tok_0'=2,'tok_1'=2,'voc_0'=4,'voc_1'=4] {'tok_0','tok_1'}, dimensions={0}, use_global_device_ids=true | all-gather | bytes 81920 | tf_op jit(solution)/shard_map/all_gather | solution.py:394
  60.9 0.6 shard_map.97
  61.5 10.6 %all_to_all.5.refs_0_ = f32[16,4,512]{2,1,0:T(4,128)S(1)} all-to-all(f32[16,4,512]{2,1,0:T(4,128)S(1)} %shard_map.97), channel_id=1, replica_groups=mesh['rep'=4,'tok_0'=2,'tok_1'=2,'voc_0'=4,'voc_1'=4] {'voc_0','voc_1'}, dimensions={0} | all-to-all | bytes 262144 | tf_op jit(solution)/shard_map/all_to_all | solution.py:396
  72.1 3.0 %shard_map.98 = (f32[8,1]{1,0:T(8,128)S(1)}, f32[512,1]{1,0:T(8,128)S(1)}, f32[128,1024]{1,0:T(8,128)S(1)}, bf16[128,1024]{1,0:T(8,128)(2,1)S(1)}, bf16[128,1024...) custom-call(s32[6]{0:T(128)S(1)} %stack.33.here, f32[16,4,512]{2,1,0:T(4,128)S(1)} %all_to_all.5.refs_0_, ...), custom_call_target="tpu_custom_call" | custom-call | flops 536870912 | bytes 8261688 | tf_op jit(solution)/shard_map/pallas_call | solution.py:33
  75.1 5.8 %shard_map.101 = bf16[256,4096]{1,0:T(8,128)(2,1)} custom-call(s32[6]{0:T(128)S(1)} %stack.33.here, f32[128,1024]{1,0:T(8,128)S(1)} %get-tuple-element.30.refs_1_.refs_0_, f32[256,1024]{1,0:T(8,128)S(1)} %get-tuple-element.31.refs_2_.refs_1_, f32[128,1024]{1,0:T(8,128)S(1)} %get-tuple-element.32.refs_3_.refs_2_, ...), custom_call_target="tpu_custom_call" | custom-call | flops 2147483648 | bytes 12587032 | tf_op jit(solution)/shard_map/pallas_call | solution.py:33
  80.9 2.3 %slice.71 = bf16[1,128,4096]{2,1,0:T(8,128)(2,1)} slice(bf16[1,1024,4096]{2,1,0:T(8,128)(2,1)} %param.7), slice={[0:1], [0:128], [0:4096]} | slice | bytes 2097152 | tf_op jit(solution)/shard_map/slice | solution.py:361
  83.2 1.3 dynamic-slice_bitcast_fusion
  84.5 6.0 %collective-permute-start.24 = (bf16[128,1024]{1,0:T(8,128)(2,1)S(1)}, bf16[128,1024]{1,0:T(8,128)(2,1)S(1)}, u32[]{:S(2)}, u32[]{:S(2)}) collective-permute-start(bf16[128,1024]{1,0:T(8,128)(2,1)S(1)} %get-tuple-element.56), channel_id=1, source_target_pairs={{64,0},{128,64},{192,128},{0,192},{65,1},{129,65},{193,129},{1,193... | collective-permute-start | bytes 786440 | tf_op jit(solution)/shard_map/ppermute | solution.py:78
  90.5 1.0 collective-permute-start.25
  91.5 2.8 %collective-permute-start.26 = (bf16[128,1024]{1,0:T(8,128)(2,1)S(1)}, bf16[128,1024]{1,0:T(8,128)(2,1)S(1)}, u32[]{:S(2)}, u32[]{:S(2)}) collective-permute-start(bf16[128,1024]{1,0:T(8,128)(2,1)S(1)} %get-tuple-element.54), channel_id=1, source_target_pairs={{192,0},{0,64},{64,128},{128,192},{193,1},{1,65},{65,129},{129,193... | collective-permute-start | bytes 786440 | tf_op jit(solution)/shard_map/ppermute | solution.py:78
  94.3 2.1 %collective-permute-start.27 = (bf16[128,1024]{1,0:T(8,128)(2,1)S(1)}, bf16[128,1024]{1,0:T(8,128)(2,1)S(1)}, u32[]{:S(2)}, u32[]{:S(2)}) collective-permute-start(bf16[128,1024]{1,0:T(8,128)(2,1)S(1)} %copy-done.7), channel_id=1, source_target_pairs={{128,0},{192,64},{0,128},{64,192},{129,1},{193,65},{1,129},{65,193... | collective-permute-start | bytes 786440 | tf_op jit(solution)/shard_map/ppermute | solution.py:78
  96.4 3.4 %copy-done.1 = bf16[1024,4096]{1,0:T(8,128)(2,1)S(1)} copy-done((bf16[1024,4096]{1,0:T(8,128)(2,1)S(1)}, bf16[1024,4096]{1,0:T(8,128)(2,1)}, u32[]{:S(2)}) %copy-start.1) | copy-done | bytes 8388632
  99.8 4.5 %shard_map.100 = bf16[256,4096]{1,0:T(8,128)(2,1)S(1)} custom-call(s32[6]{0:T(128)S(1)} %stack.33.here, f32[128,1024]{1,0:T(8,128)S(1)} %get-tuple-element.30.refs_1_.refs_0_, f32[256,1024]{1,0:T(8,128)S(1)} %get-tuple-element.31.refs_2_.refs_1_, f32[128,1024]{1,0:T(8,128)S(1)} %get-tuple-element.32.refs_3_.refs_2_, ...), custom_call_target="tpu_custom_call" | custom-call | flops 2147483648 | bytes 12587032 | tf_op jit(solution)/shard_map/pallas_call | solution.py:33
  104.3 2.4 %convert_add_fusion = (f32[256,4096]{1,0:T(8,128)S(1)}, bf16[256,4096]{1,0:T(8,128)(2,1)S(1)}) fusion(bf16[256,4096]{1,0:T(8,128)(2,1)} %collective-permute-done.16, bf16[256,4096]{1,0:T(8,128)(2,1)S(1)} %shard_map.100), kind=kLoop, calls=%fused_computation | loop fusion | flops 4194304 | bytes 10485760 | tf_op jit(solution)/shard_map/add | solution.py:434
  106.7 0.1 fusion.5
  106.9 1.2 collective-permute-start.19
  108.1 5.8 %collective-permute-done.24.w1 = bf16[128,1024]{1,0:T(8,128)(2,1)S(1)} collective-permute-done((bf16[128,1024]{1,0:T(8,128)(2,1)S(1)}, bf16[128,1024]{1,0:T(8,128)(2,1)S(1)}, u32[]{:S(2)}, u32[]{:S(2)}) %collective-permute-start.24) | collective-permute-done | bytes 262176 | tf_op jit(solution)/shard_map/ppermute | solution.py:78
  113.9 0.6 collective-permute-start.18
  114.5 6.6 %collective-permute-done.25.w2 = bf16[128,1024]{1,0:T(8,128)(2,1)S(1)} collective-permute-done((bf16[128,1024]{1,0:T(8,128)(2,1)S(1)}, bf16[128,1024]{1,0:T(8,128)(2,1)S(1)}, u32[]{:S(2)}, u32[]{:S(2)}) %collective-permute-start.25) | collective-permute-done | bytes 262176 | tf_op jit(solution)/shard_map/ppermute | solution.py:78
  121.1 1.4 collective-permute-start.17
  122.5 7.2 %collective-permute-done.26.w3 = bf16[128,1024]{1,0:T(8,128)(2,1)S(1)} collective-permute-done((bf16[128,1024]{1,0:T(8,128)(2,1)S(1)}, bf16[128,1024]{1,0:T(8,128)(2,1)S(1)}, u32[]{:S(2)}, u32[]{:S(2)}) %collective-permute-start.26) | collective-permute-done | bytes 262176 | tf_op jit(solution)/shard_map/ppermute | solution.py:78
  129.8 2.5 %collective-permute-start.28 = (bf16[128,1024]{1,0:T(8,128)(2,1)S(1)}, bf16[128,1024]{1,0:T(8,128)(2,1)S(1)}, u32[]{:S(2)}, u32[]{:S(2)}) collective-permute-start(bf16[128,1024]{1,0:T(8,128)(2,1)S(1)} %copy-done.5), channel_id=1, source_target_pairs={{192,0},{0,64},{64,128},{128,192},{193,1},{1,65},{65,129},{129,193... | collective-permute-start | bytes 786440 | tf_op jit(solution)/shard_map/ppermute | solution.py:78
  132.2 2.7 %collective-permute-start.29 = (bf16[128,1024]{1,0:T(8,128)(2,1)S(1)}, bf16[128,1024]{1,0:T(8,128)(2,1)S(1)}, u32[]{:S(2)}, u32[]{:S(2)}) collective-permute-start(bf16[128,1024]{1,0:T(8,128)(2,1)S(1)} %get-tuple-element.44), channel_id=1, source_target_pairs={{64,0},{128,64},{192,128},{0,192},{65,1},{129,65},{193,129},{1,193... | collective-permute-start | bytes 786440 | tf_op jit(solution)/shard_map/ppermute | solution.py:78
  135.0 6.0 %collective-permute-done.28.g2 = bf16[128,1024]{1,0:T(8,128)(2,1)S(1)} collective-permute-done((bf16[128,1024]{1,0:T(8,128)(2,1)S(1)}, bf16[128,1024]{1,0:T(8,128)(2,1)S(1)}, u32[]{:S(2)}, u32[]{:S(2)}) %collective-permute-start.28) | collective-permute-done | bytes 262176 | tf_op jit(solution)/shard_map/ppermute | solution.py:78
  141.0 5.1 %collective-permute-done.29.g3 = bf16[128,1024]{1,0:T(8,128)(2,1)S(1)} collective-permute-done((bf16[128,1024]{1,0:T(8,128)(2,1)S(1)}, bf16[128,1024]{1,0:T(8,128)(2,1)S(1)}, u32[]{:S(2)}, u32[]{:S(2)}) %collective-permute-start.29) | collective-permute-done | bytes 262176 | tf_op jit(solution)/shard_map/ppermute | solution.py:78
  146.1 0.9 shard_map.103.mine
  147.0 2.7 %collective-permute-start.30 = (bf16[128,1024]{1,0:T(8,128)(2,1)S(1)}, bf16[128,1024]{1,0:T(8,128)(2,1)S(1)}, u32[]{:S(2)}, u32[]{:S(2)}) collective-permute-start(bf16[128,1024]{1,0:T(8,128)(2,1)S(1)} %shard_map.103.mine), channel_id=1, source_target_pairs={{64,0},{128,64},{192,128},{0,192},{65,1},{129,65},{193,129},{1,193... | collective-permute-start | bytes 786440 | tf_op jit(solution)/shard_map/ppermute | solution.py:78
  149.7 4.6 %collective-permute-start.32 = (bf16[128,1024]{1,0:T(8,128)(2,1)S(1)}, bf16[128,1024]{1,0:T(8,128)(2,1)S(1)}, u32[]{:S(2)}, u32[]{:S(2)}) collective-permute-start(bf16[128,1024]{1,0:T(8,128)(2,1)S(1)} %shard_map.103.mine), channel_id=1, source_target_pairs={{192,0},{0,64},{64,128},{128,192},{193,1},{1,65},{65,129},{129,193... | collective-permute-start | bytes 786440 | tf_op jit(solution)/shard_map/ppermute | solution.py:78
  154.3 0.2 fusion.4
  154.6 1.1 collective-permute-start.22
  155.7 0.4 collective-permute-start.21
  156.0 1.3 collective-permute-start.20
  157.4 3.9 %collective-permute-done.30.up = bf16[128,1024]{1,0:T(8,128)(2,1)S(1)} collective-permute-done((bf16[128,1024]{1,0:T(8,128)(2,1)S(1)}, bf16[128,1024]{1,0:T(8,128)(2,1)S(1)}, u32[]{:S(2)}, u32[]{:S(2)}) %collective-permute-start.30) | collective-permute-done | bytes 262176 | tf_op jit(solution)/shard_map/ppermute | solution.py:78
  161.3 1.5 collective-permute-start.31
  162.8 1.6 collective-permute-start.33
  164.6 1.1 shard_map.99
  165.7 1.9 %shard_map.102 = (f32[128,1024]{1,0:T(8,128)}, f32[128,1024]{1,0:T(8,128)}) custom-call(s32[6]{0:T(128)S(1)} %stack.33.here, f32[128,1024]{1,0:T(8,128)S(1)} %copy-done.2, f32[128,1024]{1,0:T(8,128)S(1)} %copy-done.3, bf16[128,1024]{1,0:T(8,128)(2,1)S(1)} %get-tuple-element.57.w0, bf16[128,1024]{1,0:T(8,128)(2,1)S(1)} %collective-permute-done.24.w1, ...), custom_call_target="tpu_custom_call" | custom-call | flops 4456472 | bytes 4456472 | tf_op jit(solution)/shard_map/pallas_call | solution.py:33
  167.6 2.5 %collective-permute-done.33.high = bf16[64,1024]{1,0:T(8,128)(2,1)S(1)} collective-permute-done((bf16[64,1024]{1,0:T(8,128)(2,1)S(1)}, bf16[64,1024]{1,0:T(8,128)(2,1)S(1)}, u32[]{:S(2)}, u32[]{:S(2)}) %collective-permute-start.33) | collective-permute-done | bytes 131104 | tf_op jit(solution)/shard_map/ppermute | solution.py:78
  170.1 1.6 shard_map.104
  171.6 0.7 fusion.1
  (53 shorter events, 0.6 us)
Async XLA Ops:
  2.2 8.1 %collective-permute-start = (bf16[8,4224]{1,0:T(8,128)(2,1)S(1)}, bf16[8,4224]{1,0:T(8,128)(2,1)S(1)}, u32[]{:S(2)}, u32[]{:S(2)}) collective-permute-start(bf16[8,4224]{1,0:T(8,128)(2,1)S(1)} %fusion.2.refs_0_), channel_id=1, source_target_pairs={{32,0},{33,1},{34,2},{35,3},{36,4},{37,5},{38,6},{39,7},{40,8},{41... | collective-permute-start | bytes 202760 | tf_op jit(solution)/shard_map/ppermute | solution.py:73
  4.1 7.5 %collective-permute-start.1 = (bf16[8,4224]{1,0:T(8,128)(2,1)S(1)}, bf16[8,4224]{1,0:T(8,128)(2,1)S(1)}, u32[]{:S(2)}, u32[]{:S(2)}) collective-permute-start(bf16[8,4224]{1,0:T(8,128)(2,1)S(1)} %fusion.2.refs_0_), channel_id=1, source_target_pairs={{4,0},{5,1},{6,2},{7,3},{8,4},{9,5},{10,6},{11,7},{12,8},{13,9},{1... | collective-permute-start | bytes 202760 | tf_op jit(solution)/shard_map/ppermute | solution.py:66
  5.1 8.0 %collective-permute-start.2 = (bf16[8,4224]{1,0:T(8,128)(2,1)S(1)}, bf16[8,4224]{1,0:T(8,128)(2,1)S(1)}, u32[]{:S(2)}, u32[]{:S(2)}) collective-permute-start(bf16[8,4224]{1,0:T(8,128)(2,1)S(1)} %fusion.2.refs_0_), channel_id=1, source_target_pairs={{36,0},{37,1},{38,2},{39,3},{40,4},{41,5},{42,6},{43,7},{44,8},{45... | collective-permute-start | bytes 202760 | tf_op jit(solution)/shard_map/ppermute | solution.py:73
  7.3 5.8 %collective-permute-start.3 = (bf16[8,4224]{1,0:T(8,128)(2,1)S(1)}, bf16[8,4224]{1,0:T(8,128)(2,1)S(1)}, u32[]{:S(2)}, u32[]{:S(2)}) collective-permute-start(bf16[8,4224]{1,0:T(8,128)(2,1)S(1)} %fusion.2.refs_0_), channel_id=1, source_target_pairs={{8,0},{9,1},{10,2},{11,3},{12,4},{13,5},{14,6},{15,7},{0,8},{1,9},... | collective-permute-start | bytes 202760 | tf_op jit(solution)/shard_map/ppermute | solution.py:66
  7.8 7.0 %collective-permute-start.4 = (bf16[8,4224]{1,0:T(8,128)(2,1)S(1)}, bf16[8,4224]{1,0:T(8,128)(2,1)S(1)}, u32[]{:S(2)}, u32[]{:S(2)}) collective-permute-start(bf16[8,4224]{1,0:T(8,128)(2,1)S(1)} %fusion.2.refs_0_), channel_id=1, source_target_pairs={{40,0},{41,1},{42,2},{43,3},{44,4},{45,5},{46,6},{47,7},{32,8},{33... | collective-permute-start | bytes 202760 | tf_op jit(solution)/shard_map/ppermute | solution.py:73
  10.4 5.5 %collective-permute-start.5 = (bf16[8,4224]{1,0:T(8,128)(2,1)S(1)}, bf16[8,4224]{1,0:T(8,128)(2,1)S(1)}, u32[]{:S(2)}, u32[]{:S(2)}) collective-permute-start(bf16[8,4224]{1,0:T(8,128)(2,1)S(1)} %fusion.2.refs_0_), channel_id=1, source_target_pairs={{12,0},{13,1},{14,2},{15,3},{0,4},{1,5},{2,6},{3,7},{4,8},{5,9},{6... | collective-permute-start | bytes 202760 | tf_op jit(solution)/shard_map/ppermute | solution.py:66
  11.6 6.4 %collective-permute-start.6 = (bf16[8,4224]{1,0:T(8,128)(2,1)S(1)}, bf16[8,4224]{1,0:T(8,128)(2,1)S(1)}, u32[]{:S(2)}, u32[]{:S(2)}) collective-permute-start(bf16[8,4224]{1,0:T(8,128)(2,1)S(1)} %fusion.2.refs_0_), channel_id=1, source_target_pairs={{44,0},{45,1},{46,2},{47,3},{32,4},{33,5},{34,6},{35,7},{36,8},{37... | collective-permute-start | bytes 202760 | tf_op jit(solution)/shard_map/ppermute | solution.py:73
  18.6 10.0 %collective-permute-start.7 = (bf16[64,4224]{1,0:T(8,128)(2,1)S(1)}, bf16[64,4224]{1,0:T(8,128)(2,1)S(1)}, u32[]{:S(2)}, u32[]{:S(2)}) collective-permute-start(bf16[64,4224]{1,0:T(8,128)(2,1)S(1)} %shard_map.92.refs_0_), channel_id=1, source_target_pairs={{1,0},{2,1},{3,2},{0,3},{5,4},{6,5},{7,6},{4,7},{9,8},{10,9},{11,1... | collective-permute-start | bytes 1622024 | tf_op jit(solution)/shard_map/ppermute | solution.py:62
  21.7 10.6 %collective-permute-start.9 = (bf16[64,4224]{1,0:T(8,128)(2,1)S(1)}, bf16[64,4224]{1,0:T(8,128)(2,1)S(1)}, u32[]{:S(2)}, u32[]{:S(2)}) collective-permute-start(bf16[64,4224]{1,0:T(8,128)(2,1)S(1)} %shard_map.92.refs_0_), channel_id=1, source_target_pairs={{3,0},{0,1},{1,2},{2,3},{7,4},{4,5},{5,6},{6,7},{11,8},{8,9},{9,10... | collective-permute-start | bytes 1622024 | tf_op jit(solution)/shard_map/ppermute | solution.py:62
  21.7 19.0 %collective-permute-start.13 = (bf16[64,4224]{1,0:T(8,128)(2,1)S(1)}, bf16[64,4224]{1,0:T(8,128)(2,1)S(1)}, u32[]{:S(2)}, u32[]{:S(2)}) collective-permute-start(bf16[64,4224]{1,0:T(8,128)(2,1)S(1)} %shard_map.92.refs_0_), channel_id=1, source_target_pairs={{16,0},{0,16},{17,1},{1,17},{18,2},{2,18},{19,3},{3,19},{20,4},{4,... | collective-permute-start | bytes 1622024 | tf_op jit(solution)/shard_map/ppermute | solution.py:78
  28.5 17.9 %collective-permute-start.14 = (bf16[64,4224]{1,0:T(8,128)(2,1)S(1)}, bf16[64,4224]{1,0:T(8,128)(2,1)S(1)}, u32[]{:S(2)}, u32[]{:S(2)}) collective-permute-start(bf16[64,4224]{1,0:T(8,128)(2,1)S(1)} %collective-permute-done.7.refs_0_), channel_id=1, source_target_pairs={{16,0},{0,16},{17,1},{1,17},{18,2},{2,18},{19,3},{3,19},{20,4},{4,... | collective-permute-start | bytes 1622024 | tf_op jit(solution)/shard_map/ppermute | solution.py:78
  32.2 14.2 %collective-permute-start.15 = (bf16[64,4224]{1,0:T(8,128)(2,1)S(1)}, bf16[64,4224]{1,0:T(8,128)(2,1)S(1)}, u32[]{:S(2)}, u32[]{:S(2)}) collective-permute-start(bf16[64,4224]{1,0:T(8,128)(2,1)S(1)} %collective-permute-done.9.refs_1_), channel_id=1, source_target_pairs={{16,0},{0,16},{17,1},{1,17},{18,2},{2,18},{19,3},{3,19},{20,4},{4,... | collective-permute-start | bytes 1622024 | tf_op jit(solution)/shard_map/ppermute | solution.py:78
  32.2 6.5 %collective-permute-start.8 = (bf16[32,4224]{1,0:T(8,128)(2,1)S(1)}, bf16[32,4224]{1,0:T(8,128)(2,1)S(1)}, u32[]{:S(2)}, u32[]{:S(2)}) collective-permute-start(bf16[32,4224]{1,0:T(8,128)(2,1)S(1)} %slice.74), channel_id=1, source_target_pairs={{1,0},{2,1},{3,2},{0,3},{5,4},{6,5},{7,6},{4,7},{9,8},{10,9},{11,1... | collective-permute-start | bytes 811016 | tf_op jit(solution)/shard_map/ppermute | solution.py:62
  32.9 7.7 %collective-permute-start.10 = (bf16[32,4224]{1,0:T(8,128)(2,1)S(1)}, bf16[32,4224]{1,0:T(8,128)(2,1)S(1)}, u32[]{:S(2)}, u32[]{:S(2)}) collective-permute-start(bf16[32,4224]{1,0:T(8,128)(2,1)S(1)} %slice.75), channel_id=1, source_target_pairs={{3,0},{0,1},{1,2},{2,3},{7,4},{4,5},{5,6},{6,7},{11,8},{8,9},{9,10... | collective-permute-start | bytes 811016 | tf_op jit(solution)/shard_map/ppermute | solution.py:62
  38.8 11.9 %collective-permute-start.11 = (bf16[32,4224]{1,0:T(8,128)(2,1)S(1)}, bf16[32,4224]{1,0:T(8,128)(2,1)S(1)}, u32[]{:S(2)}, u32[]{:S(2)}) collective-permute-start(bf16[32,4224]{1,0:T(8,128)(2,1)S(1)} %collective-permute-done.8.refs_0_), channel_id=1, source_target_pairs={{16,0},{0,16},{17,1},{1,17},{18,2},{2,18},{19,3},{3,19},{20,4},{4,... | collective-permute-start | bytes 811016 | tf_op jit(solution)/shard_map/ppermute | solution.py:78
  40.6 10.0 %collective-permute-start.12 = (bf16[32,4224]{1,0:T(8,128)(2,1)S(1)}, bf16[32,4224]{1,0:T(8,128)(2,1)S(1)}, u32[]{:S(2)}, u32[]{:S(2)}) collective-permute-start(bf16[32,4224]{1,0:T(8,128)(2,1)S(1)} %collective-permute-done.10.refs_1_), channel_id=1, source_target_pairs={{16,0},{0,16},{17,1},{1,17},{18,2},{2,18},{19,3},{3,19},{20,4},{4,... | collective-permute-start | bytes 811016 | tf_op jit(solution)/shard_map/ppermute | solution.py:78
  46.4 28.7 %copy-start = (bf16[1024,4096]{1,0:T(8,128)(2,1)}, bf16[1024,4096]{1,0:T(8,128)(2,1)S(1)}, u32[]{:S(2)}) copy-start(bf16[1024,4096]{1,0:T(8,128)(2,1)S(1)} %get-tuple-element.26.refs_4_.refs_7_) | copy-start | bytes 25165828
  75.1 5.8 %copy-start.4 = (bf16[128,1024]{1,0:T(8,128)(2,1)}, bf16[128,1024]{1,0:T(8,128)(2,1)S(1)}, u32[]{:S(2)}) copy-start(bf16[128,1024]{1,0:T(8,128)(2,1)S(1)} %get-tuple-element.43) | copy-start | bytes 786436
  75.1 5.8 %copy-start.6 = (bf16[128,1024]{1,0:T(8,128)(2,1)}, bf16[128,1024]{1,0:T(8,128)(2,1)S(1)}, u32[]{:S(2)}) copy-start(bf16[128,1024]{1,0:T(8,128)(2,1)S(1)} %get-tuple-element.42) | copy-start | bytes 786436
  80.9 23.4 %collective-permute-start.16 = (bf16[256,4096]{1,0:T(8,128)(2,1)}, bf16[256,4096]{1,0:T(8,128)(2,1)}, u32[]{:S(2)}, u32[]{:S(2)}) collective-permute-start(bf16[256,4096]{1,0:T(8,128)(2,1)} %shard_map.101), channel_id=1, source_target_pairs={{16,0},{0,16},{17,1},{1,17},{18,2},{2,18},{19,3},{3,19},{20,4},{4,... | collective-permute-start | bytes 6291464 | tf_op jit(solution)/shard_map/ppermute | solution.py:78
  83.2 11.1 %copy-start.7 = (bf16[128,1024]{1,0:T(8,128)(2,1)S(1)}, bf16[128,1024]{1,0:T(8,128)(2,1)}, u32[]{:S(2)}) copy-start(bf16[128,1024]{1,0:T(8,128)(2,1)} %copy-done.6) | copy-start | bytes 786436
  84.5 29.5 %collective-permute-start.24 = (bf16[128,1024]{1,0:T(8,128)(2,1)S(1)}, bf16[128,1024]{1,0:T(8,128)(2,1)S(1)}, u32[]{:S(2)}, u32[]{:S(2)}) collective-permute-start(bf16[128,1024]{1,0:T(8,128)(2,1)S(1)} %get-tuple-element.56), channel_id=1, source_target_pairs={{64,0},{128,64},{192,128},{0,192},{65,1},{129,65},{193,129},{1,193... | collective-permute-start | bytes 786440 | tf_op jit(solution)/shard_map/ppermute | solution.py:78
  90.5 30.6 %collective-permute-start.25 = (bf16[128,1024]{1,0:T(8,128)(2,1)S(1)}, bf16[128,1024]{1,0:T(8,128)(2,1)S(1)}, u32[]{:S(2)}, u32[]{:S(2)}) collective-permute-start(bf16[128,1024]{1,0:T(8,128)(2,1)S(1)} %get-tuple-element.55), channel_id=1, source_target_pairs={{128,0},{192,64},{0,128},{64,192},{129,1},{193,65},{1,129},{65,193... | collective-permute-start | bytes 786440 | tf_op jit(solution)/shard_map/ppermute | solution.py:78
  91.5 38.3 %collective-permute-start.26 = (bf16[128,1024]{1,0:T(8,128)(2,1)S(1)}, bf16[128,1024]{1,0:T(8,128)(2,1)S(1)}, u32[]{:S(2)}, u32[]{:S(2)}) collective-permute-start(bf16[128,1024]{1,0:T(8,128)(2,1)S(1)} %get-tuple-element.54), channel_id=1, source_target_pairs={{192,0},{0,64},{64,128},{128,192},{193,1},{1,65},{65,129},{129,193... | collective-permute-start | bytes 786440 | tf_op jit(solution)/shard_map/ppermute | solution.py:78
  94.3 37.9 %collective-permute-start.27 = (bf16[128,1024]{1,0:T(8,128)(2,1)S(1)}, bf16[128,1024]{1,0:T(8,128)(2,1)S(1)}, u32[]{:S(2)}, u32[]{:S(2)}) collective-permute-start(bf16[128,1024]{1,0:T(8,128)(2,1)S(1)} %copy-done.7), channel_id=1, source_target_pairs={{128,0},{192,64},{0,128},{64,192},{129,1},{193,65},{1,129},{65,193... | collective-permute-start | bytes 786440 | tf_op jit(solution)/shard_map/ppermute | solution.py:78
  96.4 3.4 %copy-start.1 = (bf16[1024,4096]{1,0:T(8,128)(2,1)S(1)}, bf16[1024,4096]{1,0:T(8,128)(2,1)}, u32[]{:S(2)}) copy-start(bf16[1024,4096]{1,0:T(8,128)(2,1)} %copy-done) | copy-start | bytes 25165828
  106.7 23.1 %copy-start.5 = (bf16[128,1024]{1,0:T(8,128)(2,1)S(1)}, bf16[128,1024]{1,0:T(8,128)(2,1)}, u32[]{:S(2)}) copy-start(bf16[128,1024]{1,0:T(8,128)(2,1)} %copy-done.4) | copy-start | bytes 786436
  106.7 39.4 %copy-start.2 = (f32[128,1024]{1,0:T(8,128)S(1)}, f32[128,1024]{1,0:T(8,128)}, u32[]{:S(2)}) copy-start(f32[128,1024]{1,0:T(8,128)} %outer.3) | copy-start | bytes 1572868
  106.7 39.4 %copy-start.3 = (f32[128,1024]{1,0:T(8,128)S(1)}, f32[128,1024]{1,0:T(8,128)}, u32[]{:S(2)}) copy-start(f32[128,1024]{1,0:T(8,128)} %momentum.3) | copy-start | bytes 1572868
  106.9 47.5 %collective-permute-start.19 = (bf16[64,4096]{1,0:T(8,128)(2,1)S(1)}, bf16[64,4096]{1,0:T(8,128)(2,1)S(1)}, u32[]{:S(2)}, u32[]{:S(2)}) collective-permute-start(bf16[64,4096]{1,0:T(8,128)(2,1)S(1)} %get-tuple-element.52), channel_id=1, source_target_pairs={{1,0},{2,1},{3,2},{0,3},{5,4},{6,5},{7,6},{4,7},{9,8},{10,9},{11,1... | collective-permute-start | bytes 1572872 | tf_op jit(solution)/shard_map/ppermute | solution.py:62
  113.9 40.4 %collective-permute-start.18 = (bf16[64,4096]{1,0:T(8,128)(2,1)S(1)}, bf16[64,4096]{1,0:T(8,128)(2,1)S(1)}, u32[]{:S(2)}, u32[]{:S(2)}) collective-permute-start(bf16[64,4096]{1,0:T(8,128)(2,1)S(1)} %get-tuple-element.53), channel_id=1, source_target_pairs={{3,0},{0,1},{1,2},{2,3},{7,4},{4,5},{5,6},{6,7},{11,8},{8,9},{9,10... | collective-permute-start | bytes 1572872 | tf_op jit(solution)/shard_map/ppermute | solution.py:62
  121.1 33.2 %collective-permute-start.17 = (bf16[64,4096]{1,0:T(8,128)(2,1)S(1)}, bf16[64,4096]{1,0:T(8,128)(2,1)S(1)}, u32[]{:S(2)}, u32[]{:S(2)}) collective-permute-start(bf16[64,4096]{1,0:T(8,128)(2,1)S(1)} %get-tuple-element.51), channel_id=1, source_target_pairs={{2,0},{3,1},{0,2},{1,3},{6,4},{7,5},{4,6},{5,7},{10,8},{11,9},{8,1... | collective-permute-start | bytes 1572872 | tf_op jit(solution)/shard_map/ppermute | solution.py:62
  129.8 11.2 %collective-permute-start.28 = (bf16[128,1024]{1,0:T(8,128)(2,1)S(1)}, bf16[128,1024]{1,0:T(8,128)(2,1)S(1)}, u32[]{:S(2)}, u32[]{:S(2)}) collective-permute-start(bf16[128,1024]{1,0:T(8,128)(2,1)S(1)} %copy-done.5), channel_id=1, source_target_pairs={{192,0},{0,64},{64,128},{128,192},{193,1},{1,65},{65,129},{129,193... | collective-permute-start | bytes 786440 | tf_op jit(solution)/shard_map/ppermute | solution.py:78
  132.2 13.9 %collective-permute-start.29 = (bf16[128,1024]{1,0:T(8,128)(2,1)S(1)}, bf16[128,1024]{1,0:T(8,128)(2,1)S(1)}, u32[]{:S(2)}, u32[]{:S(2)}) collective-permute-start(bf16[128,1024]{1,0:T(8,128)(2,1)S(1)} %get-tuple-element.44), channel_id=1, source_target_pairs={{64,0},{128,64},{192,128},{0,192},{65,1},{129,65},{193,129},{1,193... | collective-permute-start | bytes 786440 | tf_op jit(solution)/shard_map/ppermute | solution.py:78
  147.0 14.3 %collective-permute-start.30 = (bf16[128,1024]{1,0:T(8,128)(2,1)S(1)}, bf16[128,1024]{1,0:T(8,128)(2,1)S(1)}, u32[]{:S(2)}, u32[]{:S(2)}) collective-permute-start(bf16[128,1024]{1,0:T(8,128)(2,1)S(1)} %shard_map.103.mine), channel_id=1, source_target_pairs={{64,0},{128,64},{192,128},{0,192},{65,1},{129,65},{193,129},{1,193... | collective-permute-start | bytes 786440 | tf_op jit(solution)/shard_map/ppermute | solution.py:78
  149.7 13.1 %collective-permute-start.32 = (bf16[128,1024]{1,0:T(8,128)(2,1)S(1)}, bf16[128,1024]{1,0:T(8,128)(2,1)S(1)}, u32[]{:S(2)}, u32[]{:S(2)}) collective-permute-start(bf16[128,1024]{1,0:T(8,128)(2,1)S(1)} %shard_map.103.mine), channel_id=1, source_target_pairs={{192,0},{0,64},{64,128},{128,192},{193,1},{1,65},{65,129},{129,193... | collective-permute-start | bytes 786440 | tf_op jit(solution)/shard_map/ppermute | solution.py:78
  154.6 9.8 %collective-permute-start.22 = (bf16[16,4096]{1,0:T(8,128)(2,1)S(1)}, bf16[16,4096]{1,0:T(8,128)(2,1)S(1)}, u32[]{:S(2)}, u32[]{:S(2)}) collective-permute-start(bf16[16,4096]{1,0:T(8,128)(2,1)S(1)} %get-tuple-element.59), channel_id=1, source_target_pairs={{4,0},{5,1},{6,2},{7,3},{8,4},{9,5},{10,6},{11,7},{12,8},{13,9},{1... | collective-permute-start | bytes 393224 | tf_op jit(solution)/shard_map/ppermute | solution.py:66
  155.7 8.7 %collective-permute-start.21 = (bf16[16,4096]{1,0:T(8,128)(2,1)S(1)}, bf16[16,4096]{1,0:T(8,128)(2,1)S(1)}, u32[]{:S(2)}, u32[]{:S(2)}) collective-permute-start(bf16[16,4096]{1,0:T(8,128)(2,1)S(1)} %get-tuple-element.60), channel_id=1, source_target_pairs={{8,0},{9,1},{10,2},{11,3},{12,4},{13,5},{14,6},{15,7},{0,8},{1,9},... | collective-permute-start | bytes 393224 | tf_op jit(solution)/shard_map/ppermute | solution.py:66
  156.0 8.4 %collective-permute-start.20 = (bf16[16,4096]{1,0:T(8,128)(2,1)S(1)}, bf16[16,4096]{1,0:T(8,128)(2,1)S(1)}, u32[]{:S(2)}, u32[]{:S(2)}) collective-permute-start(bf16[16,4096]{1,0:T(8,128)(2,1)S(1)} %get-tuple-element.58), channel_id=1, source_target_pairs={{12,0},{13,1},{14,2},{15,3},{0,4},{1,5},{2,6},{3,7},{4,8},{5,9},{6... | collective-permute-start | bytes 393224 | tf_op jit(solution)/shard_map/ppermute | solution.py:66
  161.3 6.3 %collective-permute-start.31 = (bf16[64,1024]{1,0:T(8,128)(2,1)S(1)}, bf16[64,1024]{1,0:T(8,128)(2,1)S(1)}, u32[]{:S(2)}, u32[]{:S(2)}) collective-permute-start(bf16[64,1024]{1,0:T(8,128)(2,1)S(1)} %slice.86), channel_id=1, source_target_pairs={{64,0},{128,64},{192,128},{0,192},{65,1},{129,65},{193,129},{1,193... | collective-permute-start | bytes 393224 | tf_op jit(solution)/shard_map/ppermute | solution.py:78
  162.8 7.3 %collective-permute-start.33 = (bf16[64,1024]{1,0:T(8,128)(2,1)S(1)}, bf16[64,1024]{1,0:T(8,128)(2,1)S(1)}, u32[]{:S(2)}, u32[]{:S(2)}) collective-permute-start(bf16[64,1024]{1,0:T(8,128)(2,1)S(1)} %slice.87), channel_id=1, source_target_pairs={{192,0},{0,64},{64,128},{128,192},{193,1},{1,65},{65,129},{129,193... | collective-permute-start | bytes 393224 | tf_op jit(solution)/shard_map/ppermute | solution.py:78
  164.5 7.1 %collective-permute-start.23 = (bf16[8,4096]{1,0:T(8,128)(2,1)S(1)}, bf16[8,4096]{1,0:T(8,128)(2,1)S(1)}, u32[]{:S(2)}, u32[]{:S(2)}) collective-permute-start(bf16[8,4096]{1,0:T(8,128)(2,1)S(1)} %slice.94), channel_id=1, source_target_pairs={{32,0},{0,32},{33,1},{1,33},{34,2},{2,34},{35,3},{3,35},{36,4},{4,... | collective-permute-start | bytes 196616 | tf_op jit(solution)/shard_map/ppermute | solution.py:78

commit v2 on v1

--- a/solution.py
+++ b/solution.py
@@ -14,11 +14,12 @@
 Z, CORE, X, Y = TOK_VOC
 F32, BF16 = jnp.float32, jnp.bfloat16
 
-PARTS = (
-    (0, 0, 0, 4), (1, 0, 0, 4),
-    (0, 1, 0, 4), (0, 3, 0, 4), (1, 1, 0, 4), (1, 3, 0, 4),
-    (0, 2, 0, 2), (0, 2, 2, 2), (1, 2, 0, 2), (1, 2, 2, 2),
+GROUPS = (
+    ((0, 0, 0, 4), (1, 0, 0, 4)),
+    ((0, 1, 0, 4), (0, 3, 0, 4), (1, 1, 0, 4)),
+    ((1, 3, 0, 4), (0, 2, 0, 2), (0, 2, 2, 2), (1, 2, 0, 2), (1, 2, 2, 2)),
 )
+PARTS = sum(GROUPS, ())
 
 
 inner_rate = 0.5
@@ -66,13 +67,6 @@
     return lax.ppermute(value, (CORE, X, Y), by_core(k, True))
 
 
-def take_across(value, k):
-    pairs = by_core(k, True)
-    half = len(pairs)
-    both = [(a + (1 - z) * half, b + z * half) for z in range(2) for a, b in pairs]
-    return lax.ppermute(value, (Z, CORE, X, Y), both)
-
-
 def take(value, axis, k):
     n = lax.axis_size(axis)
     return lax.ppermute(value, axis, [((i + k) % n, i) for i in range(n)])
@@ -82,13 +76,17 @@
     return lambda value, k: take(value, axis, k)
 
 
-def ring_gather(value, take):
-    half = value.shape[0] // 2
-    up = take(value, 1)
-    down = take(value, -1)
-    far_up = take(up[:half], 1)
-    far_down = take(down[half:], -1)
-    return value, up, far_up, far_down, down
+def ring_gather(first, second, take):
+    got = {}
+    for name, value, k in (
+        ("first_up", first, 1), ("first_down", second, -1), ("second_up", second, 1), ("second_down", first, -1)
+    ):
+        got[name] = take(value, k)
+    far_up = take(got["first_up"], 1)
+    far_down = take(got["first_down"], -1)
+    return (
+        first, second, got["first_up"], got["second_up"], far_up, far_down, got["second_down"], got["first_down"]
+    )
 
 
 def to_f32(value):
@@ -256,17 +254,21 @@
     lane = lax.broadcasted_iota(jnp.int32, (1, strip), 1)
     unit = out.shape[0] // 4
     start = 0
-    for values, id_part, lines in zip(logits, ids, ((0,), (1, 3), (2,))):
-        for n, line in enumerate(lines):
-            first = (other * len(lines) + n) * unit
-            hits = id_part[first : first + unit, :] - here[4]
-            total = log_total[start + first : start + first + unit, :]
-            for k in range(0, vocab_rows, strip):
-                onehot = (hits - k == lane).astype(F32)
-                errors[line * unit : (line + 1) * unit, k : k + strip] = (
-                    jnp.exp(values[first : first + unit, k : k + strip] - total) - onehot
-                ).astype(BF16)
-        start += values.shape[0]
+    for values, id_part, parts in zip(logits, ids, GROUPS):
+        first = 0
+        for whose, line, cell, count in parts:
+            last = first + unit * count // 4
+            to = line * unit + unit * cell // 4
+            if whose == other:
+                hits = id_part[first:last, :] - here[4]
+                total = log_total[start + first : start + last, :]
+                for k in range(0, vocab_rows, strip):
+                    onehot = (hits - k == lane).astype(F32)
+                    errors[to : to + last - first, k : k + strip] = (
+                        jnp.exp(values[first:last, k : k + strip] - total) - onehot
+                    ).astype(BF16)
+            first = last
+        start += first
 
     def step(j, _):
         cols = pl.ds(pl.multiple_of(j * block, block), block)
@@ -283,9 +285,19 @@
     pseudo_grad = outer[...] - (mean_weight - (inner_rate / 4) * slab_grad)
     moved = momentum_coef * momentum[...] + pseudo_grad
     new_outer = outer[...] - outer_rate * (pseudo_grad + momentum_coef * moved)
-    outs[0][...] = new_outer.astype(outs[0].dtype)
-    if len(outs) == 2:
-        outs[1][...] = moved
+    if outs[0].dtype == F32:
+        outs[0][...], outs[1][...] = new_outer, moved
+    else:
+        half = outs[0].shape[0]
+        outs[0][...], outs[1][...] = new_outer[:half].astype(BF16), new_outer[half:].astype(BF16)
+
+
+def grad_kernel(here, first, second, third, fourth, *outs):
+    rows = outs[0].shape[0]
+    for k, out in enumerate(outs):
+        at = pl.ds(k * rows, rows)
+        value = first[at, :] + to_f32(second[at, :]) + to_f32(third[at, :]) + to_f32(fourth[at, :])
+        out[...] = value.astype(out.dtype)
 
 
 def join_kernel(here, *refs):
@@ -305,17 +317,14 @@
     row[...] = jnp.sum(jnp.where(at[0] == at[1], column[...], 0.0), axis=0, keepdims=True)
 
 
-def place_kernel(part, here, mine, up, low, high, down, out, sems):
-    half = low.shape[0]
-
-    def copy(piece, k, first, n):
-        at = pl.multiple_of(lax.rem(here[5] + k, 4) * part, part)
-        to = out.at[pl.ds(first, piece.shape[0]), pl.ds(at, part)]
-        return pltpu.make_async_copy(piece, to, sems.at[n])
-
-    copies = [
-        copy(mine, 0, 0, 0), copy(up, 1, 0, 1), copy(low, 2, 0, 2), copy(high, 2, half, 3), copy(down, 3, 0, 4)
-    ]
+def place_kernel(part, here, *refs):
+    pieces, out, sems = refs[:8], refs[8], refs[9]
+    half = pieces[0].shape[0]
+    copies = []
+    for k, piece in enumerate(pieces):
+        at = pl.multiple_of(lax.rem(here[5] + k // 2, 4) * part, part)
+        to = out.at[pl.ds(k % 2 * half, half), pl.ds(at, part)]
+        copies.append(pltpu.make_async_copy(piece, to, sems.at[k]))
     for one in copies:
         one.start()
     for one in copies:
@@ -338,22 +347,28 @@
     ids = targets[0]
     codes = jnp.stack((ids >> 8, ids & 255), 1).astype(BF16)
     piece = jnp.concatenate((hidden[0], jnp.pad(codes, ((0, 0), (0, 126)))), 1)
-    cells = {(0, 0): piece}
+    across = take(piece, Z, 1)
+    piece = call(join_kernel, shaped(BF16, 2 * own, piece.shape[1]), here, piece, across)
     order = call(functools.partial(table_kernel, own), shaped(BF16, tokens, tokens), here)
-    for k in (2, 1, 3, 0):
-        for plane, get in ((1, take_across), (0, take_inner)):
-            if k or plane:
-                cells[k, plane] = get(piece, k)
-    cells = [cells[k, plane] for k in range(4) for plane in range(2)]
-    line = call(join_kernel, shaped(BF16, 8 * own, piece.shape[1]), here, *cells)
+    inner = {}
+    for k in (2, 1, 3):
+        inner[k] = take_inner(piece, k)
+    line = call(
+        join_kernel, shaped(BF16, 8 * own, piece.shape[1]), here, piece, inner[1], inner[2], inner[3]
+    )
     up = take_outer(line, 1)
     down = take_outer(line, -1)
     cut = line.shape[0] // 2
     far_up = take_outer(up[:cut], 1)
     far_down = take_outer(down[cut:], -1)
 
-    def with_other(*parts):
-        return (*parts, *[take(one, CORE, 1) for one in parts])
+    def swapped(*parts):
+        return [take(one, CORE, 1) for one in parts]
+
+    parts_0 = line, *swapped(line)
+    up_swapped, down_swapped = swapped(up, down)
+    parts_1 = up, down, up_swapped
+    parts_2 = down_swapped, far_up, far_down, *swapped(far_up, far_down)
 
     def features(value, k):
         return lax.dynamic_slice_in_dim(value, ((rep + k) % reps) * part, part, 1)
@@ -385,9 +400,9 @@
             flops=2 * max(rows, 256) * vocab_rows * width, **kind,
         )
 
-    logits_0, ids_0, states_0, table_0, w = logits_of(with_other(line), weights, ())
-    logits_1, ids_1, states_1, table_1 = logits_of(with_other(up, down), w, (table_0,))
-    logits_2, ids_2, states_2, stats = logits_of(with_other(far_up, far_down), w, (table_0, table_1, order))
+    logits_0, ids_0, states_0, table_0, w = logits_of(parts_0, weights, ())
+    logits_1, ids_1, states_1, table_1 = logits_of(parts_1, w, (table_0,))
+    logits_2, ids_2, states_2, stats = logits_of(parts_2, w, (table_0, table_1, order))
     logits, every_id = (logits_0, logits_1, logits_2), (ids_0, ids_1, ids_2)
     states = (states_0, states_1, states_2)
 
@@ -422,21 +437,26 @@
 
     slab_grads = [mine, *arrivals(grads, along("rep"))]
     operands = (here, outer_weight, momentum, *slab_weights, *slab_grads)
-    rounded = call(outer_kernel, shaped(BF16, slab_rows, part), *operands)
+    rounded = call(outer_kernel, [shaped(BF16, slab_rows // 2, part)] * 2, *operands)
     new_outer, new_momentum = call(outer_kernel, [shaped(F32, slab_rows, part)] * 2, *operands)
-    pieces = ring_gather(rounded, along("rep"))
+    pieces = ring_gather(*rounded, along("rep"))
     next_inner = call(
         functools.partial(place_kernel, part), shaped(BF16, slab_rows, width), here, *pieces,
-        scratch=[pltpu.SemaphoreType.DMA((5,))], out_spec=pl.BlockSpec(memory_space=pltpu.HBM),
+        scratch=[pltpu.SemaphoreType.DMA((8,))], out_spec=pl.BlockSpec(memory_space=pltpu.HBM),
     )
 
     got = take(send, CORE, 1)
     total = (to_f32(keep) + to_f32(got)).reshape(4, 8 * own, width)
     rounded = total.astype(BF16)
     got = arrivals(rounded[1:], take_outer)
-    line = (total[0] + sum(to_f32(one) for one in got)).reshape(4, 2 * own, width)
-    rounded = line.astype(BF16)
-    pair = line[0] + sum(to_f32(take_inner(rounded[k], -k)) for k in (1, 2, 3))
+    pair, *others = call(
+        grad_kernel,
+        [shaped(F32, 2 * own, width)] + [shaped(BF16, 2 * own, width)] * 3,
+        here, total[0], *got,
+    )
+    for k in (2, 1, 3):
+        got = take_inner(others[k - 1], -k)
+        pair = pair + to_f32(got)
     pair_sent = take(pair[own:].astype(BF16), Z, 1)
     token_grad = (pair[:own] + to_f32(pair_sent))[None]
     return (token_loss, token_grad, new_outer, new_momentum, next_inner)

time: 173 us -> 174 us (level)
  the two profiles are of different devices: /device:TPU:32 before, /device:TPU:1 now
where the time goes in v2:
time: 174 us
  starting transfers between devices  61.9 us (36%)
  waiting for transfers between devices  46.5 us (27%)
  Pallas kernels  37.5 us (22%)
  blocking collectives  15 us (9%)
  local copies, waits for them, and re-layouts  7.45 us (4%)
  other arithmetic  4.61 us (3%)
    ppermute x20, starting transfers between devices, take(): return lax.ppermute(value, axis, [((i + k) % n, i) for i in range(n)])  48.1 us
    pallas_call x15, Pallas kernels, call(): pl.pallas_call(kernel, in_specs=[SMEM] + [specs.get(k, VMEM) for k in ran...  37.5 us
    ppermute x20, waiting for transfers between devices, take(): return lax.ppermute(value, axis, [((i + k) % n, i) for i in range(n)])  36.8 us
    all_to_all x1, blocking collectives, per_device(): stats = lax.all_to_all(stats, VOC, 0, 0, tiled=True)  9.52 us
    ppermute x7, starting transfers between devices, take_outer(): return lax.ppermute(value, (CORE, X, Y), by_core(k, False))  7.36 us
    ppermute x6, starting transfers between devices, take_inner(): return lax.ppermute(value, (CORE, X, Y), by_core(k, True))  6.38 us
    ppermute x6, waiting for transfers between devices, take_inner(): return lax.ppermute(value, (CORE, X, Y), by_core(k, True))  6.07 us
    all_gather x1, blocking collectives, per_device(): stats = lax.all_gather(stats, TOK)  5.45 us
  transfers between devices with their start and end apart: 33, of which 12 were waited for; matrix products, arithmetic and copies ran while one was open for 4% of the time, Pallas kernels for 13%

profile of v2, /device:TPU:1, one launch (start us, length us, event | category | flops | bytes accessed | tf_op | source)
XLA Modules:
  0.0 173.9 jit_solution(3427928033479666281)
XLA Ops:
  0.6 0.7 convert_bitcast_fusion.1
  1.4 0.8 fusion.2.refs_0_
  2.2 2.5 %collective-permute-start = (bf16[8,4224]{1,0:T(8,128)(2,1)S(1)}, bf16[8,4224]{1,0:T(8,128)(2,1)S(1)}, u32[]{:S(2)}, u32[]{:S(2)}) collective-permute-start(bf16[8,4224]{1,0:T(8,128)(2,1)S(1)} %fusion.2.refs_0_), channel_id=1, source_target_pairs={{32,0},{0,32},{33,1},{1,33},{34,2},{2,34},{35,3},{3,35},{36,4},{4,... | collective-permute-start | bytes 202760 | tf_op jit(solution)/shard_map/ppermute | solution.py:72
  4.8 1.6 collective-permute-done.refs_1_
  6.4 0.5 shard_map.92.refs_0_
  6.9 2.8 %collective-permute-start.1 = (bf16[16,4224]{1,0:T(8,128)(2,1)S(1)}, bf16[16,4224]{1,0:T(8,128)(2,1)S(1)}, u32[]{:S(2)}, u32[]{:S(2)}) collective-permute-start(bf16[16,4224]{1,0:T(8,128)(2,1)S(1)} %shard_map.92.refs_0_), channel_id=1, source_target_pairs={{4,0},{5,1},{6,2},{7,3},{8,4},{9,5},{10,6},{11,7},{12,8},{13,9},{1... | collective-permute-start | bytes 405512 | tf_op jit(solution)/shard_map/ppermute | solution.py:67
  9.7 0.3 collective-permute-start.2
  10.1 0.7 collective-permute-start.3
  10.8 2.4 %collective-permute-done.1.refs_1_ = bf16[16,4224]{1,0:T(8,128)(2,1)S(1)} collective-permute-done((bf16[16,4224]{1,0:T(8,128)(2,1)S(1)}, bf16[16,4224]{1,0:T(8,128)(2,1)S(1)}, u32[]{:S(2)}, u32[]{:S(2)}) %collective-permute-start.1) | collective-permute-done | bytes 135200 | tf_op jit(solution)/shard_map/ppermute | solution.py:67
  13.2 2.1 %collective-permute-done.2.refs_2_ = bf16[16,4224]{1,0:T(8,128)(2,1)S(1)} collective-permute-done((bf16[16,4224]{1,0:T(8,128)(2,1)S(1)}, bf16[16,4224]{1,0:T(8,128)(2,1)S(1)}, u32[]{:S(2)}, u32[]{:S(2)}) %collective-permute-start.2) | collective-permute-done | bytes 135200 | tf_op jit(solution)/shard_map/ppermute | solution.py:67
  15.2 1.6 collective-permute-done.3.refs_3_
  16.9 0.6 shard_map.93.refs_0_
  17.4 2.3 %collective-permute-start.6 = (bf16[64,4224]{1,0:T(8,128)(2,1)S(1)}, bf16[64,4224]{1,0:T(8,128)(2,1)S(1)}, u32[]{:S(2)}, u32[]{:S(2)}) collective-permute-start(bf16[64,4224]{1,0:T(8,128)(2,1)S(1)} %shard_map.93.refs_0_), channel_id=1, source_target_pairs={{1,0},{2,1},{3,2},{0,3},{5,4},{6,5},{7,6},{4,7},{9,8},{10,9},{11,1... | collective-permute-start | bytes 1622024 | tf_op jit(solution)/shard_map/ppermute | solution.py:63
  19.7 3.4 %collective-permute-start.11 = (bf16[64,4224]{1,0:T(8,128)(2,1)S(1)}, bf16[64,4224]{1,0:T(8,128)(2,1)S(1)}, u32[]{:S(2)}, u32[]{:S(2)}) collective-permute-start(bf16[64,4224]{1,0:T(8,128)(2,1)S(1)} %shard_map.93.refs_0_), channel_id=1, source_target_pairs={{16,0},{0,16},{17,1},{1,17},{18,2},{2,18},{19,3},{3,19},{20,4},{4,... | collective-permute-start | bytes 1622024 | tf_op jit(solution)/shard_map/ppermute | solution.py:72
  23.1 3.0 %collective-permute-done.6.refs_0_ = bf16[64,4224]{1,0:T(8,128)(2,1)S(1)} collective-permute-done((bf16[64,4224]{1,0:T(8,128)(2,1)S(1)}, bf16[64,4224]{1,0:T(8,128)(2,1)S(1)}, u32[]{:S(2)}, u32[]{:S(2)}) %collective-permute-start.6) | collective-permute-done | bytes 540704 | tf_op jit(solution)/shard_map/ppermute | solution.py:63
  26.0 3.9 %collective-permute-start.12 = (bf16[64,4224]{1,0:T(8,128)(2,1)S(1)}, bf16[64,4224]{1,0:T(8,128)(2,1)S(1)}, u32[]{:S(2)}, u32[]{:S(2)}) collective-permute-start(bf16[64,4224]{1,0:T(8,128)(2,1)S(1)} %collective-permute-done.6.refs_0_), channel_id=1, source_target_pairs={{16,0},{0,16},{17,1},{1,17},{18,2},{2,18},{19,3},{3,19},{20,4},{4,... | collective-permute-start | bytes 1622024 | tf_op jit(solution)/shard_map/ppermute | solution.py:72
  30.0 0.4 collective-permute-start.7
  30.3 1.3 collective-permute-start.8
  31.6 2.3 %collective-permute-start.5 = (bf16[64,4224]{1,0:T(8,128)(2,1)S(1)}, bf16[64,4224]{1,0:T(8,128)(2,1)S(1)}, u32[]{:S(2)}, u32[]{:S(2)}) collective-permute-start(bf16[64,4224]{1,0:T(8,128)(2,1)S(1)} %collective-permute-done.4.refs_1_), channel_id=1, source_target_pairs={{16,0},{0,16},{17,1},{1,17},{18,2},{2,18},{19,3},{3,19},{20,4},{4,... | collective-permute-start | bytes 1622024 | tf_op jit(solution)/shard_map/ppermute | solution.py:72
  33.9 0.9 shard_map.96.refs_8_.refs_10_
  34.9 0.7 collective-permute-done.7.refs_1_
  35.6 2.1 %collective-permute-start.9 = (bf16[32,4224]{1,0:T(8,128)(2,1)S(1)}, bf16[32,4224]{1,0:T(8,128)(2,1)S(1)}, u32[]{:S(2)}, u32[]{:S(2)}) collective-permute-start(bf16[32,4224]{1,0:T(8,128)(2,1)S(1)} %collective-permute-done.7.refs_1_), channel_id=1, source_target_pairs={{16,0},{0,16},{17,1},{1,17},{18,2},{2,18},{19,3},{3,19},{20,4},{4,... | collective-permute-start | bytes 811016 | tf_op jit(solution)/shard_map/ppermute | solution.py:72
  37.7 3.8 %collective-permute-start.10 = (bf16[32,4224]{1,0:T(8,128)(2,1)S(1)}, bf16[32,4224]{1,0:T(8,128)(2,1)S(1)}, u32[]{:S(2)}, u32[]{:S(2)}) collective-permute-start(bf16[32,4224]{1,0:T(8,128)(2,1)S(1)} %collective-permute-done.8.refs_2_), channel_id=1, source_target_pairs={{16,0},{0,16},{17,1},{1,17},{18,2},{2,18},{19,3},{3,19},{20,4},{4,... | collective-permute-start | bytes 811016 | tf_op jit(solution)/shard_map/ppermute | solution.py:72
  41.5 5.8 %shard_map.94 = (f32[128,1024]{1,0:T(8,128)S(1)}, s32[128,1]{1,0:T(8,128)S(1)}, bf16[128,4096]{1,0:T(8,128)(2,1)S(1)}, f32[128,128]{1,0:T(8,128)S(1)}, bf16[1024,4096]{1,0:T(8,128)(2,1)S(1)}) custom-call(s32[6]{0:T(128)S(1)} %stack.33.here, bf16[64,4224]{1,0:T(8,128)(2,1)S(1)} %shard_map.93.refs_0_, bf16[64,4224]{1,0:T(8,128)(2,1)S(1)} %collective-permute-done.11.refs_1_, ...), custom_call_target="tpu_custom_call" | custom-call | flops 2147483648 | bytes 19497496 | tf_op jit(solution)/shard_map/pallas_call | solution.py:34
  47.3 4.5 %shard_map.95 = (f32[192,1024]{1,0:T(8,128)S(1)}, s32[192,1]{1,0:T(8,128)S(1)}, bf16[192,4096]{1,0:T(8,128)(2,1)S(1)}, f32[192,128]{1,0:T(8,128)S(1)}) custom-call(s32[6]{0:T(128)S(1)} %stack.33.here, bf16[64,4224]{1,0:T(8,128)(2,1)S(1)} %collective-permute-done.6.refs_0_, bf16[64,4224]{1,0:T(8,128)(2,1)S(1)} %collective-permute-done.4.refs_1_, ...), custom_call_target="tpu_custom_call" | custom-call | flops 2147483648 | bytes 12534552 | tf_op jit(solution)/shard_map/pallas_call | solution.py:34
  51.8 4.8 %shard_map.97 = (f32[192,1024]{1,0:T(8,128)S(1)}, s32[192,1]{1,0:T(8,128)S(1)}, bf16[192,4096]{1,0:T(8,128)(2,1)S(1)}, f32[8,512]{1,0:T(8,128)S(1)}) custom-call(s32[6]{0:T(128)S(1)} %stack.33.here, bf16[64,4224]{1,0:T(8,128)(2,1)S(1)} %collective-permute-done.5.refs_0_, bf16[32,4224]{1,0:T(8,128)(2,1)S(1)} %collective-permute-done.7.refs_1_, ...), custom_call_target="tpu_custom_call" | custom-call | flops 2147483648 | bytes 13075224 | tf_op jit(solution)/shard_map/pallas_call | solution.py:34
  56.7 5.4 %all-gather = f32[32,512]{1,0:T(8,128)S(1)} all-gather(f32[8,512]{1,0:T(8,128)S(1)} %get-tuple-element.35), channel_id=2, replica_groups=mesh['rep'=4,'tok_0'=2,'tok_1'=2,'voc_0'=4,'voc_1'=4] {'tok_0','tok_1'}, dimensions={0}, use_global_device_ids=true | all-gather | bytes 81920 | tf_op jit(solution)/shard_map/all_gather | solution.py:409
  62.1 0.6 shard_map.98
  62.7 9.5 %all_to_all.5.refs_0_ = f32[16,4,512]{2,1,0:T(4,128)S(1)} all-to-all(f32[16,4,512]{2,1,0:T(4,128)S(1)} %shard_map.98), channel_id=1, replica_groups=mesh['rep'=4,'tok_0'=2,'tok_1'=2,'voc_0'=4,'voc_1'=4] {'voc_0','voc_1'}, dimensions={0} | all-to-all | bytes 262144 | tf_op jit(solution)/shard_map/all_to_all | solution.py:411
  72.2 3.1 %shard_map.99 = (f32[8,1]{1,0:T(8,128)S(1)}, f32[512,1]{1,0:T(8,128)S(1)}, f32[128,1024]{1,0:T(8,128)S(1)}, bf16[128,1024]{1,0:T(8,128)(2,1)S(1)}, bf16[128,1024...) custom-call(s32[6]{0:T(128)S(1)} %stack.33.here, f32[16,4,512]{2,1,0:T(4,128)S(1)} %all_to_all.5.refs_0_, ...), custom_call_target="tpu_custom_call" | custom-call | flops 536870912 | bytes 8261688 | tf_op jit(solution)/shard_map/pallas_call | solution.py:34
  75.4 5.8 %shard_map.102 = bf16[256,4096]{1,0:T(8,128)(2,1)} custom-call(s32[6]{0:T(128)S(1)} %stack.33.here, f32[128,1024]{1,0:T(8,128)S(1)} %get-tuple-element.36.refs_1_.refs_0_, f32[192,1024]{1,0:T(8,128)S(1)} %get-tuple-element.37.refs_2_.refs_1_, f32[192,1024]{1,0:T(8,128)S(1)} %get-tuple-element.38.refs_3_.refs_2_, ...), custom_call_target="tpu_custom_call" | custom-call | flops 2147483648 | bytes 12587032 | tf_op jit(solution)/shard_map/pallas_call | solution.py:34
  81.2 1.4 collective-permute-start.13
  82.6 2.3 %slice.45 = bf16[1,128,4096]{2,1,0:T(8,128)(2,1)} slice(bf16[1,1024,4096]{2,1,0:T(8,128)(2,1)} %param.7), slice={[0:1], [0:128], [0:4096]} | slice | bytes 2097152 | tf_op jit(solution)/shard_map/slice | solution.py:376
  84.9 1.3 dynamic-slice_bitcast_fusion
  86.2 5.7 %collective-permute-start.21 = (bf16[128,1024]{1,0:T(8,128)(2,1)S(1)}, bf16[128,1024]{1,0:T(8,128)(2,1)S(1)}, u32[]{:S(2)}, u32[]{:S(2)}) collective-permute-start(bf16[128,1024]{1,0:T(8,128)(2,1)S(1)} %get-tuple-element.66), channel_id=1, source_target_pairs={{64,0},{128,64},{192,128},{0,192},{65,1},{129,65},{193,129},{1,193... | collective-permute-start | bytes 786440 | tf_op jit(solution)/shard_map/ppermute | solution.py:72
  91.9 1.0 collective-permute-start.22
  92.9 2.3 %collective-permute-start.23 = (bf16[128,1024]{1,0:T(8,128)(2,1)S(1)}, bf16[128,1024]{1,0:T(8,128)(2,1)S(1)}, u32[]{:S(2)}, u32[]{:S(2)}) collective-permute-start(bf16[128,1024]{1,0:T(8,128)(2,1)S(1)} %get-tuple-element.64), channel_id=1, source_target_pairs={{192,0},{0,64},{64,128},{128,192},{193,1},{1,65},{65,129},{129,193... | collective-permute-start | bytes 786440 | tf_op jit(solution)/shard_map/ppermute | solution.py:72
  95.2 2.1 %collective-permute-start.24 = (bf16[128,1024]{1,0:T(8,128)(2,1)S(1)}, bf16[128,1024]{1,0:T(8,128)(2,1)S(1)}, u32[]{:S(2)}, u32[]{:S(2)}) collective-permute-start(bf16[128,1024]{1,0:T(8,128)(2,1)S(1)} %copy-done.7), channel_id=1, source_target_pairs={{128,0},{192,64},{0,128},{64,192},{129,1},{193,65},{1,129},{65,193... | collective-permute-start | bytes 786440 | tf_op jit(solution)/shard_map/ppermute | solution.py:72
  97.3 3.4 %copy-done.1 = bf16[1024,4096]{1,0:T(8,128)(2,1)S(1)} copy-done((bf16[1024,4096]{1,0:T(8,128)(2,1)S(1)}, bf16[1024,4096]{1,0:T(8,128)(2,1)}, u32[]{:S(2)}) %copy-start.1) | copy-done | bytes 8388632
  100.7 4.5 %shard_map.101 = bf16[256,4096]{1,0:T(8,128)(2,1)S(1)} custom-call(s32[6]{0:T(128)S(1)} %stack.33.here, f32[128,1024]{1,0:T(8,128)S(1)} %get-tuple-element.36.refs_1_.refs_0_, f32[192,1024]{1,0:T(8,128)S(1)} %get-tuple-element.37.refs_2_.refs_1_, f32[192,1024]{1,0:T(8,128)S(1)} %get-tuple-element.38.refs_3_.refs_2_, ...), custom_call_target="tpu_custom_call" | custom-call | flops 2147483648 | bytes 12587032 | tf_op jit(solution)/shard_map/pallas_call | solution.py:34
  105.2 2.4 %fusion.3 = (bf16[256,4096]{1,0:T(8,128)(2,1)S(1)}, f32[256,4096]{1,0:T(8,128)S(1)}) fusion(bf16[256,4096]{1,0:T(8,128)(2,1)} %collective-permute-done.13, bf16[256,4096]{1,0:T(8,128)(2,1)S(1)} %shard_map.101), kind=kLoop, calls=%fused_computation.15 | loop fusion | flops 4194304 | bytes 10485760 | tf_op jit(solution)/shard_map/convert_element_type | solution.py:450
  107.8 1.0 collective-permute-start.14
  108.8 0.4 collective-permute-start.15
  109.4 2.1 %collective-permute-start.16 = (bf16[64,4096]{1,0:T(8,128)(2,1)S(1)}, bf16[64,4096]{1,0:T(8,128)(2,1)S(1)}, u32[]{:S(2)}, u32[]{:S(2)}) collective-permute-start(bf16[64,4096]{1,0:T(8,128)(2,1)S(1)} %get-tuple-element.61), channel_id=1, source_target_pairs={{1,0},{2,1},{3,2},{0,3},{5,4},{6,5},{7,6},{4,7},{9,8},{10,9},{11,1... | collective-permute-start | bytes 1572872 | tf_op jit(solution)/shard_map/ppermute | solution.py:63
  111.4 0.4 collective-permute-done.23.w3
  111.9 2.8 %collective-permute-start.25 = (bf16[128,1024]{1,0:T(8,128)(2,1)S(1)}, bf16[128,1024]{1,0:T(8,128)(2,1)S(1)}, u32[]{:S(2)}, u32[]{:S(2)}) collective-permute-start(bf16[128,1024]{1,0:T(8,128)(2,1)S(1)} %copy-done.5), channel_id=1, source_target_pairs={{192,0},{0,64},{64,128},{128,192},{193,1},{1,65},{65,129},{129,193... | collective-permute-start | bytes 786440 | tf_op jit(solution)/shard_map/ppermute | solution.py:72
  114.7 16.4 %collective-permute-done.24.g1 = bf16[128,1024]{1,0:T(8,128)(2,1)S(1)} collective-permute-done((bf16[128,1024]{1,0:T(8,128)(2,1)S(1)}, bf16[128,1024]{1,0:T(8,128)(2,1)S(1)}, u32[]{:S(2)}, u32[]{:S(2)}) %collective-permute-start.24) | collective-permute-done | bytes 262176 | tf_op jit(solution)/shard_map/ppermute | solution.py:72
  131.1 1.7 collective-permute-start.26
  132.8 9.5 %collective-permute-done.25.g2 = bf16[128,1024]{1,0:T(8,128)(2,1)S(1)} collective-permute-done((bf16[128,1024]{1,0:T(8,128)(2,1)S(1)}, bf16[128,1024]{1,0:T(8,128)(2,1)S(1)}, u32[]{:S(2)}, u32[]{:S(2)}) %collective-permute-start.25) | collective-permute-done | bytes 262176 | tf_op jit(solution)/shard_map/ppermute | solution.py:72
  142.3 1.0 shard_map.105
  143.3 4.9 %collective-permute-start.27 = (bf16[64,1024]{1,0:T(8,128)(2,1)S(1)}, bf16[64,1024]{1,0:T(8,128)(2,1)S(1)}, u32[]{:S(2)}, u32[]{:S(2)}) collective-permute-start(bf16[64,1024]{1,0:T(8,128)(2,1)S(1)} %get-tuple-element.57.refs_0_), channel_id=1, source_target_pairs={{64,0},{128,64},{192,128},{0,192},{65,1},{129,65},{193,129},{1,193... | collective-permute-start | bytes 393224 | tf_op jit(solution)/shard_map/ppermute | solution.py:72
  148.2 0.8 shard_map.103
  149.0 0.7 collective-permute-start.19
  149.7 0.9 collective-permute-start.18
  150.6 1.0 collective-permute-start.17
  151.6 4.5 %collective-permute-start.28 = (bf16[64,1024]{1,0:T(8,128)(2,1)S(1)}, bf16[64,1024]{1,0:T(8,128)(2,1)S(1)}, u32[]{:S(2)}, u32[]{:S(2)}) collective-permute-start(bf16[64,1024]{1,0:T(8,128)(2,1)S(1)} %get-tuple-element.58.refs_1_), channel_id=1, source_target_pairs={{64,0},{128,64},{192,128},{0,192},{65,1},{129,65},{193,129},{1,193... | collective-permute-start | bytes 393224 | tf_op jit(solution)/shard_map/ppermute | solution.py:72
  156.0 3.6 %collective-permute-start.29 = (bf16[64,1024]{1,0:T(8,128)(2,1)S(1)}, bf16[64,1024]{1,0:T(8,128)(2,1)S(1)}, u32[]{:S(2)}, u32[]{:S(2)}) collective-permute-start(bf16[64,1024]{1,0:T(8,128)(2,1)S(1)} %collective-permute-done.27.refs_2_), channel_id=1, source_target_pairs={{64,0},{128,64},{192,128},{0,192},{65,1},{129,65},{193,129},{1,193... | collective-permute-start | bytes 393224 | tf_op jit(solution)/shard_map/ppermute | solution.py:72
  159.7 0.3 collective-permute-start.20
  160.0 1.1 shard_map.100
  161.1 1.9 %shard_map.104 = (f32[128,1024]{1,0:T(8,128)}, f32[128,1024]{1,0:T(8,128)}) custom-call(s32[6]{0:T(128)S(1)} %stack.33.here, f32[128,1024]{1,0:T(8,128)S(1)} %copy-done.2, f32[128,1024]{1,0:T(8,128)S(1)} %copy-done.3, bf16[128,1024]{1,0:T(8,128)(2,1)S(1)} %get-tuple-element.67.w0, bf16[128,1024]{1,0:T(8,128)(2,1)S(1)} %collective-permute-done.21.w1, ...), custom_call_target="tpu_custom_call" | custom-call | flops 4456472 | bytes 4456472 | tf_op jit(solution)/shard_map/pallas_call | solution.py:34
  163.0 1.7 collective-permute-done.29.refs_4_
  164.7 7.0 %collective-permute-done.31.refs_5_ = bf16[64,1024]{1,0:T(8,128)(2,1)S(1)} collective-permute-done((bf16[64,1024]{1,0:T(8,128)(2,1)S(1)}, bf16[64,1024]{1,0:T(8,128)(2,1)S(1)}, u32[]{:S(2)}, u32[]{:S(2)}) %collective-permute-start.31) | collective-permute-done | bytes 131104 | tf_op jit(solution)/shard_map/ppermute | solution.py:72
  171.7 1.6 shard_map.106
  173.2 0.7 fusion.1
  (50 shorter events, 0.8 us)
Async XLA Ops:
  2.2 4.1 %collective-permute-start = (bf16[8,4224]{1,0:T(8,128)(2,1)S(1)}, bf16[8,4224]{1,0:T(8,128)(2,1)S(1)}, u32[]{:S(2)}, u32[]{:S(2)}) collective-permute-start(bf16[8,4224]{1,0:T(8,128)(2,1)S(1)} %fusion.2.refs_0_), channel_id=1, source_target_pairs={{32,0},{0,32},{33,1},{1,33},{34,2},{2,34},{35,3},{3,35},{36,4},{4,... | collective-permute-start | bytes 202760 | tf_op jit(solution)/shard_map/ppermute | solution.py:72
  6.9 6.2 %collective-permute-start.1 = (bf16[16,4224]{1,0:T(8,128)(2,1)S(1)}, bf16[16,4224]{1,0:T(8,128)(2,1)S(1)}, u32[]{:S(2)}, u32[]{:S(2)}) collective-permute-start(bf16[16,4224]{1,0:T(8,128)(2,1)S(1)} %shard_map.92.refs_0_), channel_id=1, source_target_pairs={{4,0},{5,1},{6,2},{7,3},{8,4},{9,5},{10,6},{11,7},{12,8},{13,9},{1... | collective-permute-start | bytes 405512 | tf_op jit(solution)/shard_map/ppermute | solution.py:67
  9.7 5.5 %collective-permute-start.2 = (bf16[16,4224]{1,0:T(8,128)(2,1)S(1)}, bf16[16,4224]{1,0:T(8,128)(2,1)S(1)}, u32[]{:S(2)}, u32[]{:S(2)}) collective-permute-start(bf16[16,4224]{1,0:T(8,128)(2,1)S(1)} %shard_map.92.refs_0_), channel_id=1, source_target_pairs={{8,0},{9,1},{10,2},{11,3},{12,4},{13,5},{14,6},{15,7},{0,8},{1,9},... | collective-permute-start | bytes 405512 | tf_op jit(solution)/shard_map/ppermute | solution.py:67
  10.1 6.8 %collective-permute-start.3 = (bf16[16,4224]{1,0:T(8,128)(2,1)S(1)}, bf16[16,4224]{1,0:T(8,128)(2,1)S(1)}, u32[]{:S(2)}, u32[]{:S(2)}) collective-permute-start(bf16[16,4224]{1,0:T(8,128)(2,1)S(1)} %shard_map.92.refs_0_), channel_id=1, source_target_pairs={{12,0},{13,1},{14,2},{15,3},{0,4},{1,5},{2,6},{3,7},{4,8},{5,9},{6... | collective-permute-start | bytes 405512 | tf_op jit(solution)/shard_map/ppermute | solution.py:67
  17.4 8.6 %collective-permute-start.6 = (bf16[64,4224]{1,0:T(8,128)(2,1)S(1)}, bf16[64,4224]{1,0:T(8,128)(2,1)S(1)}, u32[]{:S(2)}, u32[]{:S(2)}) collective-permute-start(bf16[64,4224]{1,0:T(8,128)(2,1)S(1)} %shard_map.93.refs_0_), channel_id=1, source_target_pairs={{1,0},{2,1},{3,2},{0,3},{5,4},{6,5},{7,6},{4,7},{9,8},{10,9},{11,1... | collective-permute-start | bytes 1622024 | tf_op jit(solution)/shard_map/ppermute | solution.py:63
  19.7 10.6 %collective-permute-start.4 = (bf16[64,4224]{1,0:T(8,128)(2,1)S(1)}, bf16[64,4224]{1,0:T(8,128)(2,1)S(1)}, u32[]{:S(2)}, u32[]{:S(2)}) collective-permute-start(bf16[64,4224]{1,0:T(8,128)(2,1)S(1)} %shard_map.93.refs_0_), channel_id=1, source_target_pairs={{3,0},{0,1},{1,2},{2,3},{7,4},{4,5},{5,6},{6,7},{11,8},{8,9},{9,10... | collective-permute-start | bytes 1622024 | tf_op jit(solution)/shard_map/ppermute | solution.py:63
  19.7 21.8 %collective-permute-start.11 = (bf16[64,4224]{1,0:T(8,128)(2,1)S(1)}, bf16[64,4224]{1,0:T(8,128)(2,1)S(1)}, u32[]{:S(2)}, u32[]{:S(2)}) collective-permute-start(bf16[64,4224]{1,0:T(8,128)(2,1)S(1)} %shard_map.93.refs_0_), channel_id=1, source_target_pairs={{16,0},{0,16},{17,1},{1,17},{18,2},{2,18},{19,3},{3,19},{20,4},{4,... | collective-permute-start | bytes 1622024 | tf_op jit(solution)/shard_map/ppermute | solution.py:72
  26.0 21.3 %collective-permute-start.12 = (bf16[64,4224]{1,0:T(8,128)(2,1)S(1)}, bf16[64,4224]{1,0:T(8,128)(2,1)S(1)}, u32[]{:S(2)}, u32[]{:S(2)}) collective-permute-start(bf16[64,4224]{1,0:T(8,128)(2,1)S(1)} %collective-permute-done.6.refs_0_), channel_id=1, source_target_pairs={{16,0},{0,16},{17,1},{1,17},{18,2},{2,18},{19,3},{3,19},{20,4},{4,... | collective-permute-start | bytes 1622024 | tf_op jit(solution)/shard_map/ppermute | solution.py:72
  30.0 5.7 %collective-permute-start.7 = (bf16[32,4224]{1,0:T(8,128)(2,1)S(1)}, bf16[32,4224]{1,0:T(8,128)(2,1)S(1)}, u32[]{:S(2)}, u32[]{:S(2)}) collective-permute-start(bf16[32,4224]{1,0:T(8,128)(2,1)S(1)} %slice.46), channel_id=1, source_target_pairs={{1,0},{2,1},{3,2},{0,3},{5,4},{6,5},{7,6},{4,7},{9,8},{10,9},{11,1... | collective-permute-start | bytes 811016 | tf_op jit(solution)/shard_map/ppermute | solution.py:63
  30.3 7.4 %collective-permute-start.8 = (bf16[32,4224]{1,0:T(8,128)(2,1)S(1)}, bf16[32,4224]{1,0:T(8,128)(2,1)S(1)}, u32[]{:S(2)}, u32[]{:S(2)}) collective-permute-start(bf16[32,4224]{1,0:T(8,128)(2,1)S(1)} %slice.47), channel_id=1, source_target_pairs={{3,0},{0,1},{1,2},{2,3},{7,4},{4,5},{5,6},{6,7},{11,8},{8,9},{9,10... | collective-permute-start | bytes 811016 | tf_op jit(solution)/shard_map/ppermute | solution.py:63
  31.6 20.2 %collective-permute-start.5 = (bf16[64,4224]{1,0:T(8,128)(2,1)S(1)}, bf16[64,4224]{1,0:T(8,128)(2,1)S(1)}, u32[]{:S(2)}, u32[]{:S(2)}) collective-permute-start(bf16[64,4224]{1,0:T(8,128)(2,1)S(1)} %collective-permute-done.4.refs_1_), channel_id=1, source_target_pairs={{16,0},{0,16},{17,1},{1,17},{18,2},{2,18},{19,3},{3,19},{20,4},{4,... | collective-permute-start | bytes 1622024 | tf_op jit(solution)/shard_map/ppermute | solution.py:72
  35.6 16.2 %collective-permute-start.9 = (bf16[32,4224]{1,0:T(8,128)(2,1)S(1)}, bf16[32,4224]{1,0:T(8,128)(2,1)S(1)}, u32[]{:S(2)}, u32[]{:S(2)}) collective-permute-start(bf16[32,4224]{1,0:T(8,128)(2,1)S(1)} %collective-permute-done.7.refs_1_), channel_id=1, source_target_pairs={{16,0},{0,16},{17,1},{1,17},{18,2},{2,18},{19,3},{3,19},{20,4},{4,... | collective-permute-start | bytes 811016 | tf_op jit(solution)/shard_map/ppermute | solution.py:72
  37.7 14.1 %collective-permute-start.10 = (bf16[32,4224]{1,0:T(8,128)(2,1)S(1)}, bf16[32,4224]{1,0:T(8,128)(2,1)S(1)}, u32[]{:S(2)}, u32[]{:S(2)}) collective-permute-start(bf16[32,4224]{1,0:T(8,128)(2,1)S(1)} %collective-permute-done.8.refs_2_), channel_id=1, source_target_pairs={{16,0},{0,16},{17,1},{1,17},{18,2},{2,18},{19,3},{3,19},{20,4},{4,... | collective-permute-start | bytes 811016 | tf_op jit(solution)/shard_map/ppermute | solution.py:72
  47.3 28.1 %copy-start = (bf16[1024,4096]{1,0:T(8,128)(2,1)}, bf16[1024,4096]{1,0:T(8,128)(2,1)S(1)}, u32[]{:S(2)}) copy-start(bf16[1024,4096]{1,0:T(8,128)(2,1)S(1)} %get-tuple-element.32.refs_3_.refs_5_.refs_7_) | copy-start | bytes 25165828
  75.4 5.8 %copy-start.4 = (bf16[128,1024]{1,0:T(8,128)(2,1)}, bf16[128,1024]{1,0:T(8,128)(2,1)S(1)}, u32[]{:S(2)}) copy-start(bf16[128,1024]{1,0:T(8,128)(2,1)S(1)} %get-tuple-element.53) | copy-start | bytes 786436
  75.4 5.8 %copy-start.6 = (bf16[128,1024]{1,0:T(8,128)(2,1)}, bf16[128,1024]{1,0:T(8,128)(2,1)S(1)}, u32[]{:S(2)}) copy-start(bf16[128,1024]{1,0:T(8,128)(2,1)S(1)} %get-tuple-element.52) | copy-start | bytes 786436
  81.2 23.9 %collective-permute-start.13 = (bf16[256,4096]{1,0:T(8,128)(2,1)}, bf16[256,4096]{1,0:T(8,128)(2,1)}, u32[]{:S(2)}, u32[]{:S(2)}) collective-permute-start(bf16[256,4096]{1,0:T(8,128)(2,1)} %shard_map.102), channel_id=1, source_target_pairs={{16,0},{0,16},{17,1},{1,17},{18,2},{2,18},{19,3},{3,19},{20,4},{4,... | collective-permute-start | bytes 6291464 | tf_op jit(solution)/shard_map/ppermute | solution.py:72
  84.9 10.3 %copy-start.7 = (bf16[128,1024]{1,0:T(8,128)(2,1)S(1)}, bf16[128,1024]{1,0:T(8,128)(2,1)}, u32[]{:S(2)}) copy-start(bf16[128,1024]{1,0:T(8,128)(2,1)} %copy-done.6) | copy-start | bytes 786436
  86.2 22.5 %collective-permute-start.21 = (bf16[128,1024]{1,0:T(8,128)(2,1)S(1)}, bf16[128,1024]{1,0:T(8,128)(2,1)S(1)}, u32[]{:S(2)}, u32[]{:S(2)}) collective-permute-start(bf16[128,1024]{1,0:T(8,128)(2,1)S(1)} %get-tuple-element.66), channel_id=1, source_target_pairs={{64,0},{128,64},{192,128},{0,192},{65,1},{129,65},{193,129},{1,193... | collective-permute-start | bytes 786440 | tf_op jit(solution)/shard_map/ppermute | solution.py:72
  91.9 17.4 %collective-permute-start.22 = (bf16[128,1024]{1,0:T(8,128)(2,1)S(1)}, bf16[128,1024]{1,0:T(8,128)(2,1)S(1)}, u32[]{:S(2)}, u32[]{:S(2)}) collective-permute-start(bf16[128,1024]{1,0:T(8,128)(2,1)S(1)} %get-tuple-element.65), channel_id=1, source_target_pairs={{128,0},{192,64},{0,128},{64,192},{129,1},{193,65},{1,129},{65,193... | collective-permute-start | bytes 786440 | tf_op jit(solution)/shard_map/ppermute | solution.py:72
  92.9 18.9 %collective-permute-start.23 = (bf16[128,1024]{1,0:T(8,128)(2,1)S(1)}, bf16[128,1024]{1,0:T(8,128)(2,1)S(1)}, u32[]{:S(2)}, u32[]{:S(2)}) collective-permute-start(bf16[128,1024]{1,0:T(8,128)(2,1)S(1)} %get-tuple-element.64), channel_id=1, source_target_pairs={{192,0},{0,64},{64,128},{128,192},{193,1},{1,65},{65,129},{129,193... | collective-permute-start | bytes 786440 | tf_op jit(solution)/shard_map/ppermute | solution.py:72
  95.2 35.9 %collective-permute-start.24 = (bf16[128,1024]{1,0:T(8,128)(2,1)S(1)}, bf16[128,1024]{1,0:T(8,128)(2,1)S(1)}, u32[]{:S(2)}, u32[]{:S(2)}) collective-permute-start(bf16[128,1024]{1,0:T(8,128)(2,1)S(1)} %copy-done.7), channel_id=1, source_target_pairs={{128,0},{192,64},{0,128},{64,192},{129,1},{193,65},{1,129},{65,193... | collective-permute-start | bytes 786440 | tf_op jit(solution)/shard_map/ppermute | solution.py:72
  97.3 3.4 %copy-start.1 = (bf16[1024,4096]{1,0:T(8,128)(2,1)S(1)}, bf16[1024,4096]{1,0:T(8,128)(2,1)}, u32[]{:S(2)}) copy-start(bf16[1024,4096]{1,0:T(8,128)(2,1)} %copy-done) | copy-start | bytes 25165828
  107.6 4.3 %copy-start.5 = (bf16[128,1024]{1,0:T(8,128)(2,1)S(1)}, bf16[128,1024]{1,0:T(8,128)(2,1)}, u32[]{:S(2)}) copy-start(bf16[128,1024]{1,0:T(8,128)(2,1)} %copy-done.4) | copy-start | bytes 786436
  107.6 34.7 %copy-start.2 = (f32[128,1024]{1,0:T(8,128)S(1)}, f32[128,1024]{1,0:T(8,128)}, u32[]{:S(2)}) copy-start(f32[128,1024]{1,0:T(8,128)} %outer.3) | copy-start | bytes 1572868
  107.6 34.7 %copy-start.3 = (f32[128,1024]{1,0:T(8,128)S(1)}, f32[128,1024]{1,0:T(8,128)}, u32[]{:S(2)}) copy-start(f32[128,1024]{1,0:T(8,128)} %momentum.3) | copy-start | bytes 1572868
  107.8 40.5 %collective-permute-start.14 = (bf16[64,4096]{1,0:T(8,128)(2,1)S(1)}, bf16[64,4096]{1,0:T(8,128)(2,1)S(1)}, u32[]{:S(2)}, u32[]{:S(2)}) collective-permute-start(bf16[64,4096]{1,0:T(8,128)(2,1)S(1)} %get-tuple-element.63), channel_id=1, source_target_pairs={{2,0},{3,1},{0,2},{1,3},{6,4},{7,5},{4,6},{5,7},{10,8},{11,9},{8,1... | collective-permute-start | bytes 1572872 | tf_op jit(solution)/shard_map/ppermute | solution.py:63
  108.8 39.5 %collective-permute-start.15 = (bf16[64,4096]{1,0:T(8,128)(2,1)S(1)}, bf16[64,4096]{1,0:T(8,128)(2,1)S(1)}, u32[]{:S(2)}, u32[]{:S(2)}) collective-permute-start(bf16[64,4096]{1,0:T(8,128)(2,1)S(1)} %get-tuple-element.62), channel_id=1, source_target_pairs={{3,0},{0,1},{1,2},{2,3},{7,4},{4,5},{5,6},{6,7},{11,8},{8,9},{9,10... | collective-permute-start | bytes 1572872 | tf_op jit(solution)/shard_map/ppermute | solution.py:63
  109.4 38.9 %collective-permute-start.16 = (bf16[64,4096]{1,0:T(8,128)(2,1)S(1)}, bf16[64,4096]{1,0:T(8,128)(2,1)S(1)}, u32[]{:S(2)}, u32[]{:S(2)}) collective-permute-start(bf16[64,4096]{1,0:T(8,128)(2,1)S(1)} %get-tuple-element.61), channel_id=1, source_target_pairs={{1,0},{2,1},{3,2},{0,3},{5,4},{6,5},{7,6},{4,7},{9,8},{10,9},{11,1... | collective-permute-start | bytes 1572872 | tf_op jit(solution)/shard_map/ppermute | solution.py:63
  111.9 30.4 %collective-permute-start.25 = (bf16[128,1024]{1,0:T(8,128)(2,1)S(1)}, bf16[128,1024]{1,0:T(8,128)(2,1)S(1)}, u32[]{:S(2)}, u32[]{:S(2)}) collective-permute-start(bf16[128,1024]{1,0:T(8,128)(2,1)S(1)} %copy-done.5), channel_id=1, source_target_pairs={{192,0},{0,64},{64,128},{128,192},{193,1},{1,65},{65,129},{129,193... | collective-permute-start | bytes 786440 | tf_op jit(solution)/shard_map/ppermute | solution.py:72
  131.1 11.2 %collective-permute-start.26 = (bf16[128,1024]{1,0:T(8,128)(2,1)S(1)}, bf16[128,1024]{1,0:T(8,128)(2,1)S(1)}, u32[]{:S(2)}, u32[]{:S(2)}) collective-permute-start(bf16[128,1024]{1,0:T(8,128)(2,1)S(1)} %get-tuple-element.54), channel_id=1, source_target_pairs={{64,0},{128,64},{192,128},{0,192},{65,1},{129,65},{193,129},{1,193... | collective-permute-start | bytes 786440 | tf_op jit(solution)/shard_map/ppermute | solution.py:72
  143.3 8.3 %collective-permute-start.27 = (bf16[64,1024]{1,0:T(8,128)(2,1)S(1)}, bf16[64,1024]{1,0:T(8,128)(2,1)S(1)}, u32[]{:S(2)}, u32[]{:S(2)}) collective-permute-start(bf16[64,1024]{1,0:T(8,128)(2,1)S(1)} %get-tuple-element.57.refs_0_), channel_id=1, source_target_pairs={{64,0},{128,64},{192,128},{0,192},{65,1},{129,65},{193,129},{1,193... | collective-permute-start | bytes 393224 | tf_op jit(solution)/shard_map/ppermute | solution.py:72
  148.1 7.9 %collective-permute-start.30 = (bf16[64,1024]{1,0:T(8,128)(2,1)S(1)}, bf16[64,1024]{1,0:T(8,128)(2,1)S(1)}, u32[]{:S(2)}, u32[]{:S(2)}) collective-permute-start(bf16[64,1024]{1,0:T(8,128)(2,1)S(1)} %get-tuple-element.58.refs_1_), channel_id=1, source_target_pairs={{192,0},{0,64},{64,128},{128,192},{193,1},{1,65},{65,129},{129,193... | collective-permute-start | bytes 393224 | tf_op jit(solution)/shard_map/ppermute | solution.py:72
  149.0 7.0 %collective-permute-start.19 = (bf16[16,4096]{1,0:T(8,128)(2,1)S(1)}, bf16[16,4096]{1,0:T(8,128)(2,1)S(1)}, u32[]{:S(2)}, u32[]{:S(2)}) collective-permute-start(bf16[16,4096]{1,0:T(8,128)(2,1)S(1)} %get-tuple-element.50), channel_id=1, source_target_pairs={{4,0},{5,1},{6,2},{7,3},{8,4},{9,5},{10,6},{11,7},{12,8},{13,9},{1... | collective-permute-start | bytes 393224 | tf_op jit(solution)/shard_map/ppermute | solution.py:67
  149.7 9.9 %collective-permute-start.18 = (bf16[16,4096]{1,0:T(8,128)(2,1)S(1)}, bf16[16,4096]{1,0:T(8,128)(2,1)S(1)}, u32[]{:S(2)}, u32[]{:S(2)}) collective-permute-start(bf16[16,4096]{1,0:T(8,128)(2,1)S(1)} %get-tuple-element.49), channel_id=1, source_target_pairs={{12,0},{13,1},{14,2},{15,3},{0,4},{1,5},{2,6},{3,7},{4,8},{5,9},{6... | collective-permute-start | bytes 393224 | tf_op jit(solution)/shard_map/ppermute | solution.py:67
  150.6 9.0 %collective-permute-start.17 = (bf16[16,4096]{1,0:T(8,128)(2,1)S(1)}, bf16[16,4096]{1,0:T(8,128)(2,1)S(1)}, u32[]{:S(2)}, u32[]{:S(2)}) collective-permute-start(bf16[16,4096]{1,0:T(8,128)(2,1)S(1)} %get-tuple-element.48), channel_id=1, source_target_pairs={{8,0},{9,1},{10,2},{11,3},{12,4},{13,5},{14,6},{15,7},{0,8},{1,9},... | collective-permute-start | bytes 393224 | tf_op jit(solution)/shard_map/ppermute | solution.py:67
  151.6 11.4 %collective-permute-start.28 = (bf16[64,1024]{1,0:T(8,128)(2,1)S(1)}, bf16[64,1024]{1,0:T(8,128)(2,1)S(1)}, u32[]{:S(2)}, u32[]{:S(2)}) collective-permute-start(bf16[64,1024]{1,0:T(8,128)(2,1)S(1)} %get-tuple-element.58.refs_1_), channel_id=1, source_target_pairs={{64,0},{128,64},{192,128},{0,192},{65,1},{129,65},{193,129},{1,193... | collective-permute-start | bytes 393224 | tf_op jit(solution)/shard_map/ppermute | solution.py:72
  156.0 7.0 %collective-permute-start.32 = (bf16[64,1024]{1,0:T(8,128)(2,1)S(1)}, bf16[64,1024]{1,0:T(8,128)(2,1)S(1)}, u32[]{:S(2)}, u32[]{:S(2)}) collective-permute-start(bf16[64,1024]{1,0:T(8,128)(2,1)S(1)} %get-tuple-element.57.refs_0_), channel_id=1, source_target_pairs={{192,0},{0,64},{64,128},{128,192},{193,1},{1,65},{65,129},{129,193... | collective-permute-start | bytes 393224 | tf_op jit(solution)/shard_map/ppermute | solution.py:72
  156.0 8.6 %collective-permute-start.29 = (bf16[64,1024]{1,0:T(8,128)(2,1)S(1)}, bf16[64,1024]{1,0:T(8,128)(2,1)S(1)}, u32[]{:S(2)}, u32[]{:S(2)}) collective-permute-start(bf16[64,1024]{1,0:T(8,128)(2,1)S(1)} %collective-permute-done.27.refs_2_), channel_id=1, source_target_pairs={{64,0},{128,64},{192,128},{0,192},{65,1},{129,65},{193,129},{1,193... | collective-permute-start | bytes 393224 | tf_op jit(solution)/shard_map/ppermute | solution.py:72
  159.6 12.1 %collective-permute-start.31 = (bf16[64,1024]{1,0:T(8,128)(2,1)S(1)}, bf16[64,1024]{1,0:T(8,128)(2,1)S(1)}, u32[]{:S(2)}, u32[]{:S(2)}) collective-permute-start(bf16[64,1024]{1,0:T(8,128)(2,1)S(1)} %collective-permute-done.30.refs_7_), channel_id=1, source_target_pairs={{192,0},{0,64},{64,128},{128,192},{193,1},{1,65},{65,129},{129,193... | collective-permute-start | bytes 393224 | tf_op jit(solution)/shard_map/ppermute | solution.py:72
  159.7 13.5 %collective-permute-start.20 = (bf16[8,4096]{1,0:T(8,128)(2,1)S(1)}, bf16[8,4096]{1,0:T(8,128)(2,1)S(1)}, u32[]{:S(2)}, u32[]{:S(2)}) collective-permute-start(bf16[8,4096]{1,0:T(8,128)(2,1)S(1)} %slice.58), channel_id=1, source_target_pairs={{32,0},{0,32},{33,1},{1,33},{34,2},{2,34},{35,3},{3,35},{36,4},{4,... | collective-permute-start | bytes 196616 | tf_op jit(solution)/shard_map/ppermute | solution.py:72

commit v3 on v2

--- a/solution.py
+++ b/solution.py
@@ -34,7 +34,7 @@
     return pl.pallas_call(
         kernel,
         in_specs=[SMEM] + [specs.get(k, VMEM) for k in range(1, len(operands))],
-        out_specs=jax.tree.map(lambda _: out_spec, out),
+        out_specs=out_spec if isinstance(out_spec, list) else jax.tree.map(lambda _: out_spec, out),
         out_shape=out,
         scratch_shapes=scratch,
         compiler_params=pltpu.CompilerParams(vmem_limit_bytes=limit << 20),
@@ -318,7 +318,7 @@
 
 
 def place_kernel(part, here, *refs):
-    pieces, out, sems = refs[:8], refs[8], refs[9]
+    pieces, (pair, sent, out, token_grad, sems) = refs[:8], refs[8:]
     half = pieces[0].shape[0]
     copies = []
     for k, piece in enumerate(pieces):
@@ -327,6 +327,7 @@
         copies.append(pltpu.make_async_copy(piece, to, sems.at[k]))
     for one in copies:
         one.start()
+    token_grad[...] = pair[: sent.shape[0], :] + to_f32(sent[...])
     for one in copies:
         one.wait()
 
@@ -440,11 +441,6 @@
     rounded = call(outer_kernel, [shaped(BF16, slab_rows // 2, part)] * 2, *operands)
     new_outer, new_momentum = call(outer_kernel, [shaped(F32, slab_rows, part)] * 2, *operands)
     pieces = ring_gather(*rounded, along("rep"))
-    next_inner = call(
-        functools.partial(place_kernel, part), shaped(BF16, slab_rows, width), here, *pieces,
-        scratch=[pltpu.SemaphoreType.DMA((8,))], out_spec=pl.BlockSpec(memory_space=pltpu.HBM),
-    )
-
     got = take(send, CORE, 1)
     total = (to_f32(keep) + to_f32(got)).reshape(4, 8 * own, width)
     rounded = total.astype(BF16)
@@ -458,7 +454,14 @@
         got = take_inner(others[k - 1], -k)
         pair = pair + to_f32(got)
     pair_sent = take(pair[own:].astype(BF16), Z, 1)
-    token_grad = (pair[:own] + to_f32(pair_sent))[None]
+    next_inner, token_grad = call(
+        functools.partial(place_kernel, part),
+        [shaped(BF16, slab_rows, width), shaped(F32, own, width)],
+        here, *pieces, pair, pair_sent,
+        scratch=[pltpu.SemaphoreType.DMA((8,))],
+        out_spec=[pl.BlockSpec(memory_space=pltpu.HBM), VMEM],
+    )
+    token_grad = token_grad[None]
     return (token_loss, token_grad, new_outer, new_momentum, next_inner)
 
 

time: 174 us -> 172 us (0.989)
  the two profiles are of different devices: /device:TPU:1 before, /device:TPU:32 now
where the time goes in v3:
time: 172 us; the launch traced here: 170 us
  starting transfers between devices  59.2 us (34%)
  waiting for transfers between devices  42.7 us (25%)
  Pallas kernels  38.1 us (22%)
  blocking collectives  17.1 us (10%)
  local copies, waits for them, and re-layouts  7.46 us (4%)
  other arithmetic  3.94 us (2%)
    pallas_call x15, Pallas kernels, call(): pl.pallas_call(kernel, in_specs=[SMEM] + [specs.get(k, VMEM) for k in ran...  38.1 us
    ppermute x20, starting transfers between devices, take(): return lax.ppermute(value, axis, [((i + k) % n, i) for i in range(n)])  37.9 us
    ppermute x20, waiting for transfers between devices, take(): return lax.ppermute(value, axis, [((i + k) % n, i) for i in range(n)])  25.6 us
    ppermute x7, waiting for transfers between devices, take_outer(): return lax.ppermute(value, (CORE, X, Y), by_core(k, False))  13.5 us
    all_to_all x1, blocking collectives, per_device(): stats = lax.all_to_all(stats, VOC, 0, 0, tiled=True)  11.8 us
    ppermute x7, starting transfers between devices, take_outer(): return lax.ppermute(value, (CORE, X, Y), by_core(k, False))  11 us
    ppermute x6, starting transfers between devices, take_inner(): return lax.ppermute(value, (CORE, X, Y), by_core(k, True))  10.3 us
    all_gather x1, blocking collectives, per_device(): stats = lax.all_gather(stats, TOK)  5.24 us
  transfers between devices with their start and end apart: 33, of which 15 were waited for; matrix products, arithmetic and copies ran while one was open for 4% of the time, Pallas kernels for 12%

profile of v3, /device:TPU:32, one launch (start us, length us, event | category | flops | bytes accessed | tf_op | source)
XLA Modules:
  0.0 169.7 jit_solution(13145866365342199293)
XLA Ops:
  0.6 0.7 convert_bitcast_fusion.1
  1.3 0.1 copy.12
  1.4 0.8 fusion.1.refs_0_
  2.2 1.8 %collective-permute-start = (bf16[8,4224]{1,0:T(8,128)(2,1)S(1)}, bf16[8,4224]{1,0:T(8,128)(2,1)S(1)}, u32[]{:S(2)}, u32[]{:S(2)}) collective-permute-start(bf16[8,4224]{1,0:T(8,128)(2,1)S(1)} %fusion.1.refs_0_), channel_id=1, source_target_pairs={{32,0},{0,32},{33,1},{1,33},{34,2},{2,34},{35,3},{3,35},{36,4},{4,... | collective-permute-start | bytes 202760 | tf_op jit(solution)/shard_map/ppermute | solution.py:72
  4.1 2.4 %collective-permute-done.refs_1_ = bf16[8,4224]{1,0:T(8,128)(2,1)S(1)} collective-permute-done((bf16[8,4224]{1,0:T(8,128)(2,1)S(1)}, bf16[8,4224]{1,0:T(8,128)(2,1)S(1)}, u32[]{:S(2)}, u32[]{:S(2)}) %collective-permute-start) | collective-permute-done | bytes 67616 | tf_op jit(solution)/shard_map/ppermute | solution.py:72
  6.5 0.5 shard_map.92.refs_0_
  7.1 1.6 collective-permute-start.3
  8.7 2.7 %collective-permute-start.2 = (bf16[16,4224]{1,0:T(8,128)(2,1)S(1)}, bf16[16,4224]{1,0:T(8,128)(2,1)S(1)}, u32[]{:S(2)}, u32[]{:S(2)}) collective-permute-start(bf16[16,4224]{1,0:T(8,128)(2,1)S(1)} %shard_map.92.refs_0_), channel_id=1, source_target_pairs={{8,0},{9,1},{10,2},{11,3},{12,4},{13,5},{14,6},{15,7},{0,8},{1,9},... | collective-permute-start | bytes 405512 | tf_op jit(solution)/shard_map/ppermute | solution.py:67
  11.4 1.4 collective-permute-start.1
  12.8 0.6 collective-permute-done.3.refs_3_
  13.4 2.4 %collective-permute-done.2.refs_2_ = bf16[16,4224]{1,0:T(8,128)(2,1)S(1)} collective-permute-done((bf16[16,4224]{1,0:T(8,128)(2,1)S(1)}, bf16[16,4224]{1,0:T(8,128)(2,1)S(1)}, u32[]{:S(2)}, u32[]{:S(2)}) %collective-permute-start.2) | collective-permute-done | bytes 135200 | tf_op jit(solution)/shard_map/ppermute | solution.py:67
  15.8 0.6 collective-permute-done.1.refs_1_
  16.4 0.6 shard_map.93.refs_0_
  17.0 3.1 %collective-permute-start.6 = (bf16[64,4224]{1,0:T(8,128)(2,1)S(1)}, bf16[64,4224]{1,0:T(8,128)(2,1)S(1)}, u32[]{:S(2)}, u32[]{:S(2)}) collective-permute-start(bf16[64,4224]{1,0:T(8,128)(2,1)S(1)} %shard_map.93.refs_0_), channel_id=1, source_target_pairs={{1,0},{2,1},{3,2},{0,3},{5,4},{6,5},{7,6},{4,7},{9,8},{10,9},{11,1... | collective-permute-start | bytes 1622024 | tf_op jit(solution)/shard_map/ppermute | solution.py:63
  20.1 6.9 %collective-permute-done.6.refs_0_ = bf16[64,4224]{1,0:T(8,128)(2,1)S(1)} collective-permute-done((bf16[64,4224]{1,0:T(8,128)(2,1)S(1)}, bf16[64,4224]{1,0:T(8,128)(2,1)S(1)}, u32[]{:S(2)}, u32[]{:S(2)}) %collective-permute-start.6) | collective-permute-done | bytes 540704 | tf_op jit(solution)/shard_map/ppermute | solution.py:63
  27.0 3.8 %collective-permute-start.7 = (bf16[32,4224]{1,0:T(8,128)(2,1)S(1)}, bf16[32,4224]{1,0:T(8,128)(2,1)S(1)}, u32[]{:S(2)}, u32[]{:S(2)}) collective-permute-start(bf16[32,4224]{1,0:T(8,128)(2,1)S(1)} %slice.42), channel_id=1, source_target_pairs={{1,0},{2,1},{3,2},{0,3},{5,4},{6,5},{7,6},{4,7},{9,8},{10,9},{11,1... | collective-permute-start | bytes 811016 | tf_op jit(solution)/shard_map/ppermute | solution.py:63
  31.0 1.0 shard_map.96.refs_8_.refs_10_
  31.9 2.8 %collective-permute-done.7.refs_1_ = bf16[32,4224]{1,0:T(8,128)(2,1)S(1)} collective-permute-done((bf16[32,4224]{1,0:T(8,128)(2,1)S(1)}, bf16[32,4224]{1,0:T(8,128)(2,1)S(1)}, u32[]{:S(2)}, u32[]{:S(2)}) %collective-permute-start.7) | collective-permute-done | bytes 270368 | tf_op jit(solution)/shard_map/ppermute | solution.py:63
  34.7 3.8 %collective-permute-done.8.refs_2_ = bf16[32,4224]{1,0:T(8,128)(2,1)S(1)} collective-permute-done((bf16[32,4224]{1,0:T(8,128)(2,1)S(1)}, bf16[32,4224]{1,0:T(8,128)(2,1)S(1)}, u32[]{:S(2)}, u32[]{:S(2)}) %collective-permute-start.8) | collective-permute-done | bytes 270368 | tf_op jit(solution)/shard_map/ppermute | solution.py:63
  38.5 5.8 %shard_map.94 = (f32[128,1024]{1,0:T(8,128)S(1)}, s32[128,1]{1,0:T(8,128)S(1)}, bf16[128,4096]{1,0:T(8,128)(2,1)S(1)}, f32[128,128]{1,0:T(8,128)S(1)}, bf16[1024,4096]{1,0:T(8,128)(2,1)S(1)}) custom-call(s32[6]{0:T(128)S(1)} %stack.33.here, bf16[64,4224]{1,0:T(8,128)(2,1)S(1)} %shard_map.93.refs_0_, bf16[64,4224]{1,0:T(8,128)(2,1)S(1)} %collective-permute-done.11.refs_1_, ...), custom_call_target="tpu_custom_call" | custom-call | flops 2147483648 | bytes 19497496 | tf_op jit(solution)/shard_map/pallas_call | solution.py:34
  44.4 4.5 %shard_map.95 = (f32[192,1024]{1,0:T(8,128)S(1)}, s32[192,1]{1,0:T(8,128)S(1)}, bf16[192,4096]{1,0:T(8,128)(2,1)S(1)}, f32[192,128]{1,0:T(8,128)S(1)}) custom-call(s32[6]{0:T(128)S(1)} %stack.33.here, bf16[64,4224]{1,0:T(8,128)(2,1)S(1)} %collective-permute-done.6.refs_0_, bf16[64,4224]{1,0:T(8,128)(2,1)S(1)} %collective-permute-done.4.refs_1_, ...), custom_call_target="tpu_custom_call" | custom-call | flops 2147483648 | bytes 12534552 | tf_op jit(solution)/shard_map/pallas_call | solution.py:34
  48.9 4.8 %shard_map.97 = (f32[192,1024]{1,0:T(8,128)S(1)}, s32[192,1]{1,0:T(8,128)S(1)}, bf16[192,4096]{1,0:T(8,128)(2,1)S(1)}, f32[8,512]{1,0:T(8,128)S(1)}) custom-call(s32[6]{0:T(128)S(1)} %stack.33.here, bf16[64,4224]{1,0:T(8,128)(2,1)S(1)} %collective-permute-done.5.refs_0_, bf16[32,4224]{1,0:T(8,128)(2,1)S(1)} %collective-permute-done.7.refs_1_, ...), custom_call_target="tpu_custom_call" | custom-call | flops 2147483648 | bytes 13075224 | tf_op jit(solution)/shard_map/pallas_call | solution.py:34
  53.7 5.2 %all-gather = f32[32,512]{1,0:T(8,128)S(1)} all-gather(f32[8,512]{1,0:T(8,128)S(1)} %get-tuple-element.37), channel_id=2, replica_groups=mesh['rep'=4,'tok_0'=2,'tok_1'=2,'voc_0'=4,'voc_1'=4] {'tok_0','tok_1'}, dimensions={0}, use_global_device_ids=true | all-gather | bytes 81920 | tf_op jit(solution)/shard_map/all_gather | solution.py:410
  58.9 0.6 shard_map.98
  59.5 11.8 %all_to_all.5.refs_0_ = f32[16,4,512]{2,1,0:T(4,128)S(1)} all-to-all(f32[16,4,512]{2,1,0:T(4,128)S(1)} %shard_map.98), channel_id=1, replica_groups=mesh['rep'=4,'tok_0'=2,'tok_1'=2,'voc_0'=4,'voc_1'=4] {'voc_0','voc_1'}, dimensions={0} | all-to-all | bytes 262144 | tf_op jit(solution)/shard_map/all_to_all | solution.py:412
  71.4 3.1 %shard_map.99 = (f32[8,1]{1,0:T(8,128)S(1)}, f32[512,1]{1,0:T(8,128)S(1)}, f32[128,1024]{1,0:T(8,128)S(1)}, bf16[128,1024]{1,0:T(8,128)(2,1)S(1)}, bf16[128,1024...) custom-call(s32[6]{0:T(128)S(1)} %stack.33.here, f32[16,4,512]{2,1,0:T(4,128)S(1)} %all_to_all.5.refs_0_, ...), custom_call_target="tpu_custom_call" | custom-call | flops 536870912 | bytes 8261688 | tf_op jit(solution)/shard_map/pallas_call | solution.py:34
  74.5 5.8 %shard_map.103 = bf16[256,4096]{1,0:T(8,128)(2,1)} custom-call(s32[6]{0:T(128)S(1)} %stack.33.here, f32[128,1024]{1,0:T(8,128)S(1)} %get-tuple-element.38.refs_1_.refs_0_, f32[192,1024]{1,0:T(8,128)S(1)} %get-tuple-element.39.refs_2_.refs_1_, f32[192,1024]{1,0:T(8,128)S(1)} %get-tuple-element.40.refs_3_.refs_2_, ...), custom_call_target="tpu_custom_call" | custom-call | flops 2147483648 | bytes 12587032 | tf_op jit(solution)/shard_map/pallas_call | solution.py:34
  80.4 2.3 %slice.36 = bf16[1,128,4096]{2,1,0:T(8,128)(2,1)} slice(bf16[1,1024,4096]{2,1,0:T(8,128)(2,1)} %param.7), slice={[0:1], [0:128], [0:4096]} | slice | bytes 2097152 | tf_op jit(solution)/shard_map/slice | solution.py:377
  82.7 1.3 dynamic-slice_bitcast_fusion
  84.0 3.3 %collective-permute-start.15 = (bf16[128,1024]{1,0:T(8,128)(2,1)S(1)}, bf16[128,1024]{1,0:T(8,128)(2,1)S(1)}, u32[]{:S(2)}, u32[]{:S(2)}) collective-permute-start(bf16[128,1024]{1,0:T(8,128)(2,1)S(1)} %get-tuple-element.68), channel_id=1, source_target_pairs={{192,0},{0,64},{64,128},{128,192},{193,1},{1,65},{65,129},{129,193... | collective-permute-start | bytes 786440 | tf_op jit(solution)/shard_map/ppermute | solution.py:72
  87.4 4.5 %collective-permute-start.14 = (bf16[128,1024]{1,0:T(8,128)(2,1)S(1)}, bf16[128,1024]{1,0:T(8,128)(2,1)S(1)}, u32[]{:S(2)}, u32[]{:S(2)}) collective-permute-start(bf16[128,1024]{1,0:T(8,128)(2,1)S(1)} %get-tuple-element.69), channel_id=1, source_target_pairs={{128,0},{192,64},{0,128},{64,192},{129,1},{193,65},{1,129},{65,193... | collective-permute-start | bytes 786440 | tf_op jit(solution)/shard_map/ppermute | solution.py:72
  91.9 2.7 %collective-permute-start.13 = (bf16[128,1024]{1,0:T(8,128)(2,1)S(1)}, bf16[128,1024]{1,0:T(8,128)(2,1)S(1)}, u32[]{:S(2)}, u32[]{:S(2)}) collective-permute-start(bf16[128,1024]{1,0:T(8,128)(2,1)S(1)} %get-tuple-element.70), channel_id=1, source_target_pairs={{64,0},{128,64},{192,128},{0,192},{65,1},{129,65},{193,129},{1,193... | collective-permute-start | bytes 786440 | tf_op jit(solution)/shard_map/ppermute | solution.py:72
  94.5 1.0 collective-permute-start.16
  95.5 3.4 %copy-done.1 = bf16[1024,4096]{1,0:T(8,128)(2,1)S(1)} copy-done((bf16[1024,4096]{1,0:T(8,128)(2,1)S(1)}, bf16[1024,4096]{1,0:T(8,128)(2,1)}, u32[]{:S(2)}) %copy-start.1) | copy-done | bytes 8388632
  98.9 4.5 %shard_map.102 = bf16[256,4096]{1,0:T(8,128)(2,1)S(1)} custom-call(s32[6]{0:T(128)S(1)} %stack.33.here, f32[128,1024]{1,0:T(8,128)S(1)} %get-tuple-element.38.refs_1_.refs_0_, f32[192,1024]{1,0:T(8,128)S(1)} %get-tuple-element.39.refs_2_.refs_1_, f32[192,1024]{1,0:T(8,128)S(1)} %get-tuple-element.40.refs_3_.refs_2_, ...), custom_call_target="tpu_custom_call" | custom-call | flops 2147483648 | bytes 12587032 | tf_op jit(solution)/shard_map/pallas_call | solution.py:34
  103.4 2.4 %fusion.2 = (bf16[256,4096]{1,0:T(8,128)(2,1)S(1)}, f32[256,4096]{1,0:T(8,128)S(1)}) fusion(bf16[256,4096]{1,0:T(8,128)(2,1)} %collective-permute-done.25, bf16[256,4096]{1,0:T(8,128)(2,1)S(1)} %shard_map.102), kind=kLoop, calls=%fused_computation.13 | loop fusion | flops 4194304 | bytes 10485760 | tf_op jit(solution)/shard_map/convert_element_type | solution.py:446
  105.8 0.1 fusion.3
  106.0 1.3 collective-permute-start.28
  107.3 2.8 %collective-permute-done.15.w3 = bf16[128,1024]{1,0:T(8,128)(2,1)S(1)} collective-permute-done((bf16[128,1024]{1,0:T(8,128)(2,1)S(1)}, bf16[128,1024]{1,0:T(8,128)(2,1)S(1)}, u32[]{:S(2)}, u32[]{:S(2)}) %collective-permute-start.15) | collective-permute-done | bytes 262176 | tf_op jit(solution)/shard_map/ppermute | solution.py:72
  110.2 0.4 collective-permute-start.27
  110.6 2.3 %collective-permute-start.26 = (bf16[64,4096]{1,0:T(8,128)(2,1)S(1)}, bf16[64,4096]{1,0:T(8,128)(2,1)S(1)}, u32[]{:S(2)}, u32[]{:S(2)}) collective-permute-start(bf16[64,4096]{1,0:T(8,128)(2,1)S(1)} %get-tuple-element.67), channel_id=1, source_target_pairs={{2,0},{3,1},{0,2},{1,3},{6,4},{7,5},{4,6},{5,7},{10,8},{11,9},{8,1... | collective-permute-start | bytes 1572872 | tf_op jit(solution)/shard_map/ppermute | solution.py:63
  112.8 2.3 %collective-permute-start.17 = (bf16[128,1024]{1,0:T(8,128)(2,1)S(1)}, bf16[128,1024]{1,0:T(8,128)(2,1)S(1)}, u32[]{:S(2)}, u32[]{:S(2)}) collective-permute-start(bf16[128,1024]{1,0:T(8,128)(2,1)S(1)} %copy-done.5), channel_id=1, source_target_pairs={{192,0},{0,64},{64,128},{128,192},{193,1},{1,65},{65,129},{129,193... | collective-permute-start | bytes 786440 | tf_op jit(solution)/shard_map/ppermute | solution.py:72
  115.1 6.5 %collective-permute-done.16.g1 = bf16[128,1024]{1,0:T(8,128)(2,1)S(1)} collective-permute-done((bf16[128,1024]{1,0:T(8,128)(2,1)S(1)}, bf16[128,1024]{1,0:T(8,128)(2,1)S(1)}, u32[]{:S(2)}, u32[]{:S(2)}) %collective-permute-start.16) | collective-permute-done | bytes 262176 | tf_op jit(solution)/shard_map/ppermute | solution.py:72
  121.6 8.7 %collective-permute-start.18 = (bf16[128,1024]{1,0:T(8,128)(2,1)S(1)}, bf16[128,1024]{1,0:T(8,128)(2,1)S(1)}, u32[]{:S(2)}, u32[]{:S(2)}) collective-permute-start(bf16[128,1024]{1,0:T(8,128)(2,1)S(1)} %get-tuple-element.51), channel_id=1, source_target_pairs={{64,0},{128,64},{192,128},{0,192},{65,1},{129,65},{193,129},{1,193... | collective-permute-start | bytes 786440 | tf_op jit(solution)/shard_map/ppermute | solution.py:72
  130.3 0.5 collective-permute-done.17.g2
  130.8 10.8 %collective-permute-done.18.g3 = bf16[128,1024]{1,0:T(8,128)(2,1)S(1)} collective-permute-done((bf16[128,1024]{1,0:T(8,128)(2,1)S(1)}, bf16[128,1024]{1,0:T(8,128)(2,1)S(1)}, u32[]{:S(2)}, u32[]{:S(2)}) %collective-permute-start.18) | collective-permute-done | bytes 262176 | tf_op jit(solution)/shard_map/ppermute | solution.py:72
  141.5 1.0 shard_map.101
  142.5 4.7 %collective-permute-start.19 = (bf16[64,1024]{1,0:T(8,128)(2,1)S(1)}, bf16[64,1024]{1,0:T(8,128)(2,1)S(1)}, u32[]{:S(2)}, u32[]{:S(2)}) collective-permute-start(bf16[64,1024]{1,0:T(8,128)(2,1)S(1)} %get-tuple-element.52.refs_0_), channel_id=1, source_target_pairs={{64,0},{128,64},{192,128},{0,192},{65,1},{129,65},{193,129},{1,193... | collective-permute-start | bytes 393224 | tf_op jit(solution)/shard_map/ppermute | solution.py:72
  147.3 0.8 shard_map.104
  148.1 1.3 collective-permute-start.29
  149.5 0.8 collective-permute-start.30
  150.2 2.5 %collective-permute-start.31 = (bf16[16,4096]{1,0:T(8,128)(2,1)S(1)}, bf16[16,4096]{1,0:T(8,128)(2,1)S(1)}, u32[]{:S(2)}, u32[]{:S(2)}) collective-permute-start(bf16[16,4096]{1,0:T(8,128)(2,1)S(1)} %get-tuple-element.58), channel_id=1, source_target_pairs={{4,0},{5,1},{6,2},{7,3},{8,4},{9,5},{10,6},{11,7},{12,8},{13,9},{1... | collective-permute-start | bytes 393224 | tf_op jit(solution)/shard_map/ppermute | solution.py:67
  152.7 0.8 collective-permute-done.19.refs_2_
  153.5 3.1 %collective-permute-start.24 = (bf16[64,1024]{1,0:T(8,128)(2,1)S(1)}, bf16[64,1024]{1,0:T(8,128)(2,1)S(1)}, u32[]{:S(2)}, u32[]{:S(2)}) collective-permute-start(bf16[64,1024]{1,0:T(8,128)(2,1)S(1)} %get-tuple-element.52.refs_0_), channel_id=1, source_target_pairs={{192,0},{0,64},{64,128},{128,192},{193,1},{1,65},{65,129},{129,193... | collective-permute-start | bytes 393224 | tf_op jit(solution)/shard_map/ppermute | solution.py:72
  156.5 1.1 collective-permute-start.20
  157.6 2.1 %collective-permute-start.21 = (bf16[64,1024]{1,0:T(8,128)(2,1)S(1)}, bf16[64,1024]{1,0:T(8,128)(2,1)S(1)}, u32[]{:S(2)}, u32[]{:S(2)}) collective-permute-start(bf16[64,1024]{1,0:T(8,128)(2,1)S(1)} %collective-permute-done.19.refs_2_), channel_id=1, source_target_pairs={{64,0},{128,64},{192,128},{0,192},{65,1},{129,65},{193,129},{1,193... | collective-permute-start | bytes 393224 | tf_op jit(solution)/shard_map/ppermute | solution.py:72
  159.7 0.8 collective-permute-start.23
  160.6 1.7 %collective-permute-start.32 = (bf16[8,4096]{1,0:T(8,128)(2,1)S(1)}, bf16[8,4096]{1,0:T(8,128)(2,1)S(1)}, u32[]{:S(2)}, u32[]{:S(2)}) collective-permute-start(bf16[8,4096]{1,0:T(8,128)(2,1)S(1)} %slice.50), channel_id=1, source_target_pairs={{32,0},{0,32},{33,1},{1,33},{34,2},{2,34},{35,3},{3,35},{36,4},{4,... | collective-permute-start | bytes 196616 | tf_op jit(solution)/shard_map/ppermute | solution.py:72
  162.3 1.1 shard_map.100
  163.5 1.9 %shard_map.106 = (f32[128,1024]{1,0:T(8,128)}, f32[128,1024]{1,0:T(8,128)}) custom-call(s32[6]{0:T(128)S(1)} %stack.33.here, f32[128,1024]{1,0:T(8,128)S(1)} %copy-done.2, f32[128,1024]{1,0:T(8,128)S(1)} %copy-done.3, bf16[128,1024]{1,0:T(8,128)(2,1)S(1)} %get-tuple-element.71.w0, bf16[128,1024]{1,0:T(8,128)(2,1)S(1)} %collective-permute-done.13.w1, ...), custom_call_target="tpu_custom_call" | custom-call | flops 4456472 | bytes 4456472 | tf_op jit(solution)/shard_map/pallas_call | solution.py:34
  165.4 0.1 collective-permute-done.21.refs_4_
  165.5 1.4 collective-permute-done.23.refs_5_
  166.9 0.3 collective-permute-done.32.refs_9_
  167.3 2.2 %shard_map.105 = (bf16[128,4096]{1,0:T(8,128)(2,1)}, f32[8,4096]{1,0:T(8,128)}) custom-call(s32[6]{0:T(128)S(1)} %stack.33.here, bf16[64,1024]{1,0:T(8,128)(2,1)S(1)} %get-tuple-element.52.refs_0_, bf16[64,1024]{1,0:T(8,128)(2,1)S(1)} %get-tuple-element.53.refs_1_, bf16[64,1024]{1,0:T(8,128)(2,1)S(1)} %collective-permute-done.19.refs_2_, ...), custom_call_target="tpu_custom_call" | custom-call | flops 2555928 | bytes 2555928 | tf_op jit(solution)/shard_map/pallas_call | solution.py:34
  (49 shorter events, 0.6 us)
Async XLA Ops:
  2.2 4.3 %collective-permute-start = (bf16[8,4224]{1,0:T(8,128)(2,1)S(1)}, bf16[8,4224]{1,0:T(8,128)(2,1)S(1)}, u32[]{:S(2)}, u32[]{:S(2)}) collective-permute-start(bf16[8,4224]{1,0:T(8,128)(2,1)S(1)} %fusion.1.refs_0_), channel_id=1, source_target_pairs={{32,0},{0,32},{33,1},{1,33},{34,2},{2,34},{35,3},{3,35},{36,4},{4,... | collective-permute-start | bytes 202760 | tf_op jit(solution)/shard_map/ppermute | solution.py:72
  7.1 6.3 %collective-permute-start.3 = (bf16[16,4224]{1,0:T(8,128)(2,1)S(1)}, bf16[16,4224]{1,0:T(8,128)(2,1)S(1)}, u32[]{:S(2)}, u32[]{:S(2)}) collective-permute-start(bf16[16,4224]{1,0:T(8,128)(2,1)S(1)} %shard_map.92.refs_0_), channel_id=1, source_target_pairs={{12,0},{13,1},{14,2},{15,3},{0,4},{1,5},{2,6},{3,7},{4,8},{5,9},{6... | collective-permute-start | bytes 405512 | tf_op jit(solution)/shard_map/ppermute | solution.py:67
  8.7 7.2 %collective-permute-start.2 = (bf16[16,4224]{1,0:T(8,128)(2,1)S(1)}, bf16[16,4224]{1,0:T(8,128)(2,1)S(1)}, u32[]{:S(2)}, u32[]{:S(2)}) collective-permute-start(bf16[16,4224]{1,0:T(8,128)(2,1)S(1)} %shard_map.92.refs_0_), channel_id=1, source_target_pairs={{8,0},{9,1},{10,2},{11,3},{12,4},{13,5},{14,6},{15,7},{0,8},{1,9},... | collective-permute-start | bytes 405512 | tf_op jit(solution)/shard_map/ppermute | solution.py:67
  11.4 5.0 %collective-permute-start.1 = (bf16[16,4224]{1,0:T(8,128)(2,1)S(1)}, bf16[16,4224]{1,0:T(8,128)(2,1)S(1)}, u32[]{:S(2)}, u32[]{:S(2)}) collective-permute-start(bf16[16,4224]{1,0:T(8,128)(2,1)S(1)} %shard_map.92.refs_0_), channel_id=1, source_target_pairs={{4,0},{5,1},{6,2},{7,3},{8,4},{9,5},{10,6},{11,7},{12,8},{13,9},{1... | collective-permute-start | bytes 405512 | tf_op jit(solution)/shard_map/ppermute | solution.py:67
  17.0 10.0 %collective-permute-start.6 = (bf16[64,4224]{1,0:T(8,128)(2,1)S(1)}, bf16[64,4224]{1,0:T(8,128)(2,1)S(1)}, u32[]{:S(2)}, u32[]{:S(2)}) collective-permute-start(bf16[64,4224]{1,0:T(8,128)(2,1)S(1)} %shard_map.93.refs_0_), channel_id=1, source_target_pairs={{1,0},{2,1},{3,2},{0,3},{5,4},{6,5},{7,6},{4,7},{9,8},{10,9},{11,1... | collective-permute-start | bytes 1622024 | tf_op jit(solution)/shard_map/ppermute | solution.py:63
  20.1 10.7 %collective-permute-start.4 = (bf16[64,4224]{1,0:T(8,128)(2,1)S(1)}, bf16[64,4224]{1,0:T(8,128)(2,1)S(1)}, u32[]{:S(2)}, u32[]{:S(2)}) collective-permute-start(bf16[64,4224]{1,0:T(8,128)(2,1)S(1)} %shard_map.93.refs_0_), channel_id=1, source_target_pairs={{3,0},{0,1},{1,2},{2,3},{7,4},{4,5},{5,6},{6,7},{11,8},{8,9},{9,10... | collective-permute-start | bytes 1622024 | tf_op jit(solution)/shard_map/ppermute | solution.py:63
  20.1 18.4 %collective-permute-start.11 = (bf16[64,4224]{1,0:T(8,128)(2,1)S(1)}, bf16[64,4224]{1,0:T(8,128)(2,1)S(1)}, u32[]{:S(2)}, u32[]{:S(2)}) collective-permute-start(bf16[64,4224]{1,0:T(8,128)(2,1)S(1)} %shard_map.93.refs_0_), channel_id=1, source_target_pairs={{16,0},{0,16},{17,1},{1,17},{18,2},{2,18},{19,3},{3,19},{20,4},{4,... | collective-permute-start | bytes 1622024 | tf_op jit(solution)/shard_map/ppermute | solution.py:72
  27.0 17.4 %collective-permute-start.12 = (bf16[64,4224]{1,0:T(8,128)(2,1)S(1)}, bf16[64,4224]{1,0:T(8,128)(2,1)S(1)}, u32[]{:S(2)}, u32[]{:S(2)}) collective-permute-start(bf16[64,4224]{1,0:T(8,128)(2,1)S(1)} %collective-permute-done.6.refs_0_), channel_id=1, source_target_pairs={{16,0},{0,16},{17,1},{1,17},{18,2},{2,18},{19,3},{3,19},{20,4},{4,... | collective-permute-start | bytes 1622024 | tf_op jit(solution)/shard_map/ppermute | solution.py:72
  27.0 7.7 %collective-permute-start.7 = (bf16[32,4224]{1,0:T(8,128)(2,1)S(1)}, bf16[32,4224]{1,0:T(8,128)(2,1)S(1)}, u32[]{:S(2)}, u32[]{:S(2)}) collective-permute-start(bf16[32,4224]{1,0:T(8,128)(2,1)S(1)} %slice.42), channel_id=1, source_target_pairs={{1,0},{2,1},{3,2},{0,3},{5,4},{6,5},{7,6},{4,7},{9,8},{10,9},{11,1... | collective-permute-start | bytes 811016 | tf_op jit(solution)/shard_map/ppermute | solution.py:63
  30.8 7.7 %collective-permute-start.8 = (bf16[32,4224]{1,0:T(8,128)(2,1)S(1)}, bf16[32,4224]{1,0:T(8,128)(2,1)S(1)}, u32[]{:S(2)}, u32[]{:S(2)}) collective-permute-start(bf16[32,4224]{1,0:T(8,128)(2,1)S(1)} %slice.43), channel_id=1, source_target_pairs={{3,0},{0,1},{1,2},{2,3},{7,4},{4,5},{5,6},{6,7},{11,8},{8,9},{9,10... | collective-permute-start | bytes 811016 | tf_op jit(solution)/shard_map/ppermute | solution.py:63
  30.9 18.0 %collective-permute-start.5 = (bf16[64,4224]{1,0:T(8,128)(2,1)S(1)}, bf16[64,4224]{1,0:T(8,128)(2,1)S(1)}, u32[]{:S(2)}, u32[]{:S(2)}) collective-permute-start(bf16[64,4224]{1,0:T(8,128)(2,1)S(1)} %collective-permute-done.4.refs_1_), channel_id=1, source_target_pairs={{16,0},{0,16},{17,1},{1,17},{18,2},{2,18},{19,3},{3,19},{20,4},{4,... | collective-permute-start | bytes 1622024 | tf_op jit(solution)/shard_map/ppermute | solution.py:72
  34.7 14.1 %collective-permute-start.9 = (bf16[32,4224]{1,0:T(8,128)(2,1)S(1)}, bf16[32,4224]{1,0:T(8,128)(2,1)S(1)}, u32[]{:S(2)}, u32[]{:S(2)}) collective-permute-start(bf16[32,4224]{1,0:T(8,128)(2,1)S(1)} %collective-permute-done.7.refs_1_), channel_id=1, source_target_pairs={{16,0},{0,16},{17,1},{1,17},{18,2},{2,18},{19,3},{3,19},{20,4},{4,... | collective-permute-start | bytes 811016 | tf_op jit(solution)/shard_map/ppermute | solution.py:72
  38.5 10.3 %collective-permute-start.10 = (bf16[32,4224]{1,0:T(8,128)(2,1)S(1)}, bf16[32,4224]{1,0:T(8,128)(2,1)S(1)}, u32[]{:S(2)}, u32[]{:S(2)}) collective-permute-start(bf16[32,4224]{1,0:T(8,128)(2,1)S(1)} %collective-permute-done.8.refs_2_), channel_id=1, source_target_pairs={{16,0},{0,16},{17,1},{1,17},{18,2},{2,18},{19,3},{3,19},{20,4},{4,... | collective-permute-start | bytes 811016 | tf_op jit(solution)/shard_map/ppermute | solution.py:72
  44.3 30.2 %copy-start = (bf16[1024,4096]{1,0:T(8,128)(2,1)}, bf16[1024,4096]{1,0:T(8,128)(2,1)S(1)}, u32[]{:S(2)}) copy-start(bf16[1024,4096]{1,0:T(8,128)(2,1)S(1)} %get-tuple-element.34.refs_3_.refs_5_.refs_7_) | copy-start | bytes 25165828
  74.5 5.8 %copy-start.4 = (bf16[128,1024]{1,0:T(8,128)(2,1)}, bf16[128,1024]{1,0:T(8,128)(2,1)S(1)}, u32[]{:S(2)}) copy-start(bf16[128,1024]{1,0:T(8,128)(2,1)S(1)} %get-tuple-element.50) | copy-start | bytes 786436
  74.5 5.8 %copy-start.6 = (bf16[128,1024]{1,0:T(8,128)(2,1)}, bf16[128,1024]{1,0:T(8,128)(2,1)S(1)}, u32[]{:S(2)}) copy-start(bf16[128,1024]{1,0:T(8,128)(2,1)S(1)} %get-tuple-element.49) | copy-start | bytes 786436
  80.4 23.0 %collective-permute-start.25 = (bf16[256,4096]{1,0:T(8,128)(2,1)}, bf16[256,4096]{1,0:T(8,128)(2,1)}, u32[]{:S(2)}, u32[]{:S(2)}) collective-permute-start(bf16[256,4096]{1,0:T(8,128)(2,1)} %shard_map.103), channel_id=1, source_target_pairs={{16,0},{0,16},{17,1},{1,17},{18,2},{2,18},{19,3},{3,19},{20,4},{4,... | collective-permute-start | bytes 6291464 | tf_op jit(solution)/shard_map/ppermute | solution.py:72
  82.7 11.8 %copy-start.7 = (bf16[128,1024]{1,0:T(8,128)(2,1)S(1)}, bf16[128,1024]{1,0:T(8,128)(2,1)}, u32[]{:S(2)}) copy-start(bf16[128,1024]{1,0:T(8,128)(2,1)} %copy-done.6) | copy-start | bytes 786436
  84.0 26.1 %collective-permute-start.15 = (bf16[128,1024]{1,0:T(8,128)(2,1)S(1)}, bf16[128,1024]{1,0:T(8,128)(2,1)S(1)}, u32[]{:S(2)}, u32[]{:S(2)}) collective-permute-start(bf16[128,1024]{1,0:T(8,128)(2,1)S(1)} %get-tuple-element.68), channel_id=1, source_target_pairs={{192,0},{0,64},{64,128},{128,192},{193,1},{1,65},{65,129},{129,193... | collective-permute-start | bytes 786440 | tf_op jit(solution)/shard_map/ppermute | solution.py:72
  87.4 23.2 %collective-permute-start.14 = (bf16[128,1024]{1,0:T(8,128)(2,1)S(1)}, bf16[128,1024]{1,0:T(8,128)(2,1)S(1)}, u32[]{:S(2)}, u32[]{:S(2)}) collective-permute-start(bf16[128,1024]{1,0:T(8,128)(2,1)S(1)} %get-tuple-element.69), channel_id=1, source_target_pairs={{128,0},{192,64},{0,128},{64,192},{129,1},{193,65},{1,129},{65,193... | collective-permute-start | bytes 786440 | tf_op jit(solution)/shard_map/ppermute | solution.py:72
  91.9 21.0 %collective-permute-start.13 = (bf16[128,1024]{1,0:T(8,128)(2,1)S(1)}, bf16[128,1024]{1,0:T(8,128)(2,1)S(1)}, u32[]{:S(2)}, u32[]{:S(2)}) collective-permute-start(bf16[128,1024]{1,0:T(8,128)(2,1)S(1)} %get-tuple-element.70), channel_id=1, source_target_pairs={{64,0},{128,64},{192,128},{0,192},{65,1},{129,65},{193,129},{1,193... | collective-permute-start | bytes 786440 | tf_op jit(solution)/shard_map/ppermute | solution.py:72
  94.5 27.1 %collective-permute-start.16 = (bf16[128,1024]{1,0:T(8,128)(2,1)S(1)}, bf16[128,1024]{1,0:T(8,128)(2,1)S(1)}, u32[]{:S(2)}, u32[]{:S(2)}) collective-permute-start(bf16[128,1024]{1,0:T(8,128)(2,1)S(1)} %copy-done.7), channel_id=1, source_target_pairs={{128,0},{192,64},{0,128},{64,192},{129,1},{193,65},{1,129},{65,193... | collective-permute-start | bytes 786440 | tf_op jit(solution)/shard_map/ppermute | solution.py:72
  95.5 3.4 %copy-start.1 = (bf16[1024,4096]{1,0:T(8,128)(2,1)S(1)}, bf16[1024,4096]{1,0:T(8,128)(2,1)}, u32[]{:S(2)}) copy-start(bf16[1024,4096]{1,0:T(8,128)(2,1)} %copy-done) | copy-start | bytes 25165828
  105.8 7.1 %copy-start.5 = (bf16[128,1024]{1,0:T(8,128)(2,1)S(1)}, bf16[128,1024]{1,0:T(8,128)(2,1)}, u32[]{:S(2)}) copy-start(bf16[128,1024]{1,0:T(8,128)(2,1)} %copy-done.4) | copy-start | bytes 786436
  105.8 35.8 %copy-start.2 = (f32[128,1024]{1,0:T(8,128)S(1)}, f32[128,1024]{1,0:T(8,128)}, u32[]{:S(2)}) copy-start(f32[128,1024]{1,0:T(8,128)} %outer.3) | copy-start | bytes 1572868
  105.8 35.7 %copy-start.3 = (f32[128,1024]{1,0:T(8,128)S(1)}, f32[128,1024]{1,0:T(8,128)}, u32[]{:S(2)}) copy-start(f32[128,1024]{1,0:T(8,128)} %momentum.3) | copy-start | bytes 1572868
  106.0 41.4 %collective-permute-start.28 = (bf16[64,4096]{1,0:T(8,128)(2,1)S(1)}, bf16[64,4096]{1,0:T(8,128)(2,1)S(1)}, u32[]{:S(2)}, u32[]{:S(2)}) collective-permute-start(bf16[64,4096]{1,0:T(8,128)(2,1)S(1)} %get-tuple-element.65), channel_id=1, source_target_pairs={{1,0},{2,1},{3,2},{0,3},{5,4},{6,5},{7,6},{4,7},{9,8},{10,9},{11,1... | collective-permute-start | bytes 1572872 | tf_op jit(solution)/shard_map/ppermute | solution.py:63
  110.2 37.2 %collective-permute-start.27 = (bf16[64,4096]{1,0:T(8,128)(2,1)S(1)}, bf16[64,4096]{1,0:T(8,128)(2,1)S(1)}, u32[]{:S(2)}, u32[]{:S(2)}) collective-permute-start(bf16[64,4096]{1,0:T(8,128)(2,1)S(1)} %get-tuple-element.66), channel_id=1, source_target_pairs={{3,0},{0,1},{1,2},{2,3},{7,4},{4,5},{5,6},{6,7},{11,8},{8,9},{9,10... | collective-permute-start | bytes 1572872 | tf_op jit(solution)/shard_map/ppermute | solution.py:63
  110.6 36.8 %collective-permute-start.26 = (bf16[64,4096]{1,0:T(8,128)(2,1)S(1)}, bf16[64,4096]{1,0:T(8,128)(2,1)S(1)}, u32[]{:S(2)}, u32[]{:S(2)}) collective-permute-start(bf16[64,4096]{1,0:T(8,128)(2,1)S(1)} %get-tuple-element.67), channel_id=1, source_target_pairs={{2,0},{3,1},{0,2},{1,3},{6,4},{7,5},{4,6},{5,7},{10,8},{11,9},{8,1... | collective-permute-start | bytes 1572872 | tf_op jit(solution)/shard_map/ppermute | solution.py:63
  112.8 17.9 %collective-permute-start.17 = (bf16[128,1024]{1,0:T(8,128)(2,1)S(1)}, bf16[128,1024]{1,0:T(8,128)(2,1)S(1)}, u32[]{:S(2)}, u32[]{:S(2)}) collective-permute-start(bf16[128,1024]{1,0:T(8,128)(2,1)S(1)} %copy-done.5), channel_id=1, source_target_pairs={{192,0},{0,64},{64,128},{128,192},{193,1},{1,65},{65,129},{129,193... | collective-permute-start | bytes 786440 | tf_op jit(solution)/shard_map/ppermute | solution.py:72
  121.6 19.9 %collective-permute-start.18 = (bf16[128,1024]{1,0:T(8,128)(2,1)S(1)}, bf16[128,1024]{1,0:T(8,128)(2,1)S(1)}, u32[]{:S(2)}, u32[]{:S(2)}) collective-permute-start(bf16[128,1024]{1,0:T(8,128)(2,1)S(1)} %get-tuple-element.51), channel_id=1, source_target_pairs={{64,0},{128,64},{192,128},{0,192},{65,1},{129,65},{193,129},{1,193... | collective-permute-start | bytes 786440 | tf_op jit(solution)/shard_map/ppermute | solution.py:72
  142.5 11.0 %collective-permute-start.19 = (bf16[64,1024]{1,0:T(8,128)(2,1)S(1)}, bf16[64,1024]{1,0:T(8,128)(2,1)S(1)}, u32[]{:S(2)}, u32[]{:S(2)}) collective-permute-start(bf16[64,1024]{1,0:T(8,128)(2,1)S(1)} %get-tuple-element.52.refs_0_), channel_id=1, source_target_pairs={{64,0},{128,64},{192,128},{0,192},{65,1},{129,65},{193,129},{1,193... | collective-permute-start | bytes 393224 | tf_op jit(solution)/shard_map/ppermute | solution.py:72
  147.2 9.3 %collective-permute-start.22 = (bf16[64,1024]{1,0:T(8,128)(2,1)S(1)}, bf16[64,1024]{1,0:T(8,128)(2,1)S(1)}, u32[]{:S(2)}, u32[]{:S(2)}) collective-permute-start(bf16[64,1024]{1,0:T(8,128)(2,1)S(1)} %get-tuple-element.53.refs_1_), channel_id=1, source_target_pairs={{192,0},{0,64},{64,128},{128,192},{193,1},{1,65},{65,129},{129,193... | collective-permute-start | bytes 393224 | tf_op jit(solution)/shard_map/ppermute | solution.py:72
  148.1 9.5 %collective-permute-start.29 = (bf16[16,4096]{1,0:T(8,128)(2,1)S(1)}, bf16[16,4096]{1,0:T(8,128)(2,1)S(1)}, u32[]{:S(2)}, u32[]{:S(2)}) collective-permute-start(bf16[16,4096]{1,0:T(8,128)(2,1)S(1)} %get-tuple-element.56), channel_id=1, source_target_pairs={{8,0},{9,1},{10,2},{11,3},{12,4},{13,5},{14,6},{15,7},{0,8},{1,9},... | collective-permute-start | bytes 393224 | tf_op jit(solution)/shard_map/ppermute | solution.py:67
  149.5 10.3 %collective-permute-start.30 = (bf16[16,4096]{1,0:T(8,128)(2,1)S(1)}, bf16[16,4096]{1,0:T(8,128)(2,1)S(1)}, u32[]{:S(2)}, u32[]{:S(2)}) collective-permute-start(bf16[16,4096]{1,0:T(8,128)(2,1)S(1)} %get-tuple-element.57), channel_id=1, source_target_pairs={{12,0},{13,1},{14,2},{15,3},{0,4},{1,5},{2,6},{3,7},{4,8},{5,9},{6... | collective-permute-start | bytes 393224 | tf_op jit(solution)/shard_map/ppermute | solution.py:67
  150.2 10.3 %collective-permute-start.31 = (bf16[16,4096]{1,0:T(8,128)(2,1)S(1)}, bf16[16,4096]{1,0:T(8,128)(2,1)S(1)}, u32[]{:S(2)}, u32[]{:S(2)}) collective-permute-start(bf16[16,4096]{1,0:T(8,128)(2,1)S(1)} %get-tuple-element.58), channel_id=1, source_target_pairs={{4,0},{5,1},{6,2},{7,3},{8,4},{9,5},{10,6},{11,7},{12,8},{13,9},{1... | collective-permute-start | bytes 393224 | tf_op jit(solution)/shard_map/ppermute | solution.py:67
  153.5 11.9 %collective-permute-start.24 = (bf16[64,1024]{1,0:T(8,128)(2,1)S(1)}, bf16[64,1024]{1,0:T(8,128)(2,1)S(1)}, u32[]{:S(2)}, u32[]{:S(2)}) collective-permute-start(bf16[64,1024]{1,0:T(8,128)(2,1)S(1)} %get-tuple-element.52.refs_0_), channel_id=1, source_target_pairs={{192,0},{0,64},{64,128},{128,192},{193,1},{1,65},{65,129},{129,193... | collective-permute-start | bytes 393224 | tf_op jit(solution)/shard_map/ppermute | solution.py:72
  156.5 8.8 %collective-permute-start.20 = (bf16[64,1024]{1,0:T(8,128)(2,1)S(1)}, bf16[64,1024]{1,0:T(8,128)(2,1)S(1)}, u32[]{:S(2)}, u32[]{:S(2)}) collective-permute-start(bf16[64,1024]{1,0:T(8,128)(2,1)S(1)} %get-tuple-element.53.refs_1_), channel_id=1, source_target_pairs={{64,0},{128,64},{192,128},{0,192},{65,1},{129,65},{193,129},{1,193... | collective-permute-start | bytes 393224 | tf_op jit(solution)/shard_map/ppermute | solution.py:72
  157.6 7.9 %collective-permute-start.21 = (bf16[64,1024]{1,0:T(8,128)(2,1)S(1)}, bf16[64,1024]{1,0:T(8,128)(2,1)S(1)}, u32[]{:S(2)}, u32[]{:S(2)}) collective-permute-start(bf16[64,1024]{1,0:T(8,128)(2,1)S(1)} %collective-permute-done.19.refs_2_), channel_id=1, source_target_pairs={{64,0},{128,64},{192,128},{0,192},{65,1},{129,65},{193,129},{1,193... | collective-permute-start | bytes 393224 | tf_op jit(solution)/shard_map/ppermute | solution.py:72
  159.7 7.2 %collective-permute-start.23 = (bf16[64,1024]{1,0:T(8,128)(2,1)S(1)}, bf16[64,1024]{1,0:T(8,128)(2,1)S(1)}, u32[]{:S(2)}, u32[]{:S(2)}) collective-permute-start(bf16[64,1024]{1,0:T(8,128)(2,1)S(1)} %collective-permute-done.22.refs_7_), channel_id=1, source_target_pairs={{192,0},{0,64},{64,128},{128,192},{193,1},{1,65},{65,129},{129,193... | collective-permute-start | bytes 393224 | tf_op jit(solution)/shard_map/ppermute | solution.py:72
  160.6 6.6 %collective-permute-start.32 = (bf16[8,4096]{1,0:T(8,128)(2,1)S(1)}, bf16[8,4096]{1,0:T(8,128)(2,1)S(1)}, u32[]{:S(2)}, u32[]{:S(2)}) collective-permute-start(bf16[8,4096]{1,0:T(8,128)(2,1)S(1)} %slice.50), channel_id=1, source_target_pairs={{32,0},{0,32},{33,1},{1,33},{34,2},{2,34},{35,3},{3,35},{36,4},{4,... | collective-permute-start | bytes 196616 | tf_op jit(solution)/shard_map/ppermute | solution.py:72
